TPU v7x, 8 devices: a whole 2x2x1 slice. The times are simulated.
8 devices in a mesh: dp: 1 (over z), tp: 2 (over y), sp: 4 (over x, core).
Axes of the slice: x: 2, y: 2, z: 1, core: 2. Of those that a mesh axis runs over, the one named last changes fastest.
Arguments:
- encoded: bfloat16 [64, 384, 1280], P('dp', 'sp')
- enc_gain: float32 [1280], replicated
- enc_bias: float32 [1280], replicated
- probe: float32 [1280], replicated
- w_query: bfloat16 [1280, 16, 80], P(None, 'tp')
- b_query: float32 [16, 80], P('tp')
- w_key: bfloat16 [1280, 16, 80], P(None, 'tp')
- w_value: bfloat16 [1280, 16, 80], P(None, 'tp')
- b_value: float32 [16, 80], P('tp')
- w_out: bfloat16 [16, 80, 1280], P('tp')
- b_out: float32 [1280], replicated
- head_gain: float32 [1280], replicated
- head_bias: float32 [1280], replicated
- w_up: bfloat16 [1280, 5120], P(None, 'tp')
- b_up: float32 [5120], P('tp')
- w_down: bfloat16 [5120, 1280], P('tp')
- b_down: float32 [1280], replicated
- out_grad: bfloat16 [64, 1280], P('dp')
Outputs:
- output 1: bfloat16 [64, 1280], P('dp')
- output 2: bfloat16 [64, 384, 1280], P('dp', 'sp')
- output 3: float32 [1280], P('dp')
- output 4: float32 [1280, 16, 80], P('dp', 'tp')
- output 5: float32 [1280, 16, 80], P('dp', 'tp')
- output 6: float32 [1280, 16, 80], P('dp', 'tp')
- output 7: float32 [16, 80, 1280], P(('dp', 'tp'))
- output 8: float32 [1280, 5120], P('dp', 'tp')
- output 9: float32 [5120, 1280], P(('dp', 'tp'))
All inputs are finite; a program needn't handle non-finite values.
Results may differ from a plain program's by a relative error of at most 0.0187281.
Values sent between devices are 32-bit elements.
A program may use at most 1 GiB of HBM per device.

v0:
```python
import functools
import jax
import jax.numpy as jnp
from jax import lax
from jax.sharding import PartitionSpec as P

NORM_EPS = 1e-6
IN_SPECS = (P('dp', 'sp', None), P(), P(), P(), P(None, 'tp', None), P('tp', None), P(None, 'tp', None), P(None, 'tp', None), P('tp', None), P('tp', None, None), P(), P(), P(), P(None, 'tp'), P('tp'), P('tp', None), P(), P('dp', None))
OUT_SPECS = (P('dp', None), P('dp', 'sp', None), P('dp'), P('dp', 'tp', None), P('dp', 'tp', None), P('dp', 'tp', None), P(('dp', 'tp'), None, None), P('dp', 'tp'), P(('dp', 'tp'), None))


def layer_norm(rows_in, norm_gain, norm_bias):
    row_mean = jnp.mean(rows_in, axis=-1, keepdims=True)
    centred = rows_in - row_mean
    inv_std = lax.rsqrt(jnp.mean(centred * centred, axis=-1, keepdims=True) + NORM_EPS)
    return centred * inv_std * norm_gain + norm_bias


def norm_vjp(rows_in, norm_gain, norm_bias, cotangent):
    pull_back = jax.vjp(functools.partial(layer_norm, norm_gain=norm_gain, norm_bias=norm_bias), rows_in)[1]
    return pull_back(cotangent)[0]


def gelu_vjp(pre_act, cotangent):
    pull_back = jax.vjp(functools.partial(jax.nn.gelu, approximate=True), pre_act)[1]
    return pull_back(cotangent)[0]


def local_head(encoded, enc_gain, enc_bias, probe, w_query, b_query, w_key, w_value, b_value, w_out, b_out, head_gain, head_bias, w_up, b_up, w_down, b_down, out_grad):
    head_dim = b_query.shape[1]
    score_scale = head_dim ** -0.5
    enc_f32 = encoded.astype(jnp.float32)
    normed = layer_norm(enc_f32, enc_gain, enc_bias).astype(jnp.bfloat16)
    query_heads = (jnp.einsum('w,whd->hd', probe.astype(jnp.bfloat16), w_query, preferred_element_type=jnp.float32) + b_query).astype(jnp.bfloat16)
    key_heads = jnp.einsum('bnw,whd->bnhd', normed, w_key, preferred_element_type=jnp.float32).astype(jnp.bfloat16)
    value_heads = (jnp.einsum('bnw,whd->bnhd', normed, w_value, preferred_element_type=jnp.float32) + b_value).astype(jnp.bfloat16)
    scores = jnp.einsum('bnhd,hd->bhn', key_heads, query_heads, preferred_element_type=jnp.float32) * score_scale
    score_max = lax.pmax(jnp.max(scores, axis=-1, keepdims=True), 'sp')
    exp_scores = jnp.exp(scores - score_max)
    exp_total = lax.psum(jnp.sum(exp_scores, axis=-1, keepdims=True), 'sp')
    value_sum = lax.psum(jnp.einsum('bhn,bnhd->bhd', exp_scores.astype(jnp.bfloat16), value_heads, preferred_element_type=jnp.float32), 'sp')
    pooled_bf = (value_sum / exp_total).astype(jnp.bfloat16)
    attn_out = lax.psum(jnp.einsum('bhd,hdw->bw', pooled_bf, w_out, preferred_element_type=jnp.float32), 'tp') + b_out
    normed_out = layer_norm(attn_out, head_gain, head_bias).astype(jnp.bfloat16)
    pre_act = jnp.dot(normed_out, w_up, preferred_element_type=jnp.float32) + b_up
    hidden = jax.nn.gelu(pre_act, approximate=True).astype(jnp.bfloat16)
    pooled = (attn_out + lax.psum(jnp.dot(hidden, w_down, preferred_element_type=jnp.float32), 'tp') + b_down).astype(jnp.bfloat16)

    grad_w_down = jnp.einsum('bf,bw->fw', hidden, out_grad, preferred_element_type=jnp.float32)
    grad_hidden = jnp.einsum('bw,fw->bf', out_grad, w_down, preferred_element_type=jnp.float32)
    grad_pre = gelu_vjp(pre_act, grad_hidden).astype(jnp.bfloat16)
    grad_w_up = jnp.einsum('bw,bf->wf', normed_out, grad_pre, preferred_element_type=jnp.float32)
    grad_normed_out = lax.psum(jnp.einsum('bf,wf->bw', grad_pre, w_up, preferred_element_type=jnp.float32), 'tp')
    grad_attn = (out_grad.astype(jnp.float32) + norm_vjp(attn_out, head_gain, head_bias, grad_normed_out)).astype(jnp.bfloat16)
    grad_w_out = jnp.einsum('bhd,bw->hdw', pooled_bf, grad_attn, preferred_element_type=jnp.float32)
    grad_pooled = jnp.einsum('bw,hdw->bhd', grad_attn, w_out, preferred_element_type=jnp.float32).astype(jnp.bfloat16)
    weights = exp_scores / exp_total
    grad_weights = jnp.einsum('bhd,bnhd->bhn', grad_pooled, value_heads, preferred_element_type=jnp.float32)
    mean_term = lax.psum(jnp.sum(weights * grad_weights, axis=-1, keepdims=True), 'sp')
    grad_scores = (weights * (grad_weights - mean_term) * score_scale).astype(jnp.bfloat16)
    grad_query = lax.psum(jnp.einsum('bhn,bnhd->hd', grad_scores, key_heads, preferred_element_type=jnp.float32), 'sp')
    grad_keys = jnp.einsum('bhn,hd->bnhd', grad_scores, query_heads, preferred_element_type=jnp.float32).astype(jnp.bfloat16)
    grad_values = jnp.einsum('bhn,bhd->bnhd', weights.astype(jnp.bfloat16), grad_pooled, preferred_element_type=jnp.float32).astype(jnp.bfloat16)
    grad_w_key = lax.psum(jnp.einsum('bnw,bnhd->whd', normed, grad_keys, preferred_element_type=jnp.float32), 'sp')
    grad_w_value = lax.psum(jnp.einsum('bnw,bnhd->whd', normed, grad_values, preferred_element_type=jnp.float32), 'sp')
    grad_normed = lax.psum(jnp.einsum('bnhd,whd->bnw', grad_keys, w_key, preferred_element_type=jnp.float32) + jnp.einsum('bnhd,whd->bnw', grad_values, w_value, preferred_element_type=jnp.float32), 'tp')
    grad_encoded = norm_vjp(enc_f32, enc_gain, enc_bias, grad_normed).astype(jnp.bfloat16)
    grad_w_query = probe[:, None, None] * grad_query[None, :, :]
    grad_probe = lax.psum(jnp.einsum('whd,hd->w', w_query, grad_query.astype(jnp.bfloat16), preferred_element_type=jnp.float32), 'tp')
    return (pooled, grad_encoded, grad_probe, grad_w_query, grad_w_key, grad_w_value, grad_w_out, grad_w_up, grad_w_down)


def solution(mesh):
    return jax.shard_map(local_head, mesh=mesh, in_specs=IN_SPECS, out_specs=OUT_SPECS, check_vma=False)
```

profile of v0, /device:TPU:0, one launch (start us, length us, event | category | flops | bytes accessed | tf_op | source)
XLA Modules:
  0.0 1054.4 jit_solution(13227839781283701503)
XLA Ops:
  7.3 8.2 convert_reduce_fusion
  17.5 5.4 fusion.4
  24.2 15.2 %fusion.37 = bf16[64,96,8,80]{1,3,2,0:T(8,128)(2,1)S(1)} fusion(bf16[1280,8,80]{0,2,1:T(8,128)(2,1)S(1)} %copy-done, bf16[64,96,1280]{2,1,0:T(8,128)(2,1)S(1)} %copy-done.2, f32[1280]{0:T(1024)S(1)} %copy-done.43, f32[1280]{0:T(1024)S(1)} %copy-done.26, f32[64,96]{1,0:T(8,128)S(1)} %fusion.78, f32[64,96]{1,0:T(8,128)S(1)} %broadcast_multiply_fusion.1), kind=kOutput, calls=%fused_computation.41 | convolution fusion | flops 10117447680 | bytes 25290752 | tf_op jit(solution)/shard_map/bnw,whd->bnhd/dot_general | solution.py:35
  39.4 4.1 copy-done.5
  45.1 9.2 pmax.7
  55.3 17.7 %add_convert_fusion.1 = bf16[64,96,8,80]{1,3,2,0:T(8,128)(2,1)S(1)} fusion(f32[8,80]{1,0:T(8,128)S(1)} %copy-done.45, bf16[1280,8,80]{0,2,1:T(8,128)(2,1)} %param.25, bf16[64,96,1280]{2,1,0:T(8,128)(2,1)} %param.18, f32[1280]{0:T(1024)S(1)} %copy-done.43, f32[1280]{0:T(1024)S(1)} %copy-done.26, f32[64,96]{1,0:T(8,128)S(1)} %fusion.78, ...), kind=kOutput, calls=%fused_computation.16 | convolution fusion | flops 10121379840 | bytes 25293312 | tf_op jit(solution)/shard_map/bnw,whd->bnhd/dot_general | solution.py:36
  73.0 4.0 copy-done.3
  77.0 5.5 fusion.71
  83.4 5.8 psum.78
  89.1 21.0 %all-reduce.8.cloned.1.call-done = f32[64,8,80]{2,0,1:T(8,128)} async-done(((f32[64,8,80]{2,0,1:T(8,128)}), f32[64,8,80]{2,0,1:T(8,128)}) %all-reduce.8.cloned.1.call-update) | async-done | bytes 163856 | tf_op jit(solution)/shard_map/psum | solution.py:41
  112.9 5.8 fusion.95
  118.7 13.0 %all-reduce.10.cloned.1.call-done = f32[64,1280]{1,0:T(8,128)} async-done(((f32[64,1280]{1,0:T(8,128)}), f32[64,1280]{1,0:T(8,128)}) %all-reduce.10.cloned.1.call-update) | async-done | bytes 327696 | tf_op jit(solution)/shard_map/psum | solution.py:43
  134.1 4.6 fusion.62
  138.7 5.7 fusion.96
  144.6 4.9 fusion.85
  149.5 13.7 %all-reduce.12.cloned.1.call-done = f32[64,1280]{1,0:T(8,128)} async-done(((f32[64,1280]{1,0:T(8,128)}), f32[64,1280]{1,0:T(8,128)}) %all-reduce.12.cloned.1.call-update) | async-done | bytes 327696 | tf_op jit(solution)/shard_map/psum | solution.py:53
  168.8 5.5 fusion.69
  175.9 7.5 psum.82
  185.2 14.5 %fusion.20 = f32[64,96,1280,1]{2,1,0,3:T(8,128)S(1)} fusion(f32[8,64,96]{2,1,0:T(8,128)S(1)} %get-tuple-element.15, f32[8,80]{1,0:T(8,128)} %get-tuple-element.13, bf16[1280,8,80]{0,2,1:T(8,128)(2,1)S(1)} %copy-done), kind=kOutput, calls=%fused_computation.27 | convolution fusion | flops 10074193920 | bytes 33294848 | tf_op jit(solution)/shard_map/bnhd,whd->bnw/dot_general | solution.py:66
  199.8 24.2 %bitcast_add_fusion = f32[64,96,1280]{2,1,0:T(8,128)} fusion(f32[64,96,1280,1]{2,1,0,3:T(8,128)S(1)} %fusion.20, f32[64,8,96]{2,0,1:T(8,128)S(1)} %copy-done.16, f32[64,8,80]{2,0,1:T(8,128)S(1)} %copy-done.14, bf16[1280,8,80]{0,2,1:T(8,128)(2,1)} %param.25), kind=kOutput, calls=%fused_computation.12 | convolution fusion | flops 10082058240 | bytes 64913408 | tf_op jit(solution)/shard_map/bnhd,whd->bnw/dot_general | solution.py:66
  224.7 6.9 fusion.83
  231.7 6.9 fusion.84
  241.4 6.1 psum.84
  247.8 6.0 psum.85
  255.8 20.8 %fusion.47 = f32[1280,8,80]{0,2,1:T(8,128)} fusion(f32[8,64,96]{2,1,0:T(8,128)S(1)} %copy-done.9, f32[8,80]{1,0:T(8,128)S(1)} %copy-done.25, bf16[64,96,1280]{2,1,0:T(8,128)(2,1)} %param.18, f32[1280]{0:T(1024)S(1)} %copy-done.44, f32[1280]{0:T(1024)S(1)} %copy-done.27, f32[64,96]{1,0:T(8,128)S(1)} %fusion.78, f32[64,96]{1,0:T(8,128)S(1)} %broadcast_multiply_fusion.1), kind=kOutput, calls=%fused_computation.44 | convolution fusion | flops 10121379840 | bytes 19264000 | tf_op jit(solution)/shard_map/bnw,bnhd->whd/dot_general | solution.py:64
  276.7 26.2 %fusion.42 = f32[1280,8,80]{0,2,1:T(8,128)} fusion(f32[64,8,96]{2,0,1:T(8,128)S(1)} %copy-done.17, f32[64,8,80]{2,0,1:T(8,128)S(1)} %copy-done.15, bf16[64,96,1280]{2,1,0:T(8,128)(2,1)} %param.18, f32[1280]{0:T(1024)S(1)} %copy-done.44, f32[1280]{0:T(1024)S(1)} %copy-done.27, f32[64,96]{1,0:T(8,128)S(1)} %fusion.78, f32[64,96]{1,0:T(8,128)S(1)} %broadcast_multiply_fusion.1), kind=kOutput, calls=%fused_computation.43 | convolution fusion | flops 10121379840 | bytes 19425280 | tf_op jit(solution)/shard_map/bnw,bnhd->whd/dot_general | solution.py:65
  305.4 611.9 %all-reduce.16.cloned.1.call-done = (f32[64,1280]{1,0:T(8,128)}, f32[64,96,1280]{2,1,0:T(8,128)}) async-done(((f32[64,1280]{1,0:T(8,128)}, f32[64,96,1280]{2,1,0:T(8,128)}), (f32[64,1280]{1,0:T(8,128)}, f32[64,96,1280]{2,1,0:T(8,128)})) %all-reduce.16.cloned.1.call-update) | async-done | bytes 31784976 | tf_op jit(solution)/shard_map/psum | solution.py:47
  917.3 18.1 %fusion.8 = f32[64,96]{1,0:T(8,128)S(1)} fusion(bf16[64,96,1280]{2,1,0:T(8,128)(2,1)} %param.18, f32[64,96,1280]{2,1,0:T(8,128)} %get-tuple-element.12, f32[1280]{0:T(1024)S(1)} %copy-done.27, f32[64,96]{1,0:T(8,128)S(1)} %broadcast_multiply_fusion.1), kind=kLoop, calls=%fused_computation.11 | loop fusion | flops 39315456 | bytes 47240192 | tf_op jit(solution)/shard_map/transpose(jvp())/reduce_sum | solution.py:16
  935.5 19.7 %fusion.17 = f32[64,96]{1,0:T(8,128)S(1)} fusion(f32[64,96]{1,0:T(8,128)S(1)} %multiply_multiply_fusion.2, f32[64,96]{1,0:T(8,128)S(1)} %broadcast_multiply_fusion.1, bf16[64,96,1280]{2,1,0:T(8,128)(2,1)} %param.18, f32[64,96]{1,0:T(8,128)S(1)} %fusion.78, f32[64,96,1280]{2,1,0:T(8,128)} %get-tuple-element.12, f32[1280]{0:T(1024)S(1)} %copy-done.27), kind=kLoop, calls=%fused_computation.25 | loop fusion | flops 62908416 | bytes 47289344 | tf_op jit(solution)/shard_map/transpose(jvp())/reduce_sum | solution.py:14
  956.0 20.4 %add_convert_fusion = bf16[64,96,1280]{2,1,0:T(8,128)(2,1)} fusion(f32[64,96]{1,0:T(8,128)S(1)} %negate_multiply_fusion, f32[64,96]{1,0:T(8,128)S(1)} %multiply_multiply_fusion.2, f32[64,96]{1,0:T(8,128)S(1)} %broadcast_multiply_fusion.1, bf16[64,96,1280]{2,1,0:T(8,128)(2,1)S(1)} %bitcast.136, f32[64,96]{1,0:T(8,128)S(1)} %fusion.78, ...), kind=kLoop, calls=%fused_computation.13 | loop fusion | flops 70778880 | bytes 63017984 | tf_op jit(solution)/shard_map/convert_element_type | solution.py:67
  976.4 63.2 %all-reduce.14.cloned.1.call-done = (f32[1280,8,80]{0,2,1:T(8,128)}, f32[1280,8,80]{0,2,1:T(8,128)}) async-done(((f32[1280,8,80]{0,2,1:T(8,128)}, f32[1280,8,80]{0,2,1:T(8,128)}), (f32[1280,8,80]{0,2,1:T(8,128)}, f32[1280,8,80]{0,2,1:T(8,128)})) %all-reduce.14.cloned.1.call-update) | async-done | bytes 6553616 | tf_op jit(solution)/shard_map/psum | solution.py:64
  1039.6 3.9 copy.73
  (148 shorter events, 33.9 us)
Async XLA Ops:
  7.2 102.9 %all-reduce.8.cloned.1.call-start = ((), (), s32[]{:S(2)}) async-start(), calls=%async_computation | async-start | bytes 524288 | tf_op jit(solution)/shard_map/psum | solution.py:41
  24.2 31.1 %copy-start.45 = (f32[8,80]{1,0:T(8,128)S(1)}, f32[8,80]{1,0:T(8,128)}, u32[]{:S(2)}) copy-start(f32[8,80]{1,0:T(8,128)} %param.26) | copy-start | bytes 7684
  55.3 57.7 %copy-start.10 = (bf16[64,1280]{1,0:T(8,128)(2,1)S(1)}, bf16[64,1280]{1,0:T(8,128)(2,1)}, u32[]{:S(2)}) copy-start(bf16[64,1280]{1,0:T(8,128)(2,1)} %param.35) | copy-start | bytes 491524
  73.0 58.7 %copy-start.18 = (f32[1280]{0:T(1024)S(1)}, f32[1280]{0:T(1024)}, u32[]{:S(2)}) copy-start(f32[1280]{0:T(1024)} %param.28) | copy-start | bytes 15364
  73.0 61.1 %copy-start.23 = (f32[1280]{0:T(1024)S(1)}, f32[1280]{0:T(1024)}, u32[]{:S(2)}) copy-start(f32[1280]{0:T(1024)} %param.29) | copy-start | bytes 15364
  73.0 61.1 %copy-start.28 = (f32[1280]{0:T(1024)S(1)}, f32[1280]{0:T(1024)}, u32[]{:S(2)}) copy-start(f32[1280]{0:T(1024)} %param.30) | copy-start | bytes 15364
  73.0 61.1 %copy-start.38 = (f32[2560]{0:T(1024)S(1)}, f32[2560]{0:T(1024)}, u32[]{:S(2)}) copy-start(f32[2560]{0:T(1024)} %param.32) | copy-start | bytes 30724
  83.3 48.4 %all-reduce.10.cloned.1.call-start = ((), (), s32[]{:S(2)}) async-start(), calls=%async_computation.1 | async-start | bytes 655360 | tf_op jit(solution)/shard_map/psum | solution.py:43
  89.1 60.4 %copy-start.31 = (f32[64,8]{0,1:T(8,128)}, f32[64,8]{0,1:T(8,128)S(1)}, u32[]{:S(2)}) copy-start(f32[64,8]{0,1:T(8,128)S(1)} %psum.78) | copy-start | bytes 6148
  112.9 50.3 %all-reduce.12.cloned.1.call-start = ((), (), s32[]{:S(2)}) async-start(), calls=%async_computation.2 | async-start | bytes 655360 | tf_op jit(solution)/shard_map/psum | solution.py:53
  131.7 31.5 %copy-start.4 = (f32[64,1280]{1,0:T(8,128)S(1)}, f32[64,1280]{1,0:T(8,128)}, u32[]{:S(2)}) copy-start(f32[64,1280]{1,0:T(8,128)} %all-reduce.10.cloned.1.call-done) | copy-start | bytes 983044
  132.9 35.9 %copy-start.36 = (f32[64]{0:T(128)}, f32[64]{0:T(128)S(1)}, u32[]{:S(2)}) copy-start(f32[64]{0:T(128)S(1)} %broadcast_multiply_fusion.2) | copy-start | bytes 772
  134.1 34.6 %copy-start.40 = (f32[64]{0:T(128)}, f32[64]{0:T(128)S(1)}, u32[]{:S(2)}) copy-start(f32[64]{0:T(128)S(1)} %fusion.81) | copy-start | bytes 772
  144.4 772.9 %all-reduce.16.cloned.1.call-start = ((), (), s32[]{:S(2)}) async-start(), calls=%async_computation.4 | async-start | bytes 63569920 | tf_op jit(solution)/shard_map/psum | solution.py:47
  224.0 815.6 %all-reduce.14.cloned.1.call-start = ((), (), s32[]{:S(2)}) async-start(), calls=%async_computation.3 | async-start | bytes 13107200 | tf_op jit(solution)/shard_map/psum | solution.py:64
  231.6 22.2 %copy-start.35 = (f32[1280]{0:T(1024)S(1)}, f32[1280]{0:T(1024)}, u32[]{:S(2)}) copy-start(f32[1280]{0:T(1024)} %param.21) | copy-start | bytes 15364
  231.6 24.2 %copy-start.9 = (f32[8,64,96]{2,1,0:T(8,128)S(1)}, f32[8,64,96]{2,1,0:T(8,128)}, u32[]{:S(2)}) copy-start(f32[8,64,96]{2,1,0:T(8,128)} %copy-done.8) | copy-start | bytes 589828
  231.7 24.2 %copy-start.25 = (f32[8,80]{1,0:T(8,128)S(1)}, f32[8,80]{1,0:T(8,128)}, u32[]{:S(2)}) copy-start(f32[8,80]{1,0:T(8,128)} %get-tuple-element.13) | copy-start | bytes 7684
  231.7 24.2 %copy-start.27 = (f32[1280]{0:T(1024)S(1)}, f32[1280]{0:T(1024)}, u32[]{:S(2)}) copy-start(f32[1280]{0:T(1024)} %param.19) | copy-start | bytes 15364
  231.7 24.1 %copy-start.44 = (f32[1280]{0:T(1024)S(1)}, f32[1280]{0:T(1024)}, u32[]{:S(2)}) copy-start(f32[1280]{0:T(1024)} %param.20) | copy-start | bytes 15364
  255.8 20.8 %copy-start.15 = (f32[64,8,80]{2,0,1:T(8,128)S(1)}, f32[64,8,80]{2,0,1:T(8,128)}, u32[]{:S(2)}) copy-start(f32[64,8,80]{2,0,1:T(8,128)} %get-tuple-element.24) | copy-start | bytes 491524
  255.8 20.8 %copy-start.17 = (f32[64,8,96]{2,0,1:T(8,128)S(1)}, f32[64,8,96]{2,0,1:T(8,128)}, u32[]{:S(2)}) copy-start(f32[64,8,96]{2,0,1:T(8,128)} %get-tuple-element.19) | copy-start | bytes 589828
  276.6 26.3 %copy-start.13 = (bf16[64,1280,1]{1,0,2:T(8,128)(2,1)S(1)}, bf16[64,1280,1]{1,0,2:T(8,128)(2,1)}, u32[]{:S(2)}) copy-start(bf16[64,1280,1]{1,0,2:T(8,128)(2,1)} %copy-done.12) | copy-start | bytes 491524
  276.7 26.3 %copy-start.22 = (f32[64,8,80]{2,0,1:T(8,128)S(1)}, f32[64,8,80]{2,0,1:T(8,128)}, u32[]{:S(2)}) copy-start(f32[64,8,80]{2,0,1:T(8,128)} %all-reduce.8.cloned.1.call-done) | copy-start | bytes 491524
  276.7 26.3 %copy-start.33 = (f32[64,8]{0,1:T(8,128)S(1)}, f32[64,8]{0,1:T(8,128)}, u32[]{:S(2)}) copy-start(f32[64,8]{0,1:T(8,128)} %copy-done.31) | copy-start | bytes 6148
  917.3 38.7 %slice-start = ((s8[15728640]{0:T(1024)(128)(4,1)}), s8[4194304]{0:T(1024)(128)(4,1)S(1)}, s32[]{:S(2)}) async-start(s8[15728640]{0:T(1024)(128)(4,1)} %bitcast.135), calls=%async_computation.5 | async-start | bytes 8388608
  917.3 38.7 %slice-start.1 = ((s8[15728640]{0:T(1024)(128)(4,1)}), s8[4194304]{0:T(1024)(128)(4,1)S(1)}, s32[]{:S(2)}) async-start(s8[15728640]{0:T(1024)(128)(4,1)} %bitcast.135), calls=%async_computation.6 | async-start | bytes 8388608
  935.4 19.8 %copy-start.19 = (f32[64,1280]{1,0:T(8,128)S(1)}, f32[64,1280]{1,0:T(8,128)}, u32[]{:S(2)}) copy-start(f32[64,1280]{1,0:T(8,128)} %get-tuple-element.11) | copy-start | bytes 983044
  935.4 19.8 %copy-start.39 = (f32[1280]{0:T(1024)S(1)}, f32[1280]{0:T(1024)}, u32[]{:S(2)}) copy-start(f32[1280]{0:T(1024)} %param.34) | copy-start | bytes 15364
  935.4 20.5 %slice-start.2 = ((s8[15728640]{0:T(1024)(128)(4,1)}), s8[4194304]{0:T(1024)(128)(4,1)S(1)}, s32[]{:S(2)}) async-start(s8[15728640]{0:T(1024)(128)(4,1)} %bitcast.135), calls=%async_computation.7 | async-start | bytes 8388608
  935.5 20.5 %slice-start.3 = ((s8[15728640]{0:T(1024)(128)(4,1)}), s8[3145728]{0:T(1024)(128)(4,1)S(1)}, s32[]{:S(2)}) async-start(s8[15728640]{0:T(1024)(128)(4,1)} %bitcast.135), calls=%async_computation.8 | async-start | bytes 6291456
  956.0 91.5 %copy-start.1 = (bf16[1280,8,80]{0,2,1:T(8,128)(2,1)S(1)}, bf16[1280,8,80]{0,2,1:T(8,128)(2,1)}, u32[]{:S(2)}) copy-start(bf16[1280,8,80]{0,2,1:T(8,128)(2,1)} %param.24) | copy-start | bytes 4915204
  (26 other events, 268.3 us)
Sparse Core Ops, SparseCore 0:
  83.4 26.6 all-reduce.7
  113.0 18.6 all-reduce.9
  144.5 18.6 all-reduce.11
  224.1 693.1 all-reduce.15
  920.1 119.4 all-reduce.13
where the time goes:
time: 1060 us; the launch traced here: 1050 us
  waiting for transfers between devices  723 us (68%)
  matrix products  178 us (17%)
  other arithmetic  83.8 us (8%)
  blocking collectives  34.6 us (3%)
  local copies, waits for them, and re-layouts  20.1 us (2%)
  between operations  14.9 us (1%)
    psum x1, waiting for transfers between devices, local_head(): lax.psum(jnp.dot(hidden, w_down, preferred_element_type=jnp.float32), 'tp')  612 us
    psum x1, waiting for transfers between devices, local_head(): lax.psum(jnp.einsum('bnw,bnhd->whd', normed, grad_keys, preferred_element...  63.2 us
    dot_general x1, matrix products, local_head(): jnp.einsum('bnw,bnhd->whd', normed, grad_values, preferred_element_type=j...  26.2 us
    dot_general x1, matrix products, local_head(): jnp.einsum('bnhd,whd->bnw', grad_values, w_value, preferred_element_type=...  24.2 us
  transfers between devices with their start and end apart: 5, of which 5 were waited for; matrix products, arithmetic and copies ran while one was open for 13% of the time, Pallas kernels for 0%

commit v1 on v0

v1 whole, which is shorter than its diff:
```python
import functools
import jax
import jax.numpy as jnp
from jax import lax
from jax.experimental import pallas as pl
from jax.experimental.pallas import tpu as pltpu
from jax.sharding import PartitionSpec as P

NORM_EPS = 1e-6
F32 = jnp.float32
BF16 = jnp.bfloat16
IN_SPECS = (P('dp', 'sp', None), P(), P(), P(), P(None, 'tp', None), P('tp', None), P(None, 'tp', None), P(None, 'tp', None), P('tp', None), P('tp', None, None), P(), P(), P(), P(None, 'tp'), P('tp'), P('tp', None), P(), P('dp', None))
OUT_SPECS = (P('dp', None), P('dp', 'sp', None), P('dp'), P('dp', 'tp', None), P('dp', 'tp', None), P('dp', 'tp', None), P(('dp', 'tp'), None, None), P('dp', 'tp'), P(('dp', 'tp'), None))
NN = (((1,), (0,)), ((), ()))
NT = (((1,), (1,)), ((), ()))
TN = (((0,), (0,)), ((), ()))


def mm(a, b, dims=NN):
    return lax.dot_general(a, b, dims, preferred_element_type=F32)


def dot(spec, a, b):
    return jnp.einsum(spec, a, b, preferred_element_type=F32)


def row_stats(xs):
    mean = jnp.mean(xs, axis=-1, keepdims=True)
    cen = xs - mean
    return cen, lax.rsqrt(jnp.mean(cen * cen, axis=-1, keepdims=True) + NORM_EPS)


def fwd_body(nk, x_ref, gu_ref, bu_ref, xh_ref, sx_ref, rs_ref, r_ref, ml_ref):
    images, tokens, width = x_ref.shape
    nh = nk // 2
    strip = 16
    for i in range(images):
        for j in range(0, tokens, strip):
            cen, rstd = row_stats(x_ref[i, j:j + strip, :].astype(F32))
            xh_ref[i, j:j + strip, :] = (cen * rstd).astype(BF16)
            rs_ref[0, j:j + strip, i * nk:(i + 1) * nk] = jnp.broadcast_to(rstd, (strip, nk))
    parts = []
    for i in range(images):
        s2 = mm(xh_ref[i], gu_ref[...], NT)
        parts.append(s2[:, :nk] + s2[:, nk:])
    sx = jnp.concatenate(parts, axis=1)
    sx_ref[0] = sx
    s = sx + bu_ref[...]
    m = jnp.max(s, axis=0, keepdims=True)
    e = jnp.exp(s - m)
    l = jnp.sum(e, axis=0, keepdims=True)
    row = lax.broadcasted_iota(jnp.int32, (8, m.shape[1]), 0)
    ml_ref[0] = jnp.where(row == 0, m, l)
    et = jnp.transpose(e.astype(BF16))
    for i in range(images):
        r_ref[:, i, :] = mm(et[i * nk:i * nk + nh], xh_ref[i])


def run_fwd(x, gu2, bu):
    nb, tokens, width = x.shape
    nk = gu2.shape[0] // 2
    bi = 128 // nk
    ng = nb // bi
    return pl.pallas_call(
        functools.partial(fwd_body, nk),
        grid=(ng,),
        in_specs=[
            pl.BlockSpec((bi, tokens, width), lambda i: (i, 0, 0)),
            pl.BlockSpec(gu2.shape, lambda i: (0, 0)),
            pl.BlockSpec(bu.shape, lambda i: (0, 0)),
        ],
        out_specs=[
            pl.BlockSpec((bi, tokens, width), lambda i: (i, 0, 0)),
            pl.BlockSpec((1, tokens, 128), lambda i: (i, 0, 0)),
            pl.BlockSpec((1, tokens, 128), lambda i: (i, 0, 0)),
            pl.BlockSpec((nk // 2, bi, width), lambda i: (0, i, 0)),
            pl.BlockSpec((1, 8, 128), lambda i: (i, 0, 0)),
        ],
        out_shape=[
            jax.ShapeDtypeStruct((nb, tokens, width), BF16),
            jax.ShapeDtypeStruct((ng, tokens, 128), F32),
            jax.ShapeDtypeStruct((ng, tokens, 128), F32),
            jax.ShapeDtypeStruct((nk // 2, nb, width), F32),
            jax.ShapeDtypeStruct((ng, 8, 128), F32),
        ],
        cost_estimate=pl.CostEstimate(flops=8_000_000_000, bytes_accessed=40_000_000, transcendentals=0),
        name='fwd_tokens',
    )(x, gu2, bu)


def bwd_body(nk, xh_ref, sx_ref, rs_ref, gt_ref, gu_ref, aux_ref, dx_ref, z_ref, dl_ref, zacc_ref):
    step = pl.program_id(0)
    images, tokens, width = xh_ref.shape
    nh = nk // 2

    @pl.when(step == 0)
    def _():
        zacc_ref[...] = jnp.zeros_like(zacc_ref)

    sx = sx_ref[0]
    rstd = rs_ref[0]
    dpx = jnp.concatenate([mm(xh_ref[i], gt_ref[i], NT) for i in range(images)], axis=1)
    p = jnp.exp(sx - aux_ref[0, 0:1]) * aux_ref[0, 1:2]
    ds = p * (dpx + aux_ref[0, 2:3])
    dl_ref[0] = jnp.broadcast_to(jnp.sum(ds, axis=0, keepdims=True), dl_ref.shape[1:])
    prod = (ds * sx + p * dpx) * rstd * (1.0 / width)
    ph = prod.astype(BF16)
    po = (prod - ph.astype(F32)).astype(BF16)
    g0 = lax.broadcasted_iota(jnp.int32, (128, 128), 0) // nk
    g1 = lax.broadcasted_iota(jnp.int32, (128, 128), 1) // nk
    ind = jnp.where(g0 == g1, 1.0, 0.0).astype(BF16)
    c2 = mm(ph, ind) + mm(po, ind)
    dst = jnp.transpose(ds.astype(BF16))
    ca = (ds * rstd).astype(BF16)
    cb = (p * rstd).astype(BF16)
    z = zacc_ref[...]
    for i in range(images):
        xh = xh_ref[i]
        z = z + mm(dst[i * nk:i * nk + nh], xh)
        coef = jnp.concatenate([ca[:, i * nk:(i + 1) * nk], cb[:, i * nk:(i + 1) * nk]], axis=1)
        dxh = mm(coef, jnp.concatenate([gu_ref[...], gt_ref[i]], axis=0))
        dx_ref[i] = (dxh - c2[:, i * nk:i * nk + 1] * xh.astype(F32)).astype(BF16)
    zacc_ref[...] = z
    z_ref[...] = z


def run_bwd(xh, sx, rs, gt, gu_hi, aux):
    nb, tokens, width = xh.shape
    nk = gu_hi.shape[0]
    bi = 128 // nk
    ng = nb // bi
    return pl.pallas_call(
        functools.partial(bwd_body, nk),
        grid=(ng,),
        in_specs=[
            pl.BlockSpec((bi, tokens, width), lambda i: (i, 0, 0)),
            pl.BlockSpec((1, tokens, 128), lambda i: (i, 0, 0)),
            pl.BlockSpec((1, tokens, 128), lambda i: (i, 0, 0)),
            pl.BlockSpec((bi, nk, width), lambda i: (i, 0, 0)),
            pl.BlockSpec((nk, width), lambda i: (0, 0)),
            pl.BlockSpec((1, 8, 128), lambda i: (i, 0, 0)),
        ],
        out_specs=[
            pl.BlockSpec((bi, tokens, width), lambda i: (i, 0, 0)),
            pl.BlockSpec((nk // 2, width), lambda i: (0, 0)),
            pl.BlockSpec((1, 8, 128), lambda i: (i, 0, 0)),
        ],
        out_shape=[
            jax.ShapeDtypeStruct((nb, tokens, width), BF16),
            jax.ShapeDtypeStruct((nk // 2, width), F32),
            jax.ShapeDtypeStruct((ng, 8, 128), F32),
        ],
        scratch_shapes=[pltpu.VMEM((nk // 2, width), F32)],
        cost_estimate=pl.CostEstimate(flops=12_000_000_000, bytes_accessed=40_000_000, transcendentals=0),
        name='bwd_tokens',
    )(xh, sx, rs, gt, gu_hi, aux)


MESH = pl.DeviceIdType.MESH
VM = pl.BlockSpec(memory_space=pltpu.VMEM)
ANY = pl.BlockSpec(memory_space=pl.ANY)


def send(src, dst, sems, k, where):
    copy = pltpu.make_async_remote_copy(src_ref=src, dst_ref=dst, send_sem=sems.at[0, k], recv_sem=sems.at[1, k], device_id=where, device_id_type=MESH)
    copy.start()
    return copy


def greet(places):
    barrier = pltpu.get_barrier_semaphore()
    for where in places:
        pl.semaphore_signal(barrier, inc=1, device_id=where, device_id_type=MESH)
    pl.semaphore_wait(barrier, len(places))


def places():
    tp = lax.axis_index('tp')
    sp = lax.axis_index('sp')
    core = lax.rem(sp, 2)
    return {'tp': 1 - tp}, {'sp': sp + 1 - 2 * core}, {'sp': lax.rem(sp + 2, 4)}, core


def two(a):
    hi = a.astype(BF16)
    return hi, (a - hi.astype(F32)).astype(BF16)


def three(a):
    hi, rest = a.astype(BF16), a
    rest = rest - hi.astype(F32)
    mid = rest.astype(BF16)
    return hi, mid, (rest - mid.astype(F32)).astype(BF16)


def head_mask(rows, nh, hd):
    lane = lax.broadcasted_iota(jnp.int32, (rows, nh * hd), 1)
    row = lax.broadcasted_iota(jnp.int32, (rows, nh * hd), 0)
    return jnp.logical_and(lane >= row * hd, lane < (row + 1) * hd)


def unpack(packed, nk):
    groups, lanes = packed.shape
    per = lanes // nk
    rows = jnp.concatenate([jnp.broadcast_to(packed[g:g + 1], (per, lanes)) for g in range(groups)], axis=0)
    keep = own_lanes(rows.shape, nk, per)
    rows = jnp.where(keep, rows, 0.0)
    shift = nk
    while shift < lanes:
        rows = rows + pltpu.roll(rows, shift, 1)
        shift *= 2
    return rows


def own_lanes(shape, nk, per):
    lane = lax.broadcasted_iota(jnp.int32, shape, 1)
    row = lax.rem(lax.broadcasted_iota(jnp.int32, shape, 0), per)
    return jnp.logical_and(lane >= row * nk, lane < (row + 1) * nk)


def pack(rows, nk):
    images, lanes = rows.shape
    per = lanes // nk
    shift = nk
    while shift < lanes:
        rows = rows + pltpu.roll(rows, shift, 1)
        shift *= 2
    rows = jnp.where(own_lanes(rows.shape, nk, per), rows, 0.0)
    return jnp.concatenate([jnp.sum(rows[g * per:(g + 1) * per], axis=0, keepdims=True) for g in range(images // per)], axis=0)


def query_body(nh, hd, probe_ref, wq_ref, bq_ref, wk_ref, wv_ref, bv_ref, gain_ref, bias_ref, gu_ref, bu_ref, q_ref, cb_ref, us_ref, ur_ref, sems):
    tp_peer, _, _, _ = places()
    greet([tp_peer])
    width = probe_ref.shape[1]
    nk = 2 * nh
    q = (mm(jnp.broadcast_to(probe_ref[...], (8, width)).astype(BF16), wq_ref[...], NT)[:1] + bq_ref[...]).astype(BF16)
    q_ref[...] = q.astype(F32)
    qd = jnp.where(head_mask(nh, nh, hd), jnp.broadcast_to(q.astype(F32), (nh, nh * hd)), 0.0).astype(BF16)
    u = mm(qd, wk_ref[...])
    us_ref[...] = u
    copy = send(us_ref, ur_ref, sems, 0, tp_peer)
    bias = bias_ref[...]
    bh, bl = two(bias)
    row = lax.broadcasted_iota(jnp.int32, (8, width), 0)
    b2 = jnp.where(row == 0, bh.astype(F32), jnp.where(row == 1, bl.astype(F32), 0.0)).astype(BF16)
    cb_ref[...] = jnp.sum(mm(b2, wv_ref[...], NT), axis=0, keepdims=True) + bv_ref[...]
    copy.wait()
    scale = hd ** -0.5
    ua = jnp.concatenate([u, ur_ref[...]], axis=0) * scale
    gu = ua * gain_ref[...]
    gu = gu - jnp.mean(gu, axis=1, keepdims=True)
    gh, gl = two(gu)
    gu_ref[:nk] = gh
    gu_ref[nk:] = gl
    bu = jnp.broadcast_to(jnp.sum(ua * bias, axis=1, keepdims=True), (nk, 128))
    bu_ref[...] = jnp.transpose(jnp.concatenate([bu] * (128 // nk), axis=0))[:1]


def run_query(nh, hd, probe, wq, bq, wk, wv, bv, gain, bias):
    width = probe.shape[1]
    return pl.pallas_call(
        functools.partial(query_body, nh, hd),
        in_specs=[VM] * 8,
        out_specs=[VM] * 4,
        out_shape=[
            jax.ShapeDtypeStruct((4 * nh, width), BF16),
            jax.ShapeDtypeStruct((1, 128), F32),
            jax.ShapeDtypeStruct((1, nh * hd), F32),
            jax.ShapeDtypeStruct((1, nh * hd), F32),
        ],
        scratch_shapes=[pltpu.VMEM((nh, width), F32), pltpu.VMEM((nh, width), F32), pltpu.SemaphoreType.DMA((2, 1))],
        compiler_params=pltpu.CompilerParams(collective_id=0, has_side_effects=True),
        cost_estimate=pl.CostEstimate(flops=50_000_000, bytes_accessed=6_000_000, transcendentals=0),
        name='query_fold',
    )(probe, wq, bq, wk, wv, bv, gain, bias)


def swap_halves(src, buf, sems, k, tp_peer, core):
    half = src.shape[0] // 2
    rows = pl.ds(pl.multiple_of(core * half, half), half)
    return send(src.at[rows], buf.at[rows], sems, k, tp_peer)


def pass_on(buf, sems, k, sib, core):
    half = buf.shape[0] // 2
    rows = pl.ds(pl.multiple_of(core * half, half), half)
    return send(buf.at[rows], buf.at[rows], sems, k, sib)


def head_body(nh, hd, r_ref, ml_ref, wv_ref, wvh_ref, wo_ref, wup_hbm, wdn_hbm, gain_ref, bu_ref, cb_ref, bo_ref, hg_ref, hb_ref, bup_ref, bdn_ref, og_ref,
              y_out, g_out, dpre_out, o_out, da_out, pooled_out, do_out, gt_out, aux_out, rf_out,
              wup, wdn, wvs, osd, mls, ora, mra, osd2, mls2, orb, mrb, aps, apr, rs, ra, rb, rc, rd, re, dys, dyr, mps, mpr, dor, kps, kpr, dg_s, lsem, sems):
    tp_peer, sib, xp, core = places()
    nk = 2 * nh
    nb = og_ref.shape[0]
    width = og_ref.shape[1]
    load_up = pltpu.make_async_copy(wup_hbm, wup, lsem.at[0])
    load_dn = pltpu.make_async_copy(wdn_hbm, wdn, lsem.at[1])
    load_dn.start()
    load_up.start()
    gain = gain_ref[...]
    groups = ml_ref.shape[0]
    for h in range(nh):
        rh = (r_ref[h] * gain).astype(BF16)
        osd[:, h * hd:(h + 1) * hd] = mm(rh, wv_ref[h * hd:(h + 1) * hd, :], NT)
    m0 = jnp.concatenate([ml_ref[g, 0:1] for g in range(groups)], axis=0)
    l0 = jnp.concatenate([ml_ref[g, 1:2] for g in range(groups)], axis=0)
    mls[:groups] = m0
    mls[groups:] = l0
    greet([tp_peer, sib, xp])
    c_wv = send(wvh_ref, wvs, sems, 0, sib)
    c1 = send(osd, ora, sems, 1, sib)
    c2 = send(mls, mra, sems, 2, sib)
    onehot = jnp.where(head_mask(128, nh, hd), 1.0, 0.0).astype(BF16)

    def spread(rows):
        return sum(mm(part, onehot) for part in three(rows))

    def join(oa, ma, la, ob, mb, lb):
        mn = jnp.maximum(ma, mb)
        fa, fb = jnp.exp(ma - mn), jnp.exp(mb - mn)
        o = oa * spread(unpack(fa, nk)) + ob * spread(unpack(fb, nk))
        return o, mn, fa * la + fb * lb

    c1.wait()
    c2.wait()
    o1, m1, l1 = join(osd[...], m0, l0, ora[...], mra[:groups], mra[groups:])
    osd2[...] = o1
    mls2[:groups] = m1
    mls2[groups:] = l1
    c3 = send(osd2, orb, sems, 3, xp)
    c4 = send(mls2, mrb, sems, 4, xp)
    load_dn.wait()
    dg_s[...] = mm(og_ref[...], wdn[...], NT)
    c3.wait()
    c4.wait()
    o, m, l = join(o1, m1, l1, orb[...], mrb[:groups], mrb[groups:])
    inv_l = 1.0 / l
    o = o * spread(unpack(inv_l, nk)) + cb_ref[...]
    o_bf = o.astype(BF16)
    o_out[...] = o_bf
    ap = mm(o_bf, wo_ref[...])
    aps[...] = ap
    c5 = swap_halves(aps, apr, sems, 5, tp_peer, core)
    wr = unpack(jnp.exp(m0 - m) * inv_l, nk)
    for h in range(nh):
        rs[h] = r_ref[h] * wr[:, h:h + 1]
    nq = nh // 2
    mine = pl.ds(core * nq, nq)
    theirs = pl.ds((1 - core) * nq, nq)
    r1 = send(rs.at[theirs], ra, sems, 6, sib)
    c5.wait()
    c6 = pass_on(apr, sems, 7, sib, core)
    r1.wait()
    rb[...] = rs[mine] + ra[...]
    r2 = send(rb, rc, sems, 8, xp)
    c6.wait()
    a = ap + apr[...] + bo_ref[...]
    acen, arstd = row_stats(a)
    ahat = acen * arstd
    y = (ahat * hg_ref[...] + hb_ref[...]).astype(BF16)
    y_out[...] = y
    load_up.wait()
    pre = mm(y, wup[...]) + bup_ref[...]
    k0 = 0.7978845608028654
    k1 = 0.044715
    sq = pre * pre
    th = jnp.tanh(k0 * (pre + k1 * (pre * sq)))
    half = 0.5 * (1.0 + th)
    g = (pre * half).astype(BF16)
    g_out[...] = g
    dgelu = half + 0.5 * pre * (1.0 - th * th) * (k0 * (1.0 + 3.0 * k1 * sq))
    dpre = (dg_s[...] * dgelu).astype(BF16)
    dpre_out[...] = dpre
    dyp = mm(dpre, wup[...], NT)
    dys[...] = dyp
    c7 = swap_halves(dys, dyr, sems, 9, tp_peer, core)
    mp = mm(g, wdn[...])
    mps[...] = mp
    c8 = swap_halves(mps, mpr, sems, 10, tp_peer, core)
    c_wv.wait()
    c7.wait()
    c9 = pass_on(dyr, sems, 11, sib, core)
    c9.wait()
    dah = (dyp + dyr[...]) * hg_ref[...]
    da = arstd * (dah - jnp.mean(dah, axis=1, keepdims=True) - ahat * jnp.mean(dah * ahat, axis=1, keepdims=True))
    da = (og_ref[...].astype(F32) + da).astype(BF16)
    da_out[...] = da
    do_bf = mm(da, wo_ref[...], NT).astype(BF16)
    do = do_bf.astype(F32)
    do_out[...] = do
    kap = sum(mm(part, onehot, NT) for part in two(do * (cb_ref[...] - o)))
    kps[...] = kap
    c10 = swap_halves(do_out, dor, sems, 12, tp_peer, core)
    c11 = send(kps, kpr, sems, 13, tp_peer)

    def back(k, h, d, w):
        t = mm(d, w) * gain
        t = t - jnp.mean(t, axis=1, keepdims=True)
        gt_out[:, k * nh + h, :] = t

    for h in range(nh):
        back(0, h, do_bf[:, h * hd:(h + 1) * hd], wv_ref[h * hd:(h + 1) * hd, :])
    c10.wait()
    c12 = pass_on(dor, sems, 14, sib, core)
    c8.wait()
    c13 = pass_on(mpr, sems, 15, sib, core)
    c11.wait()
    kall = kap + pltpu.roll(kpr[...], nh, 1)
    kpk = pack(kall, nk)
    mb = m - bu_ref[...]
    for g_ in range(groups):
        aux_out[g_, 0:1] = mb[g_:g_ + 1]
        aux_out[g_, 1:2] = inv_l[g_:g_ + 1]
        aux_out[g_, 2:3] = kpk[g_:g_ + 1]
    c12.wait()
    dob = dor[...].astype(BF16)
    first = core == 0
    for h in range(nh):
        lo = (h % nq) * hd
        mine_w = wvh_ref[lo:lo + hd, :]
        sib_w = wvs[lo:lo + hd, :]
        pick = first if h < nq else jnp.logical_not(first)
        w = jnp.where(pick, mine_w, sib_w).astype(BF16)
        back(1, h, dob[:, h * hd:(h + 1) * hd], w)
    c13.wait()
    pooled_out[...] = (a + mp + mpr[...] + bdn_ref[...]).astype(BF16)
    r2.wait()
    rd[...] = rb[...] + rc[...]
    r3 = send(rd, re, sems, 16, sib)
    rf_out[mine] = rd[...]
    r3.wait()
    rf_out[theirs] = re[...]


def run_head(nh, hd, r_raw, ml, wv, wvh, wo, w_up, w_down, gain, bu, cb, b_out, hgain, hbias, b_up, b_down, out_grad):
    nb, width = out_grad.shape
    ff = w_up.shape[1]
    nd = nh * hd
    groups = ml.shape[0]
    full = pltpu.VMEM((nb, width), F32)
    heads = pltpu.VMEM((nb, nd), F32)
    stat = pltpu.VMEM((2 * groups, 128), F32)
    rhalf = pltpu.VMEM((nh // 2, nb, width), F32)
    return pl.pallas_call(
        functools.partial(head_body, nh, hd),
        in_specs=[VM] * 5 + [ANY] * 2 + [VM] * 9,
        out_specs=[VM] * 10,
        out_shape=[
            jax.ShapeDtypeStruct((nb, width), BF16),
            jax.ShapeDtypeStruct((nb, ff), BF16),
            jax.ShapeDtypeStruct((nb, ff), BF16),
            jax.ShapeDtypeStruct((nb, nd), BF16),
            jax.ShapeDtypeStruct((nb, width), BF16),
            jax.ShapeDtypeStruct((nb, width), BF16),
            jax.ShapeDtypeStruct((nb, nd), F32),
            jax.ShapeDtypeStruct((nb, 2 * nh, width), F32),
            jax.ShapeDtypeStruct((groups, 8, 128), F32),
            jax.ShapeDtypeStruct((nh, nb, width), F32),
        ],
        scratch_shapes=[
            pltpu.VMEM(w_up.shape, BF16), pltpu.VMEM(w_down.shape, BF16), pltpu.VMEM(wvh.shape, F32),
            heads, stat, heads, stat, heads, stat, heads, stat,
            full, full, pltpu.VMEM((nh, nb, width), F32), rhalf, rhalf, rhalf, rhalf, rhalf,
            full, full, full, full, heads, pltpu.VMEM((nb, 128), F32), pltpu.VMEM((nb, 128), F32),
            pltpu.VMEM((nb, ff), F32),
            pltpu.SemaphoreType.DMA((2,)), pltpu.SemaphoreType.DMA((2, 17)),
        ],
        compiler_params=pltpu.CompilerParams(collective_id=1, has_side_effects=True, vmem_limit_bytes=60 * 1024 * 1024),
        cost_estimate=pl.CostEstimate(flops=3_000_000_000, bytes_accessed=30_000_000, transcendentals=0),
        name='pool_head',
    )(r_raw, ml, wv, wvh, wo, w_up, w_down, gain, bu, cb, b_out, hgain, hbias, b_up, b_down, out_grad)


def tail_body(nh, hd, z_ref, dl_ref, rf_ref, wk_ref, wq_ref, gain_ref, z_out, dq_out, gp_out, zs, za, zs2, zb, ps, pr, sems):
    tp_peer, sib, xp, core = places()
    nk = 2 * nh
    groups = dl_ref.shape[0]
    nb = rf_ref.shape[1]
    width = z_ref.shape[1]
    cols = 128
    zs[:nh] = z_ref[...]
    zs[nh:, :cols] = jnp.concatenate([dl_ref[g, 0:1] for g in range(groups)], axis=0)
    greet([tp_peer, sib, xp])
    c1 = send(zs, za, sems, 0, sib)
    c1.wait()
    zs2[...] = zs[...] + za[...]
    c2 = send(zs2, zb, sems, 1, xp)
    c2.wait()
    z = zs2[:nh] + zb[:nh]
    dl = unpack(zs2[nh:, :cols] + zb[nh:, :cols], nk)
    fix = jnp.concatenate([jnp.sum(rf_ref[h] * dl[:, h:h + 1], axis=0, keepdims=True) for h in range(nh)], axis=0)
    z = (z - fix) * gain_ref[...] * (hd ** -0.5)
    z_out[...] = z
    dqm = mm(z.astype(BF16), wk_ref[...], NT)
    dq = jnp.sum(jnp.where(head_mask(nh, nh, hd), dqm, 0.0), axis=0, keepdims=True)
    dq_out[...] = dq
    gp = mm(jnp.broadcast_to(dq, (8, nh * hd)).astype(BF16), wq_ref[...])
    ps[...] = gp
    c3 = send(ps, pr, sems, 2, tp_peer)
    c3.wait()
    gp_out[...] = gp[:1] + pr[:1]


def run_tail(nh, hd, z, dl, rf, wk, wq, gain):
    width = z.shape[1]
    zz = pltpu.VMEM((nh + dl.shape[0], width), F32)
    pp = pltpu.VMEM((8, width), F32)
    return pl.pallas_call(
        functools.partial(tail_body, nh, hd),
        in_specs=[VM] * 6,
        out_specs=[VM] * 3,
        out_shape=[
            jax.ShapeDtypeStruct((nh, width), F32),
            jax.ShapeDtypeStruct((1, nh * hd), F32),
            jax.ShapeDtypeStruct((1, width), F32),
        ],
        scratch_shapes=[zz, zz, zz, zz, pp, pp, pltpu.SemaphoreType.DMA((2, 3))],
        compiler_params=pltpu.CompilerParams(collective_id=2, has_side_effects=True),
        cost_estimate=pl.CostEstimate(flops=50_000_000, bytes_accessed=6_000_000, transcendentals=0),
        name='query_back',
    )(z, dl, rf, wk, wq, gain)


def local_head(encoded, enc_gain, enc_bias, probe, w_query, b_query, w_key, w_value, b_value, w_out, b_out, head_gain, head_bias, w_up, b_up, w_down, b_down, out_grad):
    nh, hd = b_query.shape
    width = probe.shape[0]
    nd = nh * hd

    def flat(w):
        return jnp.transpose(w, (1, 2, 0)).reshape(nd, width)

    def heads(g):
        return jnp.transpose(g.reshape(nh, hd, width), (2, 0, 1))

    wq, wk, wv, wo = flat(w_query), flat(w_key), flat(w_value), w_out.reshape(nd, width)
    core = lax.rem(lax.axis_index('sp'), 2)
    wvh = lax.dynamic_slice_in_dim(wv, core * (nd // 2), nd // 2, 0).astype(F32)
    wvh = lax.ppermute(wvh, 'tp', [(0, 1), (1, 0)])
    gain, bias = enc_gain[None], enc_bias[None]
    gu2, bu, q, cb = run_query(nh, hd, probe[None], wq, b_query.reshape(1, nd), wk, wv, b_value.reshape(1, nd), gain, bias)
    xh, sx, rs, r_raw, ml = run_fwd(encoded, gu2, bu)
    y, g, dpre, o_bf, da, pooled, do, gt, aux, rf = run_head(nh, hd, r_raw, ml, wv, wvh, wo, w_up, w_down, gain, bu, cb, b_out[None], head_gain[None], head_bias[None], b_up[None], b_down[None], out_grad)
    grad_w_down = mm(g, out_grad, TN)
    grad_w_up = mm(y, dpre, TN)
    grad_w_out = mm(o_bf, da, TN).reshape(nh, hd, width)
    grad_encoded, z, dl = run_bwd(xh, sx, rs, gt.astype(BF16), gu2[:2 * nh], aux)
    z, dq, gp = run_tail(nh, hd, z, dl, rf, wk, wq, gain)
    r_bf = (rf * gain + bias).astype(BF16)
    do3 = do.astype(BF16).reshape(-1, nh, hd)
    grad_w_value = heads(dot('bhd,hbw->hdw', do3, r_bf))
    grad_w_key = heads(q.reshape(nh, hd, 1) * z[:, None, :])
    grad_w_query = heads(dq.reshape(nd, 1) * probe[None])
    return (pooled, grad_encoded, gp[0], grad_w_query, grad_w_key, grad_w_value, grad_w_out, grad_w_up, grad_w_down)


def solution(mesh):
    return jax.shard_map(local_head, mesh=mesh, in_specs=IN_SPECS, out_specs=OUT_SPECS, check_vma=False)
```

time: 1060 us -> 187 us (0.18)
  waiting for transfers between devices: 723 us -> 0.01 us
  matrix products: 178 us -> 18.4 us
  Pallas kernels: 0 us -> 134 us
  other arithmetic: 83.8 us -> 12.5 us
  blocking collectives: 34.6 us -> 0 us
  between operations: 14.9 us -> 0.79 us
    psum x5 -> x0, waiting for transfers between devices: 723 us -> none  [the longest x1 612 us: local_head(): lax.psum(jnp.dot(hidden, w_down, preferred_element_type=jnp.float32), 'tp')]
    dot_general x21 -> x4, matrix products: 178 us -> 18.4 us  [the longest x3 16 us: mm(): return lax.dot_general(a, b, dims, preferred_element_type=F32)]
    pallas_call x0 -> x5, Pallas kernels: none -> 134 us  [the longest x1 58.2 us: run_head(): pl.pallas_call(functools.partial(head_body, nh, hd), in_specs=[VM] * 5 +...]
    reduce_sum x10 -> x0, other arithmetic: 58 us -> none  [the longest x2 20.9 us: layer_norm(): centred = rows_in - row_mean]
    psum x4 -> x0, blocking collectives: 25.4 us -> none  [the longest x1 7.55 us: local_head(): lax.psum(jnp.sum(weights * grad_weights, axis=-1, keepdims=True), 'sp')]
    unnamed x108 -> x27, local copies, waits for them, and re-layouts: 19.3 us -> 1.88 us
    convert_element_type x5 -> x3, other arithmetic: 21.3 us -> 6.47 us  [the longest x1 4.29 us: local_head(): gt.astype(BF16)]
  transfers between devices with their start and end apart: 5 -> 1, of which waited for: 5 -> 0; matrix products, arithmetic and copies ran while one was open for 13% -> 8% of each run, Pallas kernels for 0% -> 24%
where the time goes in v1:
time: 187 us; the launch traced here: 186 us
  Pallas kernels  134 us (72%)
  matrix products  18.4 us (10%)
  local copies, waits for them, and re-layouts  16.6 us (9%)
  other arithmetic  12.5 us (7%)
  starting transfers between devices  3.39 us (2%)
    pallas_call x1, Pallas kernels, run_head(): pl.pallas_call(functools.partial(head_body, nh, hd), in_specs=[VM] * 5 +...  58.2 us
    pallas_call x1, Pallas kernels, run_query(): pl.pallas_call(functools.partial(query_body, nh, hd), in_specs=[VM] * 8,...  24.4 us
    pallas_call x1, Pallas kernels, run_fwd(): pl.pallas_call(functools.partial(fwd_body, nk), grid=(ng,), in_specs=[pl....  19.6 us
    pallas_call x1, Pallas kernels, run_bwd(): pl.pallas_call(functools.partial(bwd_body, nk), grid=(ng,), in_specs=[pl....  18.8 us
    dot_general x3, matrix products, mm(): return lax.dot_general(a, b, dims, preferred_element_type=F32)  16 us
    pallas_call x1, Pallas kernels, run_tail(): pl.pallas_call(functools.partial(tail_body, nh, hd), in_specs=[VM] * 6, o...  13.3 us
    convert_element_type x1, other arithmetic, local_head(): gt.astype(BF16)  4.29 us
  transfers between devices with their start and end apart: 1, of which 0 were waited for; matrix products, arithmetic and copies ran while one was open for 8% of the time, Pallas kernels for 24%

profile of v1, /device:TPU:0, one launch (start us, length us, event | category | flops | bytes accessed | tf_op | source)
XLA Modules:
  0.0 186.0 jit_solution(9333630016203566613)
XLA Ops:
  0.7 1.3 dynamic-slice_convert_fusion
  1.9 3.4 %collective-permute-start = (f32[320,1280]{1,0:T(8,128)S(1)}, f32[320,1280]{1,0:T(8,128)S(1)}, u32[]{:S(2)}, u32[]{:S(2)}) collective-permute-start(f32[320,1280]{1,0:T(8,128)S(1)} %dynamic-slice_convert_fusion), channel_id=1, source_target_pairs={{0,4},{4,0},{1,5},{5,1},{2,6},{6,2},{3,7},{7,3}} | collective-permute-start | bytes 4915208 | tf_op jit(solution)/shard_map/ppermute | solution.py:540
  5.3 1.3 reshape.62.bq_ref
  6.6 1.3 reshape.65.bv_ref
  8.0 1.3 broadcast_in_dim.27.gain_ref
  9.3 1.3 broadcast_in_dim.29.bo_ref
  10.6 1.3 broadcast_in_dim.30.hg_ref
  11.9 1.3 broadcast_in_dim.31.hb_ref
  13.2 1.3 broadcast_in_dim.33.bdn_ref
  14.5 1.3 broadcast_in_dim.28.bias_ref
  15.8 1.3 broadcast_in_dim.26.probe_ref
  17.1 1.3 broadcast_in_dim.32.bup_ref
  18.4 24.4 %query_fold.1 = (bf16[32,1280]{1,0:T(8,128)(2,1)}, f32[1,128]{1,0:T(1,128)}, f32[1,640]{1,0:T(1,128)}, f32[1,640]{1,0:T(1,128)}) custom-call(f32[1,1280]{1,0:T(1,128)} %broadcast_in_dim.26.probe_ref, bf16[640,1280]{1,0:T(8,128)(2,1)} %bitcast.23, f32[1,640]{1,0:T(1,128)} %reshape.62.bq_ref, bf16[640,1280]{1,0:T(8,128)(2,1)} %bitcast.25, ...), custom_call_target="tpu_custom_call" | custom-call | flops 50000000 | bytes 6000000 | tf_op jit(solution)/shard_map/query_fold/pallas_call | solution.py:262
  42.7 0.6 reduce.2
  43.4 0.1 mul.51
  43.5 1.4 slice.3.gu_ref
  44.9 19.6 %fwd_tokens.1 = (bf16[64,96,1280]{2,1,0:T(8,128)(2,1)}, f32[8,96,128]{2,1,0:T(8,128)}, f32[8,96,128]{2,1,0:T(8,128)}, f32[8,64,1280]{2,1,0:T(8,128)}, f32[8,8,128]{2,1,0:T(8,128)}) custom-call(bf16[64,96,1280]{2,1,0:T(8,128)(2,1)} %x_ref.1, bf16[32,1280]{1,0:T(8,128)(2,1)} %get-tuple-element.34.gu_ref, f32[1,128]{1,0:T(1,128)} %get-tuple-element.35.bu_ref), custom_call_target="tpu_custom_call" | custom-call | flops 8000000000 | bytes 40000000 | tf_op jit(solution)/shard_map/fwd_tokens/pallas_call | solution.py:64
  64.5 1.2 copy-done.1
  65.7 58.2 %pool_head.1 = (bf16[64,1280]{1,0:T(8,128)(2,1)}, bf16[64,2560]{1,0:T(8,128)(2,1)}, bf16[64,2560]{1,0:T(8,128)(2,1)}, bf16[64,640]{1,0:T(8,128)(2,1)}, bf16[64,1...) custom-call(f32[8,64,1280]{2,1,0:T(8,128)} %get-tuple-element.36.r_r, ...), custom_call_target="tpu_custom_call" | custom-call | flops 3000000000 | bytes 30000000 | tf_op jit(solution)/shard_map/pool_head/pallas_call | solution.py:446
  123.9 0.9 convert_element_type.14
  124.8 0.2 reshape.67
  125.0 4.3 %convert_element_type.13.gt_ref = bf16[64,16,1280]{2,1,0:T(8,128)(2,1)} convert(f32[64,16,1280]{2,1,0:T(8,128)} %get-tuple-element.43) | non-fusion elementwise | flops 1310720 | bytes 7864320 | tf_op jit(solution)/shard_map/convert_element_type | solution.py:548
  129.3 18.8 %bwd_tokens.1 = (bf16[64,96,1280]{2,1,0:T(8,128)(2,1)}, f32[8,1280]{1,0:T(8,128)}, f32[8,8,128]{2,1,0:T(8,128)}) custom-call(bf16[64,96,1280]{2,1,0:T(8,128)(2,1)} %get-tuple-element.40.xh_ref, f32[8,96,128]{2,1,0:T(8,128)} %get-tuple-element.41.sx_ref, f32[8,96,128]{2,1,0:T(8,128)} %get-tuple-element.42.rs_ref, ...), custom_call_target="tpu_custom_call" | custom-call | flops 12000000000 | bytes 40000000 | tf_op jit(solution)/shard_map/bwd_tokens/pallas_call | solution.py:132
  148.1 13.3 %query_back.1 = (f32[8,1280]{1,0:T(8,128)}, f32[1,640]{1,0:T(1,128)}, f32[1,1280]{1,0:T(1,128)}) custom-call(f32[8,1280]{1,0:T(8,128)} %get-tuple-element.46.z_ref, f32[8,8,128]{2,1,0:T(8,128)} %get-tuple-element.47.dl_ref, f32[8,64,1280]{2,1,0:T(8,128)} %get-tuple-element.48.rf_ref, bf16[640,1280]{1,0:T(8,128)(2,1)} %bitcast.26, ...), custom_call_target="tpu_custom_call" | custom-call | flops 50000000 | bytes 6000000 | tf_op jit(solution)/shard_map/query_back/pallas_call | solution.py:510
  161.4 1.4 reduce
  162.8 0.7 reduce.1
  163.6 2.3 %convolution_bitcast_fusion = f32[1280,8,80]{0,2,1:T(8,128)} fusion(f32[8,64,1280]{2,1,0:T(8,128)S(1)} %copy-done, f32[1280]{0:T(1024)S(1)} %copy-done.11, f32[1280]{0:T(1024)S(1)} %copy-done.10, bf16[64,8,80]{2,1,0:T(8,128)(2,1)S(1)} %reshape.67), kind=kOutput, calls=%fused_computation | convolution fusion | flops 106823680 | bytes 5990400 | tf_op jit(solution)/shard_map/bhd,hbw->hdw/dot_general | solution.py:24
  165.9 6.9 %fusion.5 = f32[2560,1280]{1,0:T(8,128)} fusion(bf16[64,2560]{1,0:T(8,128)(2,1)S(1)} %copy-done.3, bf16[64,1280]{1,0:T(8,128)(2,1)S(1)} %copy-done.2), kind=kOutput, calls=%fused_computation.10 | convolution fusion | flops 419430400 | bytes 13598720 | tf_op jit(solution)/shard_map/dot_general | solution.py:20
  172.8 2.3 %fusion.3 = f32[640,1280]{1,0:T(8,128)} fusion(bf16[64,640]{1,0:T(8,128)(2,1)S(1)} %copy-done.8, bf16[64,1280]{1,0:T(8,128)(2,1)S(1)} %copy-done.6), kind=kOutput, calls=%fused_computation.8 | convolution fusion | flops 104857600 | bytes 3522560 | tf_op jit(solution)/shard_map/dot_general | solution.py:20
  175.1 6.8 %fusion.4 = f32[1280,2560]{1,0:T(8,128)} fusion(bf16[64,1280]{1,0:T(8,128)(2,1)S(1)} %copy-done.5, bf16[64,2560]{1,0:T(8,128)(2,1)S(1)} %copy-done.4), kind=kOutput, calls=%fused_computation.9 | convolution fusion | flops 419430400 | bytes 13598720 | tf_op jit(solution)/shard_map/dot_general | solution.py:20
  182.0 3.3 %broadcast_multiply_fusion = (f32[1280,8,80]{0,2,1:T(8,128)}, f32[1280,8,80]{0,2,1:T(8,128)}) fusion(f32[1280,8]{0,1:T(8,128)S(1)} %bitcast.29, f32[8,80]{1,0:T(8,128)S(1)} %mul.51, f32[1280]{0:T(1024)S(1)} %copy-done.12, f32[8,80]{1,0:T(8,128)S(1)} %mul.47), kind=kLoop, calls=%fused_computation.2 | loop fusion | flops 1638400 | bytes 6604800 | tf_op jit(solution)/shard_map/mul | solution.py:553
  185.3 0.7 copy.31
  (27 shorter events, 0.1 us)
Async XLA Ops:
  1.9 62.6 %collective-permute-start = (f32[320,1280]{1,0:T(8,128)S(1)}, f32[320,1280]{1,0:T(8,128)S(1)}, u32[]{:S(2)}, u32[]{:S(2)}) collective-permute-start(f32[320,1280]{1,0:T(8,128)S(1)} %dynamic-slice_convert_fusion), channel_id=1, source_target_pairs={{0,4},{4,0},{1,5},{5,1},{2,6},{6,2},{3,7},{7,3}} | collective-permute-start | bytes 4915208 | tf_op jit(solution)/shard_map/ppermute | solution.py:540
  64.5 1.2 copy-start.1
  148.1 15.4 %copy-start = (f32[8,64,1280]{2,1,0:T(8,128)S(1)}, f32[8,64,1280]{2,1,0:T(8,128)}, u32[]{:S(2)}) copy-start(f32[8,64,1280]{2,1,0:T(8,128)} %get-tuple-element.48.rf_ref) | copy-start | bytes 7864324
  148.1 15.4 %copy-start.10 = (f32[1280]{0:T(1024)S(1)}, f32[1280]{0:T(1024)}, u32[]{:S(2)}) copy-start(f32[1280]{0:T(1024)} %param.19) | copy-start | bytes 15364
  148.1 15.4 %copy-start.11 = (f32[1280]{0:T(1024)S(1)}, f32[1280]{0:T(1024)}, u32[]{:S(2)}) copy-start(f32[1280]{0:T(1024)} %param.20) | copy-start | bytes 15364
  161.4 4.5 %copy-start.2 = (bf16[64,1280]{1,0:T(8,128)(2,1)S(1)}, bf16[64,1280]{1,0:T(8,128)(2,1)}, u32[]{:S(2)}) copy-start(bf16[64,1280]{1,0:T(8,128)(2,1)} %og_ref.1) | copy-start | bytes 491524
  161.4 4.5 %copy-start.3 = (bf16[64,2560]{1,0:T(8,128)(2,1)S(1)}, bf16[64,2560]{1,0:T(8,128)(2,1)}, u32[]{:S(2)}) copy-start(bf16[64,2560]{1,0:T(8,128)(2,1)} %get-tuple-element.58) | copy-start | bytes 983044
  165.9 6.9 %copy-start.6 = (bf16[64,1280]{1,0:T(8,128)(2,1)S(1)}, bf16[64,1280]{1,0:T(8,128)(2,1)}, u32[]{:S(2)}) copy-start(bf16[64,1280]{1,0:T(8,128)(2,1)} %get-tuple-element.55) | copy-start | bytes 491524
  165.9 6.9 %copy-start.8 = (bf16[64,640]{1,0:T(8,128)(2,1)S(1)}, bf16[64,640]{1,0:T(8,128)(2,1)}, u32[]{:S(2)}) copy-start(bf16[64,640]{1,0:T(8,128)(2,1)} %get-tuple-element.54) | copy-start | bytes 245764
  172.8 2.3 %copy-start.4 = (bf16[64,2560]{1,0:T(8,128)(2,1)S(1)}, bf16[64,2560]{1,0:T(8,128)(2,1)}, u32[]{:S(2)}) copy-start(bf16[64,2560]{1,0:T(8,128)(2,1)} %get-tuple-element.57) | copy-start | bytes 983044
  172.8 2.3 %copy-start.5 = (bf16[64,1280]{1,0:T(8,128)(2,1)S(1)}, bf16[64,1280]{1,0:T(8,128)(2,1)}, u32[]{:S(2)}) copy-start(bf16[64,1280]{1,0:T(8,128)(2,1)} %get-tuple-element.56) | copy-start | bytes 491524
  175.1 6.9 %copy-start.9 = (f32[8,1280]{1,0:T(8,128)S(1)}, f32[8,1280]{1,0:T(8,128)}, u32[]{:S(2)}) copy-start(f32[8,1280]{1,0:T(8,128)} %get-tuple-element.52) | copy-start | bytes 122884
  175.1 6.9 %copy-start.12 = (f32[1280]{0:T(1024)S(1)}, f32[1280]{0:T(1024)}, u32[]{:S(2)}) copy-start(f32[1280]{0:T(1024)} %param.21) | copy-start | bytes 15364
  182.0 3.3 %copy-start.7 = (bf16[64,1280]{1,0:T(8,128)(2,1)S(1)}, bf16[64,1280]{1,0:T(8,128)(2,1)}, u32[]{:S(2)}) copy-start(bf16[64,1280]{1,0:T(8,128)(2,1)} %get-tuple-element.70) | copy-start | bytes 491524

commit v2 on v1

--- a/solution.py
+++ b/solution.py
@@ -88,7 +88,7 @@
     )(x, gu2, bu)
 
 
-def bwd_body(nk, xh_ref, sx_ref, rs_ref, gt_ref, gu_ref, aux_ref, dx_ref, z_ref, dl_ref, zacc_ref):
+def bwd_body(nk, xh_ref, sx_ref, rs_ref, gt_ref, gu_ref, aux_ref, yt_ref, dpre_ref, ht_ref, og_ref, ot_ref, da_ref, dx_ref, z_ref, dl_ref, gup_ref, gdn_ref, gwo_ref, zacc_ref):
     step = pl.program_id(0)
     images, tokens, width = xh_ref.shape
     nh = nk // 2
@@ -97,9 +97,13 @@
     def _():
         zacc_ref[...] = jnp.zeros_like(zacc_ref)
 
+    gup_ref[...] = mm(yt_ref[...], dpre_ref[...])
+    gdn_ref[...] = mm(ht_ref[...], og_ref[...])
+    gwo_ref[...] = mm(ot_ref[...], da_ref[...])
     sx = sx_ref[0]
     rstd = rs_ref[0]
-    dpx = jnp.concatenate([mm(xh_ref[i], gt_ref[i], NT) for i in range(images)], axis=1)
+    gts = [gt_ref[:, i, :].astype(BF16) for i in range(images)]
+    dpx = jnp.concatenate([mm(xh_ref[i], gts[i], NT) for i in range(images)], axis=1)
     p = jnp.exp(sx - aux_ref[0, 0:1]) * aux_ref[0, 1:2]
     ds = p * (dpx + aux_ref[0, 2:3])
     dl_ref[0] = jnp.broadcast_to(jnp.sum(ds, axis=0, keepdims=True), dl_ref.shape[1:])
@@ -118,17 +122,18 @@
         xh = xh_ref[i]
         z = z + mm(dst[i * nk:i * nk + nh], xh)
         coef = jnp.concatenate([ca[:, i * nk:(i + 1) * nk], cb[:, i * nk:(i + 1) * nk]], axis=1)
-        dxh = mm(coef, jnp.concatenate([gu_ref[...], gt_ref[i]], axis=0))
+        dxh = mm(coef, jnp.concatenate([gu_ref[...], gts[i]], axis=0))
         dx_ref[i] = (dxh - c2[:, i * nk:i * nk + 1] * xh.astype(F32)).astype(BF16)
     zacc_ref[...] = z
     z_ref[...] = z
 
 
-def run_bwd(xh, sx, rs, gt, gu_hi, aux):
+def run_bwd(xh, sx, rs, gt, gu2, aux, yt, dpre, ht, out_grad, ot, da):
     nb, tokens, width = xh.shape
-    nk = gu_hi.shape[0]
+    nk = gu2.shape[0] // 2
     bi = 128 // nk
     ng = nb // bi
+    ff, nd = ht.shape[0], ot.shape[0]
     return pl.pallas_call(
         functools.partial(bwd_body, nk),
         grid=(ng,),
@@ -136,24 +141,36 @@
             pl.BlockSpec((bi, tokens, width), lambda i: (i, 0, 0)),
             pl.BlockSpec((1, tokens, 128), lambda i: (i, 0, 0)),
             pl.BlockSpec((1, tokens, 128), lambda i: (i, 0, 0)),
-            pl.BlockSpec((bi, nk, width), lambda i: (i, 0, 0)),
+            pl.BlockSpec((nk, bi, width), lambda i: (0, i, 0)),
             pl.BlockSpec((nk, width), lambda i: (0, 0)),
             pl.BlockSpec((1, 8, 128), lambda i: (i, 0, 0)),
+            pl.BlockSpec((width // ng, nb), lambda i: (i, 0)),
+            pl.BlockSpec((nb, ff), lambda i: (0, 0)),
+            pl.BlockSpec((ff // ng, nb), lambda i: (i, 0)),
+            pl.BlockSpec((nb, width), lambda i: (0, 0)),
+            pl.BlockSpec((nd // ng, nb), lambda i: (i, 0)),
+            pl.BlockSpec((nb, width), lambda i: (0, 0)),
         ],
         out_specs=[
             pl.BlockSpec((bi, tokens, width), lambda i: (i, 0, 0)),
             pl.BlockSpec((nk // 2, width), lambda i: (0, 0)),
             pl.BlockSpec((1, 8, 128), lambda i: (i, 0, 0)),
+            pl.BlockSpec((width // ng, ff), lambda i: (i, 0)),
+            pl.BlockSpec((ff // ng, width), lambda i: (i, 0)),
+            pl.BlockSpec((nd // ng, width), lambda i: (i, 0)),
         ],
         out_shape=[
             jax.ShapeDtypeStruct((nb, tokens, width), BF16),
             jax.ShapeDtypeStruct((nk // 2, width), F32),
             jax.ShapeDtypeStruct((ng, 8, 128), F32),
+            jax.ShapeDtypeStruct((width, ff), F32),
+            jax.ShapeDtypeStruct((ff, width), F32),
+            jax.ShapeDtypeStruct((nd, width), F32),
         ],
         scratch_shapes=[pltpu.VMEM((nk // 2, width), F32)],
         cost_estimate=pl.CostEstimate(flops=12_000_000_000, bytes_accessed=40_000_000, transcendentals=0),
         name='bwd_tokens',
-    )(xh, sx, rs, gt, gu_hi, aux)
+    )(xh, sx, rs, gt, gu2, aux, yt, dpre, ht, out_grad, ot, da)
 
 
 MESH = pl.DeviceIdType.MESH
@@ -229,26 +246,36 @@
     return jnp.concatenate([jnp.sum(rows[g * per:(g + 1) * per], axis=0, keepdims=True) for g in range(images // per)], axis=0)
 
 
-def query_body(nh, hd, probe_ref, wq_ref, bq_ref, wk_ref, wv_ref, bv_ref, gain_ref, bias_ref, gu_ref, bu_ref, q_ref, cb_ref, us_ref, ur_ref, sems):
+def row_of(ref):
+    return ref[...].reshape(1, ref.shape[0])
+
+
+def flat_heads(ref):
+    return jnp.concatenate([ref[h:h + 1, :] for h in range(ref.shape[0])], axis=1)
+
+
+def query_body(nh, hd, probe_ref, wq_ref, bq_ref, wk_ref, wv_ref, bv_ref, gain_ref, bias_ref, gu_ref, bu_ref, q_ref, cb_ref, wvq_ref, us_ref, ur_ref, sems):
     tp_peer, _, _, _ = places()
     greet([tp_peer])
-    width = probe_ref.shape[1]
+    width = probe_ref.shape[0]
     nk = 2 * nh
-    q = (mm(jnp.broadcast_to(probe_ref[...], (8, width)).astype(BF16), wq_ref[...], NT)[:1] + bq_ref[...]).astype(BF16)
+    q = (mm(jnp.broadcast_to(row_of(probe_ref), (8, width)).astype(BF16), wq_ref[...], NT)[:1] + flat_heads(bq_ref)).astype(BF16)
     q_ref[...] = q.astype(F32)
     qd = jnp.where(head_mask(nh, nh, hd), jnp.broadcast_to(q.astype(F32), (nh, nh * hd)), 0.0).astype(BF16)
     u = mm(qd, wk_ref[...])
     us_ref[...] = u
     copy = send(us_ref, ur_ref, sems, 0, tp_peer)
-    bias = bias_ref[...]
+    bias = row_of(bias_ref)
     bh, bl = two(bias)
     row = lax.broadcasted_iota(jnp.int32, (8, width), 0)
     b2 = jnp.where(row == 0, bh.astype(F32), jnp.where(row == 1, bl.astype(F32), 0.0)).astype(BF16)
-    cb_ref[...] = jnp.sum(mm(b2, wv_ref[...], NT), axis=0, keepdims=True) + bv_ref[...]
+    cb_ref[...] = jnp.sum(mm(b2, wv_ref[...], NT), axis=0, keepdims=True) + flat_heads(bv_ref)
+    quarter = wvq_ref.shape[0]
+    wvq_ref[...] = wv_ref[pl.ds(pl.multiple_of(lax.axis_index('sp') * quarter, quarter), quarter), :].astype(F32)
     copy.wait()
     scale = hd ** -0.5
     ua = jnp.concatenate([u, ur_ref[...]], axis=0) * scale
-    gu = ua * gain_ref[...]
+    gu = ua * row_of(gain_ref)
     gu = gu - jnp.mean(gu, axis=1, keepdims=True)
     gh, gl = two(gu)
     gu_ref[:nk] = gh
@@ -258,16 +285,17 @@
 
 
 def run_query(nh, hd, probe, wq, bq, wk, wv, bv, gain, bias):
-    width = probe.shape[1]
+    width = probe.shape[0]
     return pl.pallas_call(
         functools.partial(query_body, nh, hd),
         in_specs=[VM] * 8,
-        out_specs=[VM] * 4,
+        out_specs=[VM] * 5,
         out_shape=[
             jax.ShapeDtypeStruct((4 * nh, width), BF16),
             jax.ShapeDtypeStruct((1, 128), F32),
             jax.ShapeDtypeStruct((1, nh * hd), F32),
             jax.ShapeDtypeStruct((1, nh * hd), F32),
+            jax.ShapeDtypeStruct((nh * hd // 4, width), F32),
         ],
         scratch_shapes=[pltpu.VMEM((nh, width), F32), pltpu.VMEM((nh, width), F32), pltpu.SemaphoreType.DMA((2, 1))],
         compiler_params=pltpu.CompilerParams(collective_id=0, has_side_effects=True),
@@ -289,9 +317,10 @@
 
 
 def head_body(nh, hd, r_ref, ml_ref, wv_ref, wvh_ref, wo_ref, wup_hbm, wdn_hbm, gain_ref, bu_ref, cb_ref, bo_ref, hg_ref, hb_ref, bup_ref, bdn_ref, og_ref,
-              y_out, g_out, dpre_out, o_out, da_out, pooled_out, do_out, gt_out, aux_out, rf_out,
-              wup, wdn, wvs, osd, mls, ora, mra, osd2, mls2, orb, mrb, aps, apr, rs, ra, rb, rc, rd, re, dys, dyr, mps, mpr, dor, kps, kpr, dg_s, lsem, sems):
+              yt_out, gt_t_out, dpre_out, ot_out, da_out, pooled_out, do_out, gt_out, aux_out, rb_out,
+              wup, wdn, wall, osd, mls, ora, mra, osd2, mls2, orb, mrb, aps, apr, rs, ra, dys, dyr, mps, mpr, dor, kps, kpr, dg_s, lsem, sems):
     tp_peer, sib, xp, core = places()
+    sp = lax.axis_index('sp')
     nk = 2 * nh
     nb = og_ref.shape[0]
     width = og_ref.shape[1]
@@ -299,7 +328,7 @@
     load_dn = pltpu.make_async_copy(wdn_hbm, wdn, lsem.at[1])
     load_dn.start()
     load_up.start()
-    gain = gain_ref[...]
+    gain = row_of(gain_ref)
     groups = ml_ref.shape[0]
     for h in range(nh):
         rh = (r_ref[h] * gain).astype(BF16)
@@ -309,9 +338,10 @@
     mls[:groups] = m0
     mls[groups:] = l0
     greet([tp_peer, sib, xp])
-    c_wv = send(wvh_ref, wvs, sems, 0, sib)
     c1 = send(osd, ora, sems, 1, sib)
     c2 = send(mls, mra, sems, 2, sib)
+    wall[sp] = wvh_ref[...]
+    w1 = send(wvh_ref, wall.at[sp], sems, 0, sib)
     onehot = jnp.where(head_mask(128, nh, hd), 1.0, 0.0).astype(BF16)
 
     def spread(rows):
@@ -331,6 +361,7 @@
     mls2[groups:] = l1
     c3 = send(osd2, orb, sems, 3, xp)
     c4 = send(mls2, mrb, sems, 4, xp)
+    w2 = send(wvh_ref, wall.at[sp], sems, 8, xp)
     load_dn.wait()
     dg_s[...] = mm(og_ref[...], wdn[...], NT)
     c3.wait()
@@ -339,7 +370,6 @@
     inv_l = 1.0 / l
     o = o * spread(unpack(inv_l, nk)) + cb_ref[...]
     o_bf = o.astype(BF16)
-    o_out[...] = o_bf
     ap = mm(o_bf, wo_ref[...])
     aps[...] = ap
     c5 = swap_halves(aps, apr, sems, 5, tp_peer, core)
@@ -353,23 +383,21 @@
     c5.wait()
     c6 = pass_on(apr, sems, 7, sib, core)
     r1.wait()
-    rb[...] = rs[mine] + ra[...]
-    r2 = send(rb, rc, sems, 8, xp)
+    rb_out[...] = rs[mine] + ra[...]
     c6.wait()
-    a = ap + apr[...] + bo_ref[...]
+    a = ap + apr[...] + row_of(bo_ref)
     acen, arstd = row_stats(a)
     ahat = acen * arstd
-    y = (ahat * hg_ref[...] + hb_ref[...]).astype(BF16)
-    y_out[...] = y
+    hgain = row_of(hg_ref)
+    y = (ahat * hgain + row_of(hb_ref)).astype(BF16)
     load_up.wait()
-    pre = mm(y, wup[...]) + bup_ref[...]
+    pre = mm(y, wup[...]) + row_of(bup_ref)
     k0 = 0.7978845608028654
     k1 = 0.044715
     sq = pre * pre
     th = jnp.tanh(k0 * (pre + k1 * (pre * sq)))
     half = 0.5 * (1.0 + th)
     g = (pre * half).astype(BF16)
-    g_out[...] = g
     dgelu = half + 0.5 * pre * (1.0 - th * th) * (k0 * (1.0 + 3.0 * k1 * sq))
     dpre = (dg_s[...] * dgelu).astype(BF16)
     dpre_out[...] = dpre
@@ -379,11 +407,13 @@
     mp = mm(g, wdn[...])
     mps[...] = mp
     c8 = swap_halves(mps, mpr, sems, 10, tp_peer, core)
-    c_wv.wait()
+    yt_out[...] = jnp.transpose(y)
+    gt_t_out[...] = jnp.transpose(g)
+    ot_out[...] = jnp.transpose(o_bf)
     c7.wait()
     c9 = pass_on(dyr, sems, 11, sib, core)
     c9.wait()
-    dah = (dyp + dyr[...]) * hg_ref[...]
+    dah = (dyp + dyr[...]) * hgain
     da = arstd * (dah - jnp.mean(dah, axis=1, keepdims=True) - ahat * jnp.mean(dah * ahat, axis=1, keepdims=True))
     da = (og_ref[...].astype(F32) + da).astype(BF16)
     da_out[...] = da
@@ -398,12 +428,16 @@
     def back(k, h, d, w):
         t = mm(d, w) * gain
         t = t - jnp.mean(t, axis=1, keepdims=True)
-        gt_out[:, k * nh + h, :] = t
+        gt_out[k * nh + h] = t
 
     for h in range(nh):
         back(0, h, do_bf[:, h * hd:(h + 1) * hd], wv_ref[h * hd:(h + 1) * hd, :])
     c10.wait()
     c12 = pass_on(dor, sems, 14, sib, core)
+    w1.wait()
+    w2.wait()
+    from_x = lax.rem(sp + 2, 4)
+    w3 = send(wall.at[from_x], wall.at[from_x], sems, 16, sib)
     c8.wait()
     c13 = pass_on(mpr, sems, 15, sib, core)
     c11.wait()
@@ -416,22 +450,12 @@
         aux_out[g_, 2:3] = kpk[g_:g_ + 1]
     c12.wait()
     dob = dor[...].astype(BF16)
-    first = core == 0
+    w3.wait()
     for h in range(nh):
-        lo = (h % nq) * hd
-        mine_w = wvh_ref[lo:lo + hd, :]
-        sib_w = wvs[lo:lo + hd, :]
-        pick = first if h < nq else jnp.logical_not(first)
-        w = jnp.where(pick, mine_w, sib_w).astype(BF16)
-        back(1, h, dob[:, h * hd:(h + 1) * hd], w)
+        lo = (h % 2) * hd
+        back(1, h, dob[:, h * hd:(h + 1) * hd], wall[h // 2, lo:lo + hd, :].astype(BF16))
     c13.wait()
-    pooled_out[...] = (a + mp + mpr[...] + bdn_ref[...]).astype(BF16)
-    r2.wait()
-    rd[...] = rb[...] + rc[...]
-    r3 = send(rd, re, sems, 16, sib)
-    rf_out[mine] = rd[...]
-    r3.wait()
-    rf_out[theirs] = re[...]
+    pooled_out[...] = (a + mp + mpr[...] + row_of(bdn_ref)).astype(BF16)
 
 
 def run_head(nh, hd, r_raw, ml, wv, wvh, wo, w_up, w_down, gain, bu, cb, b_out, hgain, hbias, b_up, b_down, out_grad):
@@ -448,21 +472,21 @@
         in_specs=[VM] * 5 + [ANY] * 2 + [VM] * 9,
         out_specs=[VM] * 10,
         out_shape=[
-            jax.ShapeDtypeStruct((nb, width), BF16),
+            jax.ShapeDtypeStruct((width, nb), BF16),
+            jax.ShapeDtypeStruct((ff, nb), BF16),
             jax.ShapeDtypeStruct((nb, ff), BF16),
-            jax.ShapeDtypeStruct((nb, ff), BF16),
-            jax.ShapeDtypeStruct((nb, nd), BF16),
+            jax.ShapeDtypeStruct((nd, nb), BF16),
             jax.ShapeDtypeStruct((nb, width), BF16),
             jax.ShapeDtypeStruct((nb, width), BF16),
             jax.ShapeDtypeStruct((nb, nd), F32),
-            jax.ShapeDtypeStruct((nb, 2 * nh, width), F32),
+            jax.ShapeDtypeStruct((2 * nh, nb, width), F32),
             jax.ShapeDtypeStruct((groups, 8, 128), F32),
-            jax.ShapeDtypeStruct((nh, nb, width), F32),
+            jax.ShapeDtypeStruct((nh // 2, nb, width), F32),
         ],
         scratch_shapes=[
-            pltpu.VMEM(w_up.shape, BF16), pltpu.VMEM(w_down.shape, BF16), pltpu.VMEM(wvh.shape, F32),
+            pltpu.VMEM(w_up.shape, BF16), pltpu.VMEM(w_down.shape, BF16), pltpu.VMEM((4,) + wvh.shape, F32),
             heads, stat, heads, stat, heads, stat, heads, stat,
-            full, full, pltpu.VMEM((nh, nb, width), F32), rhalf, rhalf, rhalf, rhalf, rhalf,
+            full, full, pltpu.VMEM((nh, nb, width), F32), rhalf,
             full, full, full, full, heads, pltpu.VMEM((nb, 128), F32), pltpu.VMEM((nb, 128), F32),
             pltpu.VMEM((nb, ff), F32),
             pltpu.SemaphoreType.DMA((2,)), pltpu.SemaphoreType.DMA((2, 17)),
@@ -473,25 +497,32 @@
     )(r_raw, ml, wv, wvh, wo, w_up, w_down, gain, bu, cb, b_out, hgain, hbias, b_up, b_down, out_grad)
 
 
-def tail_body(nh, hd, z_ref, dl_ref, rf_ref, wk_ref, wq_ref, gain_ref, z_out, dq_out, gp_out, zs, za, zs2, zb, ps, pr, sems):
+def tail_body(nh, hd, z_ref, dl_ref, rb_ref, rc_ref, wk_ref, wq_ref, gain_ref, z_out, dq_out, gp_out, rf_out, zs, za, zs2, zb, ps, pr, rd, re, sems):
     tp_peer, sib, xp, core = places()
     nk = 2 * nh
     groups = dl_ref.shape[0]
-    nb = rf_ref.shape[1]
     width = z_ref.shape[1]
+    nq = nh // 2
+    mine = pl.ds(core * nq, nq)
+    theirs = pl.ds((1 - core) * nq, nq)
     cols = 128
     zs[:nh] = z_ref[...]
     zs[nh:, :cols] = jnp.concatenate([dl_ref[g, 0:1] for g in range(groups)], axis=0)
     greet([tp_peer, sib, xp])
     c1 = send(zs, za, sems, 0, sib)
+    rd[...] = rb_ref[...] + rc_ref[...]
+    r1 = send(rd, re, sems, 3, sib)
     c1.wait()
     zs2[...] = zs[...] + za[...]
     c2 = send(zs2, zb, sems, 1, xp)
+    rf_out[mine] = rd[...]
+    r1.wait()
+    rf_out[theirs] = re[...]
     c2.wait()
     z = zs2[:nh] + zb[:nh]
     dl = unpack(zs2[nh:, :cols] + zb[nh:, :cols], nk)
-    fix = jnp.concatenate([jnp.sum(rf_ref[h] * dl[:, h:h + 1], axis=0, keepdims=True) for h in range(nh)], axis=0)
-    z = (z - fix) * gain_ref[...] * (hd ** -0.5)
+    fix = jnp.concatenate([jnp.sum(rf_out[h] * dl[:, h:h + 1], axis=0, keepdims=True) for h in range(nh)], axis=0)
+    z = (z - fix) * row_of(gain_ref) * (hd ** -0.5)
     z_out[...] = z
     dqm = mm(z.astype(BF16), wk_ref[...], NT)
     dq = jnp.sum(jnp.where(head_mask(nh, nh, hd), dqm, 0.0), axis=0, keepdims=True)
@@ -500,27 +531,28 @@
     ps[...] = gp
     c3 = send(ps, pr, sems, 2, tp_peer)
     c3.wait()
-    gp_out[...] = gp[:1] + pr[:1]
-
-
-def run_tail(nh, hd, z, dl, rf, wk, wq, gain):
+    gp_out[...] = (gp[:1] + pr[:1]).reshape(width)
+
+
+def run_tail(nh, hd, z, dl, rb, rc, wk, wq, gain):
     width = z.shape[1]
     zz = pltpu.VMEM((nh + dl.shape[0], width), F32)
     pp = pltpu.VMEM((8, width), F32)
     return pl.pallas_call(
         functools.partial(tail_body, nh, hd),
-        in_specs=[VM] * 6,
-        out_specs=[VM] * 3,
+        in_specs=[VM] * 7,
+        out_specs=[VM] * 4,
         out_shape=[
             jax.ShapeDtypeStruct((nh, width), F32),
             jax.ShapeDtypeStruct((1, nh * hd), F32),
-            jax.ShapeDtypeStruct((1, width), F32),
-        ],
-        scratch_shapes=[zz, zz, zz, zz, pp, pp, pltpu.SemaphoreType.DMA((2, 3))],
+            jax.ShapeDtypeStruct((width,), F32),
+            jax.ShapeDtypeStruct((nh,) + rb.shape[1:], F32),
+        ],
+        scratch_shapes=[zz, zz, zz, zz, pp, pp, pltpu.VMEM(rb.shape, F32), pltpu.VMEM(rb.shape, F32), pltpu.SemaphoreType.DMA((2, 4))],
         compiler_params=pltpu.CompilerParams(collective_id=2, has_side_effects=True),
         cost_estimate=pl.CostEstimate(flops=50_000_000, bytes_accessed=6_000_000, transcendentals=0),
         name='query_back',
-    )(z, dl, rf, wk, wq, gain)
+    )(z, dl, rb, rc, wk, wq, gain)
 
 
 def local_head(encoded, enc_gain, enc_bias, probe, w_query, b_query, w_key, w_value, b_value, w_out, b_out, head_gain, head_bias, w_up, b_up, w_down, b_down, out_grad):
@@ -535,24 +567,19 @@
         return jnp.transpose(g.reshape(nh, hd, width), (2, 0, 1))
 
     wq, wk, wv, wo = flat(w_query), flat(w_key), flat(w_value), w_out.reshape(nd, width)
-    core = lax.rem(lax.axis_index('sp'), 2)
-    wvh = lax.dynamic_slice_in_dim(wv, core * (nd // 2), nd // 2, 0).astype(F32)
-    wvh = lax.ppermute(wvh, 'tp', [(0, 1), (1, 0)])
-    gain, bias = enc_gain[None], enc_bias[None]
-    gu2, bu, q, cb = run_query(nh, hd, probe[None], wq, b_query.reshape(1, nd), wk, wv, b_value.reshape(1, nd), gain, bias)
+    gu2, bu, q, cb, wvq = run_query(nh, hd, probe, wq, b_query, wk, wv, b_value, enc_gain, enc_bias)
+    wvq = lax.ppermute(wvq, 'tp', [(0, 1), (1, 0)])
     xh, sx, rs, r_raw, ml = run_fwd(encoded, gu2, bu)
-    y, g, dpre, o_bf, da, pooled, do, gt, aux, rf = run_head(nh, hd, r_raw, ml, wv, wvh, wo, w_up, w_down, gain, bu, cb, b_out[None], head_gain[None], head_bias[None], b_up[None], b_down[None], out_grad)
-    grad_w_down = mm(g, out_grad, TN)
-    grad_w_up = mm(y, dpre, TN)
-    grad_w_out = mm(o_bf, da, TN).reshape(nh, hd, width)
-    grad_encoded, z, dl = run_bwd(xh, sx, rs, gt.astype(BF16), gu2[:2 * nh], aux)
-    z, dq, gp = run_tail(nh, hd, z, dl, rf, wk, wq, gain)
-    r_bf = (rf * gain + bias).astype(BF16)
+    yt, ht, dpre, ot, da, pooled, do, gt, aux, rb = run_head(nh, hd, r_raw, ml, wv, wvq, wo, w_up, w_down, enc_gain, bu, cb, b_out, head_gain, head_bias, b_up, b_down, out_grad)
+    rc = lax.ppermute(rb, 'sp', [(i, (i + 2) % 4) for i in range(4)])
+    grad_encoded, z, dl, grad_w_up, grad_w_down, grad_w_out = run_bwd(xh, sx, rs, gt, gu2, aux, yt, dpre, ht, out_grad, ot, da)
+    z, dq, grad_probe, rf = run_tail(nh, hd, z, dl, rb, rc, wk, wq, enc_gain)
+    r_bf = (rf * enc_gain + enc_bias).astype(BF16)
     do3 = do.astype(BF16).reshape(-1, nh, hd)
     grad_w_value = heads(dot('bhd,hbw->hdw', do3, r_bf))
     grad_w_key = heads(q.reshape(nh, hd, 1) * z[:, None, :])
     grad_w_query = heads(dq.reshape(nd, 1) * probe[None])
-    return (pooled, grad_encoded, gp[0], grad_w_query, grad_w_key, grad_w_value, grad_w_out, grad_w_up, grad_w_down)
+    return (pooled, grad_encoded, grad_probe, grad_w_query, grad_w_key, grad_w_value, grad_w_out.reshape(nh, hd, width), grad_w_up, grad_w_down)
 
 
 def solution(mesh):

time: 187 us -> 132 us (0.71)
  Pallas kernels: 134 us -> 113 us
  matrix products: 18.4 us -> 4.09 us
  local copies, waits for them, and re-layouts: 16.6 us -> 3.55 us
  other arithmetic: 12.5 us -> 4.98 us
  waiting for transfers between devices: 0.01 us -> 2.08 us
    dot_general x3 -> x0, matrix products: 16 us -> none  [mm(): return lax.dot_general(a, b, dims, preferred_element_type=F32)]
    pallas_call x1, Pallas kernels: 58.2 us -> 42.5 us  [run_head(): pl.pallas_call(functools.partial(head_body, nh, hd), in_specs=[VM] * 5 +...]
    pallas_call x1, Pallas kernels: 24.4 us -> 9.73 us  [run_query(): pl.pallas_call(functools.partial(query_body, nh, hd), in_specs=[VM] * 8,...]
    broadcast_in_dim x8 -> x0, local copies, waits for them, and re-layouts: 10.4 us -> none  [the longest x2 2.59 us: local_head(): gain, bias = (enc_gain[None], enc_bias[None])]
    pallas_call x1, Pallas kernels: 18.8 us -> 27.2 us  [run_bwd(): pl.pallas_call(functools.partial(bwd_body, nk), grid=(ng,), in_specs=[pl....]
    convert_element_type x2 -> x0, other arithmetic: 5.55 us -> none  [the longest x1 4.29 us: local_head(): gt.astype(BF16)]
    reshape x2 -> x0, local copies, waits for them, and re-layouts: 2.69 us -> none  [the longest x1 1.35 us: local_head(): b_query.reshape(1, nd)]
    ppermute x1 -> x2, waiting for transfers between devices: 0.01 us -> 2.08 us  [the longest x1 2.07 us: local_head(): rc = lax.ppermute(rb, 'sp', [(i, (i + 2) % 4) for i in range(4)])]
  transfers between devices with their start and end apart: 1 -> 2, of which waited for: 0 -> 1; matrix products, arithmetic and copies ran while one was open for 8% -> 1% of each run, Pallas kernels for 24% -> 36%
where the time goes in v2:
time: 132 us; the launch traced here: 131 us
  Pallas kernels  113 us (86%)
  other arithmetic  4.98 us (4%)
  matrix products  4.09 us (3%)
  local copies, waits for them, and re-layouts  3.55 us (3%)
  starting transfers between devices  2.6 us (2%)
  waiting for transfers between devices  2.08 us (2%)
    pallas_call x1, Pallas kernels, run_head(): pl.pallas_call(functools.partial(head_body, nh, hd), in_specs=[VM] * 5 +...  42.5 us
    pallas_call x1, Pallas kernels, run_bwd(): pl.pallas_call(functools.partial(bwd_body, nk), grid=(ng,), in_specs=[pl....  27.2 us
    pallas_call x1, Pallas kernels, run_fwd(): pl.pallas_call(functools.partial(fwd_body, nk), grid=(ng,), in_specs=[pl....  19.6 us
    pallas_call x1, Pallas kernels, run_tail(): pl.pallas_call(functools.partial(tail_body, nh, hd), in_specs=[VM] * 7, o...  14.1 us
    pallas_call x1, Pallas kernels, run_query(): pl.pallas_call(functools.partial(query_body, nh, hd), in_specs=[VM] * 8,...  9.73 us
    dot_general x1, matrix products, dot(): return jnp.einsum(spec, a, b, preferred_element_type=F32)  4.09 us
    mul x1, other arithmetic, local_head(): grad_w_key = heads(q.reshape(nh, hd, 1) * z[:, None, :])  3.34 us
    unnamed x20, local copies, waits for them, and re-layouts  3.24 us
  transfers between devices with their start and end apart: 2, of which 1 were waited for; matrix products, arithmetic and copies ran while one was open for 1% of the time, Pallas kernels for 36%

profile of v2, /device:TPU:0, one launch (start us, length us, event | category | flops | bytes accessed | tf_op | source)
XLA Modules:
  0.0 131.2 jit_solution(1897825056882069982)
XLA Ops:
  0.6 9.7 %query_fold.1 = (bf16[32,1280]{1,0:T(8,128)(2,1)}, f32[1,128]{1,0:T(1,128)}, f32[1,640]{1,0:T(1,128)}, f32[1,640]{1,0:T(1,128)}, f32[160,1280]{1,0:T(8,128)}) custom-call(f32[1280]{0:T(1024)} %probe_ref.1, bf16[640,1280]{1,0:T(8,128)(2,1)} %bitcast.16, f32[8,80]{1,0:T(8,128)} %bq_ref.1, bf16[640,1280]{1,0:T(8,128)(2,1)} %bitcast.18, ...), custom_call_target="tpu_custom_call" | custom-call | flops 50000000 | bytes 6000000 | tf_op jit(solution)/shard_map/query_fold/pallas_call | solution.py:289
  10.4 2.0 %collective-permute-start = (f32[160,1280]{1,0:T(8,128)}, f32[160,1280]{1,0:T(8,128)S(1)}, u32[]{:S(2)}, u32[]{:S(2)}) collective-permute-start(f32[160,1280]{1,0:T(8,128)} %get-tuple-element.43), channel_id=1, source_target_pairs={{0,4},{4,0},{1,5},{5,1},{2,6},{6,2},{3,7},{7,3}} | collective-permute-start | bytes 2457608 | tf_op jit(solution)/shard_map/ppermute | solution.py:571
  12.4 19.6 %fwd_tokens.1 = (bf16[64,96,1280]{2,1,0:T(8,128)(2,1)}, f32[8,96,128]{2,1,0:T(8,128)}, f32[8,96,128]{2,1,0:T(8,128)}, f32[8,64,1280]{2,1,0:T(8,128)}, f32[8,8,128]{2,1,0:T(8,128)}) custom-call(bf16[64,96,1280]{2,1,0:T(8,128)(2,1)} %x_ref.1, bf16[32,1280]{1,0:T(8,128)(2,1)} %get-tuple-element.39.gu_ref, f32[1,128]{1,0:T(1,128)} %get-tuple-element.40.bu_ref), custom_call_target="tpu_custom_call" | custom-call | flops 8000000000 | bytes 40000000 | tf_op jit(solution)/shard_map/fwd_tokens/pallas_call | solution.py:64
  32.1 0.0 collective-permute-done.wvh_ref
  32.1 0.0 copy-start.1
  32.1 0.9 copy-done.1
  33.0 42.5 %pool_head.1 = (bf16[1280,64]{1,0:T(8,128)(2,1)}, bf16[2560,64]{1,0:T(8,128)(2,1)}, bf16[64,2560]{1,0:T(8,128)(2,1)}, bf16[640,64]{1,0:T(8,128)(2,1)}, bf16[64,1...) custom-call(f32[8,64,1280]{2,1,0:T(8,128)} %get-tuple-element.41.r_r, ...), custom_call_target="tpu_custom_call" | custom-call | flops 3000000000 | bytes 30000000 | tf_op jit(solution)/shard_map/pool_head/pallas_call | solution.py:470
  75.4 0.6 collective-permute-start.1
  76.0 0.0 copy-done.8
  76.0 0.1 mul.47
  76.1 0.9 convert_element_type.6
  77.0 0.2 reshape.59
  77.2 27.2 %bwd_tokens.1 = (bf16[64,96,1280]{2,1,0:T(8,128)(2,1)}, f32[8,1280]{1,0:T(8,128)}, f32[8,8,128]{2,1,0:T(8,128)}, f32[1280,2560]{1,0:T(8,128)}, f32[2560,1280]{1,0:T(8,128)}, /*index=5*/f32[640,1280]{1,0:T(8,128)}) custom-call(bf16[64,96,1280]{2,1,0:T(8,128)(2,1)} %get-tuple-element.46.xh_ref, f32[8,96,128]{2,1,0:T(8,128)} %get-tuple-element.47.sx_ref, ...), custom_call_target="tpu_custom_call" | custom-call | flops 12000000000 | bytes 40000000 | tf_op jit(solution)/shard_map/bwd_tokens/pallas_call | solution.py:137
  104.4 0.0 copy-start.3
  104.4 0.0 copy-start.5
  104.4 2.1 %collective-permute-done.1.rc_ref = f32[4,64,1280]{2,1,0:T(8,128)S(1)} collective-permute-done((f32[4,64,1280]{2,1,0:T(8,128)}, f32[4,64,1280]{2,1,0:T(8,128)S(1)}, u32[]{:S(2)}, u32[]{:S(2)}) %collective-permute-start.1) | collective-permute-done | bytes 1310752 | tf_op jit(solution)/shard_map/ppermute | solution.py:574
  106.5 1.1 copy-done
  107.6 14.1 %query_back.1 = (f32[8,1280]{1,0:T(8,128)}, f32[1,640]{1,0:T(1,128)}, f32[1280]{0:T(1024)}, f32[8,64,1280]{2,1,0:T(8,128)}) custom-call(f32[8,1280]{1,0:T(8,128)} %get-tuple-element.57.z_ref, f32[8,8,128]{2,1,0:T(8,128)} %get-tuple-element.58.dl_ref, f32[4,64,1280]{2,1,0:T(8,128)} %get-tuple-element.59.rb_ref, f32[4,64,1280]{2,1,0:T(8,128)} %copy-done, ...), custom_call_target="tpu_custom_call" | custom-call | flops 50000000 | bytes 6000000 | tf_op jit(solution)/shard_map/query_back/pallas_call | solution.py:541
  121.6 0.0 copy-start.4
  121.6 0.0 copy-start.6
  121.7 0.7 reduce
  122.4 0.1 mul.43
  122.4 0.0 copy-done.3
  122.4 0.0 copy-done.5
  122.4 4.1 %convolution_bitcast_fusion = f32[1280,8,80]{0,2,1:T(8,128)} fusion(f32[8,64,1280]{2,1,0:T(8,128)} %get-tuple-element.65, f32[1280]{0:T(1024)S(1)} %copy-done.5, f32[1280]{0:T(1024)S(1)} %copy-done.3, bf16[64,8,80]{2,1,0:T(8,128)(2,1)S(1)} %reshape.59), kind=kOutput, calls=%fused_computation | convolution fusion | flops 106823680 | bytes 5990400 | tf_op jit(solution)/shard_map/bhd,hbw->hdw/dot_general | solution.py:24
  126.5 0.0 copy-done.4
  126.5 0.0 copy-done.6
  126.6 3.3 %broadcast_multiply_fusion = (f32[1280,8,80]{0,2,1:T(8,128)}, f32[1280,8,80]{0,2,1:T(8,128)}) fusion(f32[1280,8]{0,1:T(8,128)S(1)} %bitcast.21, f32[8,80]{1,0:T(8,128)S(1)} %mul.47, f32[1280]{0:T(1024)S(1)} %copy-done.6, f32[8,80]{1,0:T(8,128)S(1)} %mul.43), kind=kLoop, calls=%fused_computation.2 | loop fusion | flops 1638400 | bytes 6604800 | tf_op jit(solution)/shard_map/mul | solution.py:580
  129.9 0.0 copy-done.2
  129.9 0.7 copy.32
  130.6 0.0 copy-done.7
  130.6 0.6 copy.33
  (5 shorter events, 0.0 us)
Async XLA Ops:
  10.4 21.7 %collective-permute-start = (f32[160,1280]{1,0:T(8,128)}, f32[160,1280]{1,0:T(8,128)S(1)}, u32[]{:S(2)}, u32[]{:S(2)}) collective-permute-start(f32[160,1280]{1,0:T(8,128)} %get-tuple-element.43), channel_id=1, source_target_pairs={{0,4},{4,0},{1,5},{5,1},{2,6},{6,2},{3,7},{7,3}} | collective-permute-start | bytes 2457608 | tf_op jit(solution)/shard_map/ppermute | solution.py:571
  32.1 0.9 copy-start.1
  33.0 43.0 %copy-start.8 = (f32[1,640]{1,0:T(1,128)S(1)}, f32[1,640]{1,0:T(1,128)}, u32[]{:S(2)}) copy-start(f32[1,640]{1,0:T(1,128)} %get-tuple-element.62) | copy-start | bytes 7684
  75.4 31.1 %collective-permute-start.1 = (f32[4,64,1280]{2,1,0:T(8,128)}, f32[4,64,1280]{2,1,0:T(8,128)S(1)}, u32[]{:S(2)}, u32[]{:S(2)}) collective-permute-start(f32[4,64,1280]{2,1,0:T(8,128)} %get-tuple-element.59.rb_ref), channel_id=1, source_target_pairs={{0,2},{1,3},{2,0},{3,1},{4,6},{5,7},{6,4},{7,5}} | collective-permute-start | bytes 3932168 | tf_op jit(solution)/shard_map/ppermute | solution.py:574
  104.4 18.0 %copy-start.3 = (f32[1280]{0:T(1024)S(1)}, f32[1280]{0:T(1024)}, u32[]{:S(2)}) copy-start(f32[1280]{0:T(1024)} %gain_ref.5) | copy-start | bytes 15364
  104.4 18.0 %copy-start.5 = (f32[1280]{0:T(1024)S(1)}, f32[1280]{0:T(1024)}, u32[]{:S(2)}) copy-start(f32[1280]{0:T(1024)} %bias_ref.1) | copy-start | bytes 15364
  106.5 1.1 copy-start
  121.6 4.9 %copy-start.4 = (f32[8,1280]{1,0:T(8,128)S(1)}, f32[8,1280]{1,0:T(8,128)}, u32[]{:S(2)}) copy-start(f32[8,1280]{1,0:T(8,128)} %get-tuple-element.63) | copy-start | bytes 122884
  121.6 4.9 %copy-start.6 = (f32[1280]{0:T(1024)S(1)}, f32[1280]{0:T(1024)}, u32[]{:S(2)}) copy-start(f32[1280]{0:T(1024)} %probe_ref.1) | copy-start | bytes 15364
  126.5 3.3 %copy-start.2 = (bf16[64,1280]{1,0:T(8,128)(2,1)S(1)}, bf16[64,1280]{1,0:T(8,128)(2,1)}, u32[]{:S(2)}) copy-start(bf16[64,1280]{1,0:T(8,128)(2,1)} %get-tuple-element.80) | copy-start | bytes 491524
  126.5 4.0 %copy-start.7 = (f32[1280]{0:T(1024)S(1)}, f32[1280]{0:T(1024)}, u32[]{:S(2)}) copy-start(f32[1280]{0:T(1024)} %get-tuple-element.82) | copy-start | bytes 15364

commit v3 on v2

--- a/solution.py
+++ b/solution.py
@@ -30,15 +30,36 @@
     return cen, lax.rsqrt(jnp.mean(cen * cen, axis=-1, keepdims=True) + NORM_EPS)
 
 
-def fwd_body(nk, x_ref, gu_ref, bu_ref, xh_ref, sx_ref, rs_ref, r_ref, ml_ref):
+def fwd_body(nk, x_ref, gu_ref, bu_ref, xh_ref, sx_ref, rs_ref, r_ref, ml_ref, st_ref):
     images, tokens, width = x_ref.shape
     nh = nk // 2
-    strip = 16
+    eye = lax.broadcasted_iota(jnp.int32, (tokens, tokens), 0) == lax.broadcasted_iota(jnp.int32, (tokens, tokens), 1)
+    ones = jnp.ones((16, width), BF16)
+    worst = jnp.full((tokens, 1), -1.0, F32)
     for i in range(images):
-        for j in range(0, tokens, strip):
-            cen, rstd = row_stats(x_ref[i, j:j + strip, :].astype(F32))
-            xh_ref[i, j:j + strip, :] = (cen * rstd).astype(BF16)
-            rs_ref[0, j:j + strip, i * nk:(i + 1) * nk] = jnp.broadcast_to(rstd, (strip, nk))
+        xb = x_ref[i]
+        mean = mm(xb, ones, NT)[:, :1] * (1.0 / width)
+        square = jnp.sum(jnp.where(eye, mm(xb, xb, NT), 0.0), axis=1, keepdims=True) * (1.0 / width)
+        var = square - mean * mean
+        worst = jnp.maximum(worst, mean * mean - 256.0 * var)
+        st_ref[0, i] = jnp.broadcast_to(mean, (tokens, 128))
+        st_ref[1, i] = jnp.broadcast_to(lax.rsqrt(jnp.maximum(var, 0.0) + NORM_EPS), (tokens, 128))
+
+    @pl.when(jnp.max(worst) > 0.0)
+    def _():
+        for i in range(images):
+            def redo(j, carry, i=i):
+                rows = pl.ds(pl.multiple_of(j * 16, 16), 16)
+                xs = x_ref[i, rows, :].astype(F32)
+                st_ref[0, i, rows, :] = jnp.broadcast_to(jnp.mean(xs, axis=-1, keepdims=True), (16, 128))
+                st_ref[1, i, rows, :] = jnp.broadcast_to(row_stats(xs)[1], (16, 128))
+                return carry
+            lax.fori_loop(0, tokens // 16, redo, 0)
+
+    for i in range(images):
+        rstd = st_ref[1, i, :, :1]
+        xh_ref[i] = ((x_ref[i].astype(F32) - st_ref[0, i, :, :1]) * rstd).astype(BF16)
+        rs_ref[0, :, i * nk:(i + 1) * nk] = st_ref[1, i, :, :nk]
     parts = []
     for i in range(images):
         s2 = mm(xh_ref[i], gu_ref[...], NT)
@@ -83,6 +104,7 @@
             jax.ShapeDtypeStruct((nk // 2, nb, width), F32),
             jax.ShapeDtypeStruct((ng, 8, 128), F32),
         ],
+        scratch_shapes=[pltpu.VMEM((2, bi, tokens, 128), F32)],
         cost_estimate=pl.CostEstimate(flops=8_000_000_000, bytes_accessed=40_000_000, transcendentals=0),
         name='fwd_tokens',
     )(x, gu2, bu)
@@ -260,8 +282,9 @@
     width = probe_ref.shape[0]
     nk = 2 * nh
     q = (mm(jnp.broadcast_to(row_of(probe_ref), (8, width)).astype(BF16), wq_ref[...], NT)[:1] + flat_heads(bq_ref)).astype(BF16)
-    q_ref[...] = q.astype(F32)
     qd = jnp.where(head_mask(nh, nh, hd), jnp.broadcast_to(q.astype(F32), (nh, nh * hd)), 0.0).astype(BF16)
+    qf = qd.astype(F32)
+    q_ref[...] = jnp.transpose(jnp.concatenate([qf, qf, qf, jnp.zeros_like(qf)], axis=0)).astype(BF16)
     u = mm(qd, wk_ref[...])
     us_ref[...] = u
     copy = send(us_ref, ur_ref, sems, 0, tp_peer)
@@ -293,7 +316,7 @@
         out_shape=[
             jax.ShapeDtypeStruct((4 * nh, width), BF16),
             jax.ShapeDtypeStruct((1, 128), F32),
-            jax.ShapeDtypeStruct((1, nh * hd), F32),
+            jax.ShapeDtypeStruct((nh * hd, 4 * nh), BF16),
             jax.ShapeDtypeStruct((1, nh * hd), F32),
             jax.ShapeDtypeStruct((nh * hd // 4, width), F32),
         ],
@@ -317,8 +340,8 @@
 
 
 def head_body(nh, hd, r_ref, ml_ref, wv_ref, wvh_ref, wo_ref, wup_hbm, wdn_hbm, gain_ref, bu_ref, cb_ref, bo_ref, hg_ref, hb_ref, bup_ref, bdn_ref, og_ref,
-              yt_out, gt_t_out, dpre_out, ot_out, da_out, pooled_out, do_out, gt_out, aux_out, rb_out,
-              wup, wdn, wall, osd, mls, ora, mra, osd2, mls2, orb, mrb, aps, apr, rs, ra, dys, dyr, mps, mpr, dor, kps, kpr, dg_s, lsem, sems):
+              yt_out, gt_t_out, dpre_out, ot_out, da_out, pooled_out, dot_out, gt_out, aux_out, rb_out,
+              wup, wdn, wall, osd, mls, ora, mra, osd2, mls2, orb, mrb, aps, apr, rs, ra, dys, dyr, mps, mpr, dos, dor, kps, kpr, dg_s, lsem, sems):
     tp_peer, sib, xp, core = places()
     sp = lax.axis_index('sp')
     nk = 2 * nh
@@ -419,10 +442,10 @@
     da_out[...] = da
     do_bf = mm(da, wo_ref[...], NT).astype(BF16)
     do = do_bf.astype(F32)
-    do_out[...] = do
+    dos[...] = do
     kap = sum(mm(part, onehot, NT) for part in two(do * (cb_ref[...] - o)))
     kps[...] = kap
-    c10 = swap_halves(do_out, dor, sems, 12, tp_peer, core)
+    c10 = swap_halves(dos, dor, sems, 12, tp_peer, core)
     c11 = send(kps, kpr, sems, 13, tp_peer)
 
     def back(k, h, d, w):
@@ -430,6 +453,7 @@
         t = t - jnp.mean(t, axis=1, keepdims=True)
         gt_out[k * nh + h] = t
 
+    dot_out[...] = jnp.transpose(do_bf)
     for h in range(nh):
         back(0, h, do_bf[:, h * hd:(h + 1) * hd], wv_ref[h * hd:(h + 1) * hd, :])
     c10.wait()
@@ -478,7 +502,7 @@
             jax.ShapeDtypeStruct((nd, nb), BF16),
             jax.ShapeDtypeStruct((nb, width), BF16),
             jax.ShapeDtypeStruct((nb, width), BF16),
-            jax.ShapeDtypeStruct((nb, nd), F32),
+            jax.ShapeDtypeStruct((nd, nb), BF16),
             jax.ShapeDtypeStruct((2 * nh, nb, width), F32),
             jax.ShapeDtypeStruct((groups, 8, 128), F32),
             jax.ShapeDtypeStruct((nh // 2, nb, width), F32),
@@ -487,7 +511,7 @@
             pltpu.VMEM(w_up.shape, BF16), pltpu.VMEM(w_down.shape, BF16), pltpu.VMEM((4,) + wvh.shape, F32),
             heads, stat, heads, stat, heads, stat, heads, stat,
             full, full, pltpu.VMEM((nh, nb, width), F32), rhalf,
-            full, full, full, full, heads, pltpu.VMEM((nb, 128), F32), pltpu.VMEM((nb, 128), F32),
+            full, full, full, full, heads, heads, pltpu.VMEM((nb, 128), F32), pltpu.VMEM((nb, 128), F32),
             pltpu.VMEM((nb, ff), F32),
             pltpu.SemaphoreType.DMA((2,)), pltpu.SemaphoreType.DMA((2, 17)),
         ],
@@ -497,7 +521,7 @@
     )(r_raw, ml, wv, wvh, wo, w_up, w_down, gain, bu, cb, b_out, hgain, hbias, b_up, b_down, out_grad)
 
 
-def tail_body(nh, hd, z_ref, dl_ref, rb_ref, rc_ref, wk_ref, wq_ref, gain_ref, z_out, dq_out, gp_out, rf_out, zs, za, zs2, zb, ps, pr, rd, re, sems):
+def tail_body(nh, hd, z_ref, dl_ref, rb_ref, rc_ref, wk_hbm, wq_hbm, gain_ref, probe_ref, z_out, dq_out, pm_out, gp_out, rf_out, zs, za, zs2, zb, ds, da, ds2, db, ps, pr, rd, re, wk, wq, lsem, sems):
     tp_peer, sib, xp, core = places()
     nk = 2 * nh
     groups = dl_ref.shape[0]
@@ -505,54 +529,99 @@
     nq = nh // 2
     mine = pl.ds(core * nq, nq)
     theirs = pl.ds((1 - core) * nq, nq)
-    cols = 128
-    zs[:nh] = z_ref[...]
-    zs[nh:, :cols] = jnp.concatenate([dl_ref[g, 0:1] for g in range(groups)], axis=0)
+    load_k = pltpu.make_async_copy(wk_hbm, wk, lsem.at[0])
+    load_q = pltpu.make_async_copy(wq_hbm, wq, lsem.at[1])
+    load_k.start()
+    load_q.start()
+    ds[...] = jnp.concatenate([dl_ref[g, 0:1] for g in range(groups)], axis=0)
+    zs[...] = z_ref[...]
     greet([tp_peer, sib, xp])
     c1 = send(zs, za, sems, 0, sib)
+    d1 = send(ds, da, sems, 1, sib)
     rd[...] = rb_ref[...] + rc_ref[...]
-    r1 = send(rd, re, sems, 3, sib)
+    r1 = send(rd, re, sems, 2, sib)
     c1.wait()
+    d1.wait()
     zs2[...] = zs[...] + za[...]
-    c2 = send(zs2, zb, sems, 1, xp)
+    ds2[...] = ds[...] + da[...]
+    c2 = send(zs2, zb, sems, 3, xp)
+    d2 = send(ds2, db, sems, 4, xp)
     rf_out[mine] = rd[...]
+    p1, p2, p3 = three(row_of(probe_ref))
+    pm_out[...] = jnp.concatenate([p1, p2, p1, p3, p2, p1, jnp.zeros((2, width), BF16)], axis=0)
     r1.wait()
     rf_out[theirs] = re[...]
+    load_k.wait()
+    load_q.wait()
     c2.wait()
-    z = zs2[:nh] + zb[:nh]
-    dl = unpack(zs2[nh:, :cols] + zb[nh:, :cols], nk)
+    d2.wait()
+    dl = unpack(ds2[...] + db[...], nk)
     fix = jnp.concatenate([jnp.sum(rf_out[h] * dl[:, h:h + 1], axis=0, keepdims=True) for h in range(nh)], axis=0)
-    z = (z - fix) * row_of(gain_ref) * (hd ** -0.5)
-    z_out[...] = z
-    dqm = mm(z.astype(BF16), wk_ref[...], NT)
+    z = (zs2[...] + zb[...] - fix) * row_of(gain_ref) * (hd ** -0.5)
+    dqm = mm(z.astype(BF16), wk[...], NT)
     dq = jnp.sum(jnp.where(head_mask(nh, nh, hd), dqm, 0.0), axis=0, keepdims=True)
-    dq_out[...] = dq
-    gp = mm(jnp.broadcast_to(dq, (8, nh * hd)).astype(BF16), wq_ref[...])
+    gp = mm(jnp.broadcast_to(dq, (8, nh * hd)).astype(BF16), wq[...])[:1]
     ps[...] = gp
-    c3 = send(ps, pr, sems, 2, tp_peer)
+    c3 = send(ps, pr, sems, 5, tp_peer)
+    z_out[...] = jnp.concatenate(list(three(z)) + [jnp.zeros((nh, width), BF16)], axis=0)
+    d1_, d2_, d3_ = (part.astype(F32) for part in three(dq))
+    zero = jnp.zeros_like(dq)
+    dq_out[...] = jnp.transpose(jnp.concatenate([d1_, d1_, d2_, d1_, d2_, d3_, zero, zero], axis=0)).astype(BF16)
     c3.wait()
-    gp_out[...] = (gp[:1] + pr[:1]).reshape(width)
-
-
-def run_tail(nh, hd, z, dl, rb, rc, wk, wq, gain):
+    gp_out[...] = (gp + pr[...]).reshape(width)
+
+
+def run_tail(nh, hd, z, dl, rb, rc, wk, wq, gain, probe):
     width = z.shape[1]
-    zz = pltpu.VMEM((nh + dl.shape[0], width), F32)
-    pp = pltpu.VMEM((8, width), F32)
+    nd = nh * hd
+    zz = pltpu.VMEM((nh, width), F32)
+    dd = pltpu.VMEM((dl.shape[0], 128), F32)
+    pp = pltpu.VMEM((1, width), F32)
     return pl.pallas_call(
         functools.partial(tail_body, nh, hd),
-        in_specs=[VM] * 7,
-        out_specs=[VM] * 4,
+        in_specs=[VM] * 4 + [ANY] * 2 + [VM] * 2,
+        out_specs=[VM] * 5,
         out_shape=[
-            jax.ShapeDtypeStruct((nh, width), F32),
-            jax.ShapeDtypeStruct((1, nh * hd), F32),
+            jax.ShapeDtypeStruct((4 * nh, width), BF16),
+            jax.ShapeDtypeStruct((nd, 8), BF16),
+            jax.ShapeDtypeStruct((8, width), BF16),
             jax.ShapeDtypeStruct((width,), F32),
             jax.ShapeDtypeStruct((nh,) + rb.shape[1:], F32),
         ],
-        scratch_shapes=[zz, zz, zz, zz, pp, pp, pltpu.VMEM(rb.shape, F32), pltpu.VMEM(rb.shape, F32), pltpu.SemaphoreType.DMA((2, 4))],
+        scratch_shapes=[zz, zz, zz, zz, dd, dd, dd, dd, pp, pp, pltpu.VMEM(rb.shape, F32), pltpu.VMEM(rb.shape, F32), pltpu.VMEM(wk.shape, BF16), pltpu.VMEM(wq.shape, BF16), pltpu.SemaphoreType.DMA((2,)), pltpu.SemaphoreType.DMA((2, 6))],
         compiler_params=pltpu.CompilerParams(collective_id=2, has_side_effects=True),
         cost_estimate=pl.CostEstimate(flops=50_000_000, bytes_accessed=6_000_000, transcendentals=0),
         name='query_back',
-    )(z, dl, rb, rc, wk, wq, gain)
+    )(z, dl, rb, rc, wk, wq, gain, probe)
+
+
+def outer_body(hd, qt_ref, z_ref, dqt_ref, pm_ref, dot_ref, rf_ref, gain_ref, bias_ref, pooled_ref, gp_ref, gwk_ref, gwq_ref, gwv_ref, pooled_out, gp_out):
+    gwk_ref[...] = mm(qt_ref[...], z_ref[...])
+    gwq_ref[...] = mm(dqt_ref[...], pm_ref[...])
+    gain, bias = row_of(gain_ref), row_of(bias_ref)
+    for h in range(rf_ref.shape[0]):
+        r = (rf_ref[h] * gain + bias).astype(BF16)
+        gwv_ref[h * hd:(h + 1) * hd, :] = mm(dot_ref[h * hd:(h + 1) * hd, :], r)
+    pooled_out[...] = pooled_ref[...]
+    gp_out[...] = gp_ref[...]
+
+
+def run_outer(nh, hd, qt, z, dqt, pm, dot, rf, gain, bias, pooled, gp):
+    nb, width = pooled.shape
+    per = 2
+    rows = per * hd
+    blk = lambda a: pl.BlockSpec((rows, a.shape[1]), lambda i: (i, 0))
+    whole = lambda a: pl.BlockSpec(a.shape, lambda i: (0,) * a.ndim)
+    big = jax.ShapeDtypeStruct((nh * hd, width), F32)
+    return pl.pallas_call(
+        functools.partial(outer_body, hd),
+        grid=(nh // per,),
+        in_specs=[blk(qt), whole(z), blk(dqt), whole(pm), blk(dot), pl.BlockSpec((per, nb, width), lambda i: (i, 0, 0)), whole(gain), whole(bias), whole(pooled), whole(gp)],
+        out_specs=[blk(big), blk(big), blk(big), whole(pooled), whole(gp)],
+        out_shape=[big, big, big, jax.ShapeDtypeStruct(pooled.shape, BF16), jax.ShapeDtypeStruct(gp.shape, F32)],
+        cost_estimate=pl.CostEstimate(flops=300_000_000, bytes_accessed=14_000_000, transcendentals=0),
+        name='outer_grads',
+    )(qt, z, dqt, pm, dot, rf, gain, bias, pooled, gp)
 
 
 def local_head(encoded, enc_gain, enc_bias, probe, w_query, b_query, w_key, w_value, b_value, w_out, b_out, head_gain, head_bias, w_up, b_up, w_down, b_down, out_grad):
@@ -567,18 +636,15 @@
         return jnp.transpose(g.reshape(nh, hd, width), (2, 0, 1))
 
     wq, wk, wv, wo = flat(w_query), flat(w_key), flat(w_value), w_out.reshape(nd, width)
-    gu2, bu, q, cb, wvq = run_query(nh, hd, probe, wq, b_query, wk, wv, b_value, enc_gain, enc_bias)
+    gu2, bu, qt, cb, wvq = run_query(nh, hd, probe, wq, b_query, wk, wv, b_value, enc_gain, enc_bias)
     wvq = lax.ppermute(wvq, 'tp', [(0, 1), (1, 0)])
     xh, sx, rs, r_raw, ml = run_fwd(encoded, gu2, bu)
-    yt, ht, dpre, ot, da, pooled, do, gt, aux, rb = run_head(nh, hd, r_raw, ml, wv, wvq, wo, w_up, w_down, enc_gain, bu, cb, b_out, head_gain, head_bias, b_up, b_down, out_grad)
+    yt, ht, dpre, ot, da, pooled, do_t, gt, aux, rb = run_head(nh, hd, r_raw, ml, wv, wvq, wo, w_up, w_down, enc_gain, bu, cb, b_out, head_gain, head_bias, b_up, b_down, out_grad)
     rc = lax.ppermute(rb, 'sp', [(i, (i + 2) % 4) for i in range(4)])
     grad_encoded, z, dl, grad_w_up, grad_w_down, grad_w_out = run_bwd(xh, sx, rs, gt, gu2, aux, yt, dpre, ht, out_grad, ot, da)
-    z, dq, grad_probe, rf = run_tail(nh, hd, z, dl, rb, rc, wk, wq, enc_gain)
-    r_bf = (rf * enc_gain + enc_bias).astype(BF16)
-    do3 = do.astype(BF16).reshape(-1, nh, hd)
-    grad_w_value = heads(dot('bhd,hbw->hdw', do3, r_bf))
-    grad_w_key = heads(q.reshape(nh, hd, 1) * z[:, None, :])
-    grad_w_query = heads(dq.reshape(nd, 1) * probe[None])
+    z, dqt, pm, grad_probe, rf = run_tail(nh, hd, z, dl, rb, rc, wk, wq, enc_gain, probe)
+    gwk, gwq, gwv, pooled, grad_probe = run_outer(nh, hd, qt, z, dqt, pm, do_t, rf, enc_gain, enc_bias, pooled, grad_probe)
+    grad_w_query, grad_w_key, grad_w_value = heads(gwq), heads(gwk), heads(gwv)
     return (pooled, grad_encoded, grad_probe, grad_w_query, grad_w_key, grad_w_value, grad_w_out.reshape(nh, hd, width), grad_w_up, grad_w_down)
 
 

time: 132 us -> 134 us (1.015)
  Pallas kernels: 113 us -> 125 us
  other arithmetic: 4.98 us -> 0 us
  matrix products: 4.09 us -> 0 us
  local copies, waits for them, and re-layouts: 3.55 us -> 1.94 us
    pallas_call x1, Pallas kernels: 19.6 us -> 27.1 us  [run_fwd(): pl.pallas_call(functools.partial(fwd_body, nk), grid=(ng,), in_specs=[pl....]
    pallas_call x1 -> x2, Pallas kernels: 14.1 us -> 18.5 us  [the longest x1 11.9 us: run_tail(): pl.pallas_call(functools.partial(tail_body, nh, hd), in_specs=[VM] * 4 +...]
    dot_general x1 -> x0, matrix products: 4.09 us -> none  [dot(): return jnp.einsum(spec, a, b, preferred_element_type=F32)]
    mul x1 -> x0, other arithmetic: 3.34 us -> none  [local_head(): grad_w_key = heads(q.reshape(nh, hd, 1) * z[:, None, :])]
    unnamed x20 -> x4, local copies, waits for them, and re-layouts: 3.24 us -> 1.94 us
  transfers between devices with their start and end apart: 2 -> 2, of which waited for: 1 -> 1; matrix products, arithmetic and copies ran while one was open for 1% -> 0% of each run, Pallas kernels for 36% -> 41%
where the time goes in v3:
time: 134 us
  Pallas kernels  125 us (93%)
  waiting for transfers between devices  3.16 us (2%)
  starting transfers between devices  2.57 us (2%)
  local copies, waits for them, and re-layouts  1.94 us (1%)
    pallas_call x1, Pallas kernels, run_head(): pl.pallas_call(functools.partial(head_body, nh, hd), in_specs=[VM] * 5 +...  42.5 us
    pallas_call x1, Pallas kernels, run_bwd(): pl.pallas_call(functools.partial(bwd_body, nk), grid=(ng,), in_specs=[pl....  27.4 us
    pallas_call x1, Pallas kernels, run_fwd(): pl.pallas_call(functools.partial(fwd_body, nk), grid=(ng,), in_specs=[pl....  27.1 us
    pallas_call x1, Pallas kernels, run_tail(): pl.pallas_call(functools.partial(tail_body, nh, hd), in_specs=[VM] * 4 +...  11.9 us
    pallas_call x1, Pallas kernels, run_query(): pl.pallas_call(functools.partial(query_body, nh, hd), in_specs=[VM] * 8,...  9.74 us
    pallas_call x1, Pallas kernels, run_outer(): pl.pallas_call(functools.partial(outer_body, hd), grid=(nh // per,), in_s...  6.54 us
    ppermute x1, waiting for transfers between devices, local_head(): rc = lax.ppermute(rb, 'sp', [(i, (i + 2) % 4) for i in range(4)])  3.16 us
  transfers between devices with their start and end apart: 2, of which 1 were waited for; matrix products, arithmetic and copies ran while one was open for 0% of the time, Pallas kernels for 41%

profile of v3, /device:TPU:0, one launch (start us, length us, event | category | flops | bytes accessed | tf_op | source)
XLA Modules:
  0.0 133.7 jit_solution(12202902755691792139)
XLA Ops:
  0.6 9.7 %query_fold.1 = (bf16[32,1280]{1,0:T(8,128)(2,1)}, f32[1,128]{1,0:T(1,128)}, bf16[640,32]{1,0:T(8,128)(2,1)}, f32[1,640]{1,0:T(1,128)}, f32[160,1280]{1,0:T(8,128)}) custom-call(f32[1280]{0:T(1024)} %probe_ref.3, bf16[640,1280]{1,0:T(8,128)(2,1)} %bitcast.22, f32[8,80]{1,0:T(8,128)} %bq_ref.1, bf16[640,1280]{1,0:T(8,128)(2,1)} %bitcast.24, ...), custom_call_target="tpu_custom_call" | custom-call | flops 50000000 | bytes 6000000 | tf_op jit(solution)/shard_map/query_fold/pallas_call | solution.py:312
  10.4 2.0 %collective-permute-start = (f32[160,1280]{1,0:T(8,128)}, f32[160,1280]{1,0:T(8,128)S(1)}, u32[]{:S(2)}, u32[]{:S(2)}) collective-permute-start(f32[160,1280]{1,0:T(8,128)} %get-tuple-element.53), channel_id=1, source_target_pairs={{0,4},{4,0},{1,5},{5,1},{2,6},{6,2},{3,7},{7,3}} | collective-permute-start | bytes 2457608 | tf_op jit(solution)/shard_map/ppermute | solution.py:640
  12.4 27.1 %fwd_tokens.1 = (bf16[64,96,1280]{2,1,0:T(8,128)(2,1)}, f32[8,96,128]{2,1,0:T(8,128)}, f32[8,96,128]{2,1,0:T(8,128)}, f32[8,64,1280]{2,1,0:T(8,128)}, f32[8,8,128]{2,1,0:T(8,128)}) custom-call(bf16[64,96,1280]{2,1,0:T(8,128)(2,1)} %x_ref.1, bf16[32,1280]{1,0:T(8,128)(2,1)} %get-tuple-element.46.gu_ref, f32[1,128]{1,0:T(1,128)} %get-tuple-element.47.bu_ref), custom_call_target="tpu_custom_call" | custom-call | flops 8000000000 | bytes 40000000 | tf_op jit(solution)/shard_map/fwd_tokens/pallas_call | solution.py:85
  39.6 0.0 collective-permute-done.wvh_ref
  39.6 0.0 copy-start.1
  39.6 0.9 copy-done.1
  40.5 42.5 %pool_head.1 = (bf16[1280,64]{1,0:T(8,128)(2,1)}, bf16[2560,64]{1,0:T(8,128)(2,1)}, bf16[64,2560]{1,0:T(8,128)(2,1)}, bf16[640,64]{1,0:T(8,128)(2,1)}, bf16[64,1...) custom-call(f32[8,64,1280]{2,1,0:T(8,128)} %get-tuple-element.51.r_r, ...), custom_call_target="tpu_custom_call" | custom-call | flops 3000000000 | bytes 30000000 | tf_op jit(solution)/shard_map/pool_head/pallas_call | solution.py:494
  83.0 0.5 collective-permute-start.1
  83.6 27.4 %bwd_tokens.1 = (bf16[64,96,1280]{2,1,0:T(8,128)(2,1)}, f32[8,1280]{1,0:T(8,128)}, f32[8,8,128]{2,1,0:T(8,128)}, f32[1280,2560]{1,0:T(8,128)}, f32[2560,1280]{1,0:T(8,128)}, /*index=5*/f32[640,1280]{1,0:T(8,128)}) custom-call(bf16[64,96,1280]{2,1,0:T(8,128)(2,1)} %get-tuple-element.48.xh_ref, f32[8,96,128]{2,1,0:T(8,128)} %get-tuple-element.49.sx_ref, ...), custom_call_target="tpu_custom_call" | custom-call | flops 12000000000 | bytes 40000000 | tf_op jit(solution)/shard_map/bwd_tokens/pallas_call | solution.py:159
  110.9 3.2 %collective-permute-done.1.rc_ref = f32[4,64,1280]{2,1,0:T(8,128)S(1)} collective-permute-done((f32[4,64,1280]{2,1,0:T(8,128)}, f32[4,64,1280]{2,1,0:T(8,128)S(1)}, u32[]{:S(2)}, u32[]{:S(2)}) %collective-permute-start.1) | collective-permute-done | bytes 1310752 | tf_op jit(solution)/shard_map/ppermute | solution.py:643
  114.1 0.0 copy-start
  114.1 1.1 copy-done
  115.2 11.9 %query_back.1 = (bf16[32,1280]{1,0:T(8,128)(2,1)}, bf16[640,8]{1,0:T(8,128)(2,1)}, bf16[8,1280]{1,0:T(8,128)(2,1)}, f32[1280]{0:T(1024)}, f32[8,64,1280]{2,1,0:T(8,128)}) custom-call(f32[8,1280]{1,0:T(8,128)} %get-tuple-element.62.z_ref, f32[8,8,128]{2,1,0:T(8,128)} %get-tuple-element.63.dl_ref, f32[4,64,1280]{2,1,0:T(8,128)} %get-tuple-element.64.rb_ref, ...), custom_call_target="tpu_custom_call" | custom-call | flops 50000000 | bytes 6000000 | tf_op jit(solution)/shard_map/query_back/pallas_call | solution.py:580
  127.1 6.5 %outer_grads.1 = (f32[640,1280]{1,0:T(8,128)}, f32[640,1280]{1,0:T(8,128)}, f32[640,1280]{1,0:T(8,128)}, bf16[64,1280]{1,0:T(8,128)(2,1)}, f32[1280]{0:T(1024)}) custom-call(bf16[640,32]{1,0:T(8,128)(2,1)} %get-tuple-element.45.qt_ref, bf16[32,1280]{1,0:T(8,128)(2,1)} %get-tuple-element.65.z_ref, bf16[640,8]{1,0:T(8,128)(2,1)} %get-tuple-element.66.dqt_ref, ...), custom_call_target="tpu_custom_call" | custom-call | flops 300000000 | bytes 14000000 | tf_op jit(solution)/shard_map/outer_grads/pallas_call | solution.py:616
Async XLA Ops:
  10.4 29.2 %collective-permute-start = (f32[160,1280]{1,0:T(8,128)}, f32[160,1280]{1,0:T(8,128)S(1)}, u32[]{:S(2)}, u32[]{:S(2)}) collective-permute-start(f32[160,1280]{1,0:T(8,128)} %get-tuple-element.53), channel_id=1, source_target_pairs={{0,4},{4,0},{1,5},{5,1},{2,6},{6,2},{3,7},{7,3}} | collective-permute-start | bytes 2457608 | tf_op jit(solution)/shard_map/ppermute | solution.py:640
  39.6 0.9 copy-start.1
  83.0 31.1 %collective-permute-start.1 = (f32[4,64,1280]{2,1,0:T(8,128)}, f32[4,64,1280]{2,1,0:T(8,128)S(1)}, u32[]{:S(2)}, u32[]{:S(2)}) collective-permute-start(f32[4,64,1280]{2,1,0:T(8,128)} %get-tuple-element.64.rb_ref), channel_id=1, source_target_pairs={{0,2},{1,3},{2,0},{3,1},{4,6},{5,7},{6,4},{7,5}} | collective-permute-start | bytes 3932168 | tf_op jit(solution)/shard_map/ppermute | solution.py:643
  114.1 1.1 copy-start

commit v4 on v3

--- a/solution.py
+++ b/solution.py
@@ -30,36 +30,15 @@
     return cen, lax.rsqrt(jnp.mean(cen * cen, axis=-1, keepdims=True) + NORM_EPS)
 
 
-def fwd_body(nk, x_ref, gu_ref, bu_ref, xh_ref, sx_ref, rs_ref, r_ref, ml_ref, st_ref):
+def fwd_body(nk, x_ref, gu_ref, bu_ref, xh_ref, sx_ref, rs_ref, r_ref, ml_ref):
     images, tokens, width = x_ref.shape
     nh = nk // 2
-    eye = lax.broadcasted_iota(jnp.int32, (tokens, tokens), 0) == lax.broadcasted_iota(jnp.int32, (tokens, tokens), 1)
-    ones = jnp.ones((16, width), BF16)
-    worst = jnp.full((tokens, 1), -1.0, F32)
+    strip = 16
     for i in range(images):
-        xb = x_ref[i]
-        mean = mm(xb, ones, NT)[:, :1] * (1.0 / width)
-        square = jnp.sum(jnp.where(eye, mm(xb, xb, NT), 0.0), axis=1, keepdims=True) * (1.0 / width)
-        var = square - mean * mean
-        worst = jnp.maximum(worst, mean * mean - 256.0 * var)
-        st_ref[0, i] = jnp.broadcast_to(mean, (tokens, 128))
-        st_ref[1, i] = jnp.broadcast_to(lax.rsqrt(jnp.maximum(var, 0.0) + NORM_EPS), (tokens, 128))
-
-    @pl.when(jnp.max(worst) > 0.0)
-    def _():
-        for i in range(images):
-            def redo(j, carry, i=i):
-                rows = pl.ds(pl.multiple_of(j * 16, 16), 16)
-                xs = x_ref[i, rows, :].astype(F32)
-                st_ref[0, i, rows, :] = jnp.broadcast_to(jnp.mean(xs, axis=-1, keepdims=True), (16, 128))
-                st_ref[1, i, rows, :] = jnp.broadcast_to(row_stats(xs)[1], (16, 128))
-                return carry
-            lax.fori_loop(0, tokens // 16, redo, 0)
-
-    for i in range(images):
-        rstd = st_ref[1, i, :, :1]
-        xh_ref[i] = ((x_ref[i].astype(F32) - st_ref[0, i, :, :1]) * rstd).astype(BF16)
-        rs_ref[0, :, i * nk:(i + 1) * nk] = st_ref[1, i, :, :nk]
+        for j in range(0, tokens, strip):
+            cen, rstd = row_stats(x_ref[i, j:j + strip, :].astype(F32))
+            xh_ref[i, j:j + strip, :] = (cen * rstd).astype(BF16)
+            rs_ref[0, j:j + strip, i * nk:(i + 1) * nk] = jnp.broadcast_to(rstd, (strip, nk))
     parts = []
     for i in range(images):
         s2 = mm(xh_ref[i], gu_ref[...], NT)
@@ -104,7 +83,6 @@
             jax.ShapeDtypeStruct((nk // 2, nb, width), F32),
             jax.ShapeDtypeStruct((ng, 8, 128), F32),
         ],
-        scratch_shapes=[pltpu.VMEM((2, bi, tokens, 128), F32)],
         cost_estimate=pl.CostEstimate(flops=8_000_000_000, bytes_accessed=40_000_000, transcendentals=0),
         name='fwd_tokens',
     )(x, gu2, bu)
@@ -276,8 +254,12 @@
     return jnp.concatenate([ref[h:h + 1, :] for h in range(ref.shape[0])], axis=1)
 
 
-def query_body(nh, hd, probe_ref, wq_ref, bq_ref, wk_ref, wv_ref, bv_ref, gain_ref, bias_ref, gu_ref, bu_ref, q_ref, cb_ref, wvq_ref, us_ref, ur_ref, sems):
+def query_body(nh, hd, probe_ref, wq_ref, bq_ref, wk_hbm, wv_hbm, bv_ref, gain_ref, bias_ref, gu_ref, bu_ref, q_ref, cb_ref, wvq_ref, us_ref, ur_ref, wk_ref, wv_ref, lsem, sems):
     tp_peer, _, _, _ = places()
+    load_k = pltpu.make_async_copy(wk_hbm, wk_ref, lsem.at[0])
+    load_v = pltpu.make_async_copy(wv_hbm, wv_ref, lsem.at[1])
+    load_k.start()
+    load_v.start()
     greet([tp_peer])
     width = probe_ref.shape[0]
     nk = 2 * nh
@@ -285,9 +267,11 @@
     qd = jnp.where(head_mask(nh, nh, hd), jnp.broadcast_to(q.astype(F32), (nh, nh * hd)), 0.0).astype(BF16)
     qf = qd.astype(F32)
     q_ref[...] = jnp.transpose(jnp.concatenate([qf, qf, qf, jnp.zeros_like(qf)], axis=0)).astype(BF16)
+    load_k.wait()
     u = mm(qd, wk_ref[...])
     us_ref[...] = u
     copy = send(us_ref, ur_ref, sems, 0, tp_peer)
+    load_v.wait()
     bias = row_of(bias_ref)
     bh, bl = two(bias)
     row = lax.broadcasted_iota(jnp.int32, (8, width), 0)
@@ -311,7 +295,7 @@
     width = probe.shape[0]
     return pl.pallas_call(
         functools.partial(query_body, nh, hd),
-        in_specs=[VM] * 8,
+        in_specs=[VM] * 3 + [ANY] * 2 + [VM] * 3,
         out_specs=[VM] * 5,
         out_shape=[
             jax.ShapeDtypeStruct((4 * nh, width), BF16),
@@ -320,7 +304,7 @@
             jax.ShapeDtypeStruct((1, nh * hd), F32),
             jax.ShapeDtypeStruct((nh * hd // 4, width), F32),
         ],
-        scratch_shapes=[pltpu.VMEM((nh, width), F32), pltpu.VMEM((nh, width), F32), pltpu.SemaphoreType.DMA((2, 1))],
+        scratch_shapes=[pltpu.VMEM((nh, width), F32), pltpu.VMEM((nh, width), F32), pltpu.VMEM(wk.shape, BF16), pltpu.VMEM(wv.shape, BF16), pltpu.SemaphoreType.DMA((2,)), pltpu.SemaphoreType.DMA((2, 1))],
         compiler_params=pltpu.CompilerParams(collective_id=0, has_side_effects=True),
         cost_estimate=pl.CostEstimate(flops=50_000_000, bytes_accessed=6_000_000, transcendentals=0),
         name='query_fold',
@@ -339,9 +323,9 @@
     return send(buf.at[rows], buf.at[rows], sems, k, sib)
 
 
-def head_body(nh, hd, r_ref, ml_ref, wv_ref, wvh_ref, wo_ref, wup_hbm, wdn_hbm, gain_ref, bu_ref, cb_ref, bo_ref, hg_ref, hb_ref, bup_ref, bdn_ref, og_ref,
-              yt_out, gt_t_out, dpre_out, ot_out, da_out, pooled_out, dot_out, gt_out, aux_out, rb_out,
-              wup, wdn, wall, osd, mls, ora, mra, osd2, mls2, orb, mrb, aps, apr, rs, ra, dys, dyr, mps, mpr, dos, dor, kps, kpr, dg_s, lsem, sems):
+def head_body(nh, hd, r_ref, ml_ref, wv_ref, wvh_ref, wo_hbm, wup_hbm, wdn_hbm, gain_ref, bu_ref, cb_ref, bo_ref, hg_ref, hb_ref, bup_ref, bdn_ref, og_ref,
+              yt_out, gt_t_out, dpre_out, ot_out, da_out, pooled_out, dot_out, gt_out, aux_out, rf1_out, rb2_out,
+              wo_ref, rb1, rc1, wup, wdn, wall, osd, mls, ora, mra, osd2, mls2, orb, mrb, aps, apr, rs, ra, dys, dyr, mps, mpr, dos, dor, kps, kpr, dg_s, lsem, sems):
     tp_peer, sib, xp, core = places()
     sp = lax.axis_index('sp')
     nk = 2 * nh
@@ -349,7 +333,9 @@
     width = og_ref.shape[1]
     load_up = pltpu.make_async_copy(wup_hbm, wup, lsem.at[0])
     load_dn = pltpu.make_async_copy(wdn_hbm, wdn, lsem.at[1])
+    load_o = pltpu.make_async_copy(wo_hbm, wo_ref, lsem.at[2])
     load_dn.start()
+    load_o.start()
     load_up.start()
     gain = row_of(gain_ref)
     groups = ml_ref.shape[0]
@@ -393,6 +379,7 @@
     inv_l = 1.0 / l
     o = o * spread(unpack(inv_l, nk)) + cb_ref[...]
     o_bf = o.astype(BF16)
+    load_o.wait()
     ap = mm(o_bf, wo_ref[...])
     aps[...] = ap
     c5 = swap_halves(aps, apr, sems, 5, tp_peer, core)
@@ -406,7 +393,10 @@
     c5.wait()
     c6 = pass_on(apr, sems, 7, sib, core)
     r1.wait()
-    rb_out[...] = rs[mine] + ra[...]
+    rb = rs[mine] + ra[...]
+    rb1[...] = rb[:1]
+    rb2_out[...] = rb[1:]
+    r2 = send(rb1, rc1, sems, 17, xp)
     c6.wait()
     a = ap + apr[...] + row_of(bo_ref)
     acen, arstd = row_stats(a)
@@ -480,6 +470,8 @@
         back(1, h, dob[:, h * hd:(h + 1) * hd], wall[h // 2, lo:lo + hd, :].astype(BF16))
     c13.wait()
     pooled_out[...] = (a + mp + mpr[...] + row_of(bdn_ref)).astype(BF16)
+    r2.wait()
+    rf1_out[...] = rb1[...] + rc1[...]
 
 
 def run_head(nh, hd, r_raw, ml, wv, wvh, wo, w_up, w_down, gain, bu, cb, b_out, hgain, hbias, b_up, b_down, out_grad):
@@ -493,8 +485,8 @@
     rhalf = pltpu.VMEM((nh // 2, nb, width), F32)
     return pl.pallas_call(
         functools.partial(head_body, nh, hd),
-        in_specs=[VM] * 5 + [ANY] * 2 + [VM] * 9,
-        out_specs=[VM] * 10,
+        in_specs=[VM] * 4 + [ANY] * 3 + [VM] * 9,
+        out_specs=[VM] * 11,
         out_shape=[
             jax.ShapeDtypeStruct((width, nb), BF16),
             jax.ShapeDtypeStruct((ff, nb), BF16),
@@ -505,15 +497,16 @@
             jax.ShapeDtypeStruct((nd, nb), BF16),
             jax.ShapeDtypeStruct((2 * nh, nb, width), F32),
             jax.ShapeDtypeStruct((groups, 8, 128), F32),
-            jax.ShapeDtypeStruct((nh // 2, nb, width), F32),
+            jax.ShapeDtypeStruct((1, nb, width), F32),
+            jax.ShapeDtypeStruct((nh // 2 - 1, nb, width), F32),
         ],
         scratch_shapes=[
-            pltpu.VMEM(w_up.shape, BF16), pltpu.VMEM(w_down.shape, BF16), pltpu.VMEM((4,) + wvh.shape, F32),
+            pltpu.VMEM(wo.shape, BF16), pltpu.VMEM((1, nb, width), F32), pltpu.VMEM((1, nb, width), F32), pltpu.VMEM(w_up.shape, BF16), pltpu.VMEM(w_down.shape, BF16), pltpu.VMEM((4,) + wvh.shape, F32),
             heads, stat, heads, stat, heads, stat, heads, stat,
             full, full, pltpu.VMEM((nh, nb, width), F32), rhalf,
             full, full, full, full, heads, heads, pltpu.VMEM((nb, 128), F32), pltpu.VMEM((nb, 128), F32),
             pltpu.VMEM((nb, ff), F32),
-            pltpu.SemaphoreType.DMA((2,)), pltpu.SemaphoreType.DMA((2, 17)),
+            pltpu.SemaphoreType.DMA((3,)), pltpu.SemaphoreType.DMA((2, 18)),
         ],
         compiler_params=pltpu.CompilerParams(collective_id=1, has_side_effects=True, vmem_limit_bytes=60 * 1024 * 1024),
         cost_estimate=pl.CostEstimate(flops=3_000_000_000, bytes_accessed=30_000_000, transcendentals=0),
@@ -521,7 +514,7 @@
     )(r_raw, ml, wv, wvh, wo, w_up, w_down, gain, bu, cb, b_out, hgain, hbias, b_up, b_down, out_grad)
 
 
-def tail_body(nh, hd, z_ref, dl_ref, rb_ref, rc_ref, wk_hbm, wq_hbm, gain_ref, probe_ref, z_out, dq_out, pm_out, gp_out, rf_out, zs, za, zs2, zb, ds, da, ds2, db, ps, pr, rd, re, wk, wq, lsem, sems):
+def tail_body(nh, hd, z_ref, dl_ref, rf1_ref, rb_ref, rc_ref, wk_hbm, wq_hbm, gain_ref, probe_ref, z_out, dq_out, pm_out, gp_out, rf_out, zs, za, zs2, zb, ds, da, ds2, db, ps, pr, rd, re, wk, wq, lsem, sems):
     tp_peer, sib, xp, core = places()
     nk = 2 * nh
     groups = dl_ref.shape[0]
@@ -538,7 +531,8 @@
     greet([tp_peer, sib, xp])
     c1 = send(zs, za, sems, 0, sib)
     d1 = send(ds, da, sems, 1, sib)
-    rd[...] = rb_ref[...] + rc_ref[...]
+    rd[:1] = rf1_ref[...]
+    rd[1:] = rb_ref[...] + rc_ref[...]
     r1 = send(rd, re, sems, 2, sib)
     c1.wait()
     d1.wait()
@@ -571,15 +565,16 @@
     gp_out[...] = (gp + pr[...]).reshape(width)
 
 
-def run_tail(nh, hd, z, dl, rb, rc, wk, wq, gain, probe):
+def run_tail(nh, hd, z, dl, rf1, rb, rc, wk, wq, gain, probe):
     width = z.shape[1]
     nd = nh * hd
     zz = pltpu.VMEM((nh, width), F32)
     dd = pltpu.VMEM((dl.shape[0], 128), F32)
     pp = pltpu.VMEM((1, width), F32)
+    rr = pltpu.VMEM((nh // 2,) + rb.shape[1:], F32)
     return pl.pallas_call(
         functools.partial(tail_body, nh, hd),
-        in_specs=[VM] * 4 + [ANY] * 2 + [VM] * 2,
+        in_specs=[VM] * 5 + [ANY] * 2 + [VM] * 2,
         out_specs=[VM] * 5,
         out_shape=[
             jax.ShapeDtypeStruct((4 * nh, width), BF16),
@@ -588,11 +583,11 @@
             jax.ShapeDtypeStruct((width,), F32),
             jax.ShapeDtypeStruct((nh,) + rb.shape[1:], F32),
         ],
-        scratch_shapes=[zz, zz, zz, zz, dd, dd, dd, dd, pp, pp, pltpu.VMEM(rb.shape, F32), pltpu.VMEM(rb.shape, F32), pltpu.VMEM(wk.shape, BF16), pltpu.VMEM(wq.shape, BF16), pltpu.SemaphoreType.DMA((2,)), pltpu.SemaphoreType.DMA((2, 6))],
+        scratch_shapes=[zz, zz, zz, zz, dd, dd, dd, dd, pp, pp, rr, rr, pltpu.VMEM(wk.shape, BF16), pltpu.VMEM(wq.shape, BF16), pltpu.SemaphoreType.DMA((2,)), pltpu.SemaphoreType.DMA((2, 6))],
         compiler_params=pltpu.CompilerParams(collective_id=2, has_side_effects=True),
         cost_estimate=pl.CostEstimate(flops=50_000_000, bytes_accessed=6_000_000, transcendentals=0),
         name='query_back',
-    )(z, dl, rb, rc, wk, wq, gain, probe)
+    )(z, dl, rf1, rb, rc, wk, wq, gain, probe)
 
 
 def outer_body(hd, qt_ref, z_ref, dqt_ref, pm_ref, dot_ref, rf_ref, gain_ref, bias_ref, pooled_ref, gp_ref, gwk_ref, gwq_ref, gwv_ref, pooled_out, gp_out):
@@ -608,7 +603,7 @@
 
 def run_outer(nh, hd, qt, z, dqt, pm, dot, rf, gain, bias, pooled, gp):
     nb, width = pooled.shape
-    per = 2
+    per = 1
     rows = per * hd
     blk = lambda a: pl.BlockSpec((rows, a.shape[1]), lambda i: (i, 0))
     whole = lambda a: pl.BlockSpec(a.shape, lambda i: (0,) * a.ndim)
@@ -639,10 +634,10 @@
     gu2, bu, qt, cb, wvq = run_query(nh, hd, probe, wq, b_query, wk, wv, b_value, enc_gain, enc_bias)
     wvq = lax.ppermute(wvq, 'tp', [(0, 1), (1, 0)])
     xh, sx, rs, r_raw, ml = run_fwd(encoded, gu2, bu)
-    yt, ht, dpre, ot, da, pooled, do_t, gt, aux, rb = run_head(nh, hd, r_raw, ml, wv, wvq, wo, w_up, w_down, enc_gain, bu, cb, b_out, head_gain, head_bias, b_up, b_down, out_grad)
+    yt, ht, dpre, ot, da, pooled, do_t, gt, aux, rf1, rb = run_head(nh, hd, r_raw, ml, wv, wvq, wo, w_up, w_down, enc_gain, bu, cb, b_out, head_gain, head_bias, b_up, b_down, out_grad)
     rc = lax.ppermute(rb, 'sp', [(i, (i + 2) % 4) for i in range(4)])
     grad_encoded, z, dl, grad_w_up, grad_w_down, grad_w_out = run_bwd(xh, sx, rs, gt, gu2, aux, yt, dpre, ht, out_grad, ot, da)
-    z, dqt, pm, grad_probe, rf = run_tail(nh, hd, z, dl, rb, rc, wk, wq, enc_gain, probe)
+    z, dqt, pm, grad_probe, rf = run_tail(nh, hd, z, dl, rf1, rb, rc, wk, wq, enc_gain, probe)
     gwk, gwq, gwv, pooled, grad_probe = run_outer(nh, hd, qt, z, dqt, pm, do_t, rf, enc_gain, enc_bias, pooled, grad_probe)
     grad_w_query, grad_w_key, grad_w_value = heads(gwq), heads(gwk), heads(gwv)
     return (pooled, grad_encoded, grad_probe, grad_w_query, grad_w_key, grad_w_value, grad_w_out.reshape(nh, hd, width), grad_w_up, grad_w_down)

time: 134 us -> 124 us (0.925)
  Pallas kernels: 125 us -> 119 us
  waiting for transfers between devices: 3.16 us -> 0.01 us
    pallas_call x1, Pallas kernels: 27.1 us -> 19.7 us  [run_fwd(): pl.pallas_call(functools.partial(fwd_body, nk), grid=(ng,), in_specs=[pl....]
    ppermute x1, waiting for transfers between devices: 3.16 us -> 0.01 us  [local_head(): rc = lax.ppermute(rb, 'sp', [(i, (i + 2) % 4) for i in range(4)])]
    pallas_call x1, Pallas kernels: 6.54 us -> 8.2 us  [run_outer(): pl.pallas_call(functools.partial(outer_body, hd), grid=(nh // per,), in_s...]
  transfers between devices with their start and end apart: 2 -> 2, of which waited for: 1 -> 0; matrix products, arithmetic and copies ran while one was open for 0% -> 0% of each run, Pallas kernels for 41% -> 38%
where the time goes in v4:
time: 124 us
  Pallas kernels  119 us (96%)
  starting transfers between devices  2.06 us (2%)
  local copies, waits for them, and re-layouts  1.82 us (1%)
    pallas_call x1, Pallas kernels, run_head(): pl.pallas_call(functools.partial(head_body, nh, hd), in_specs=[VM] * 4 +...  42.1 us
    pallas_call x1, Pallas kernels, run_bwd(): pl.pallas_call(functools.partial(bwd_body, nk), grid=(ng,), in_specs=[pl....  27.2 us
    pallas_call x1, Pallas kernels, run_fwd(): pl.pallas_call(functools.partial(fwd_body, nk), grid=(ng,), in_specs=[pl....  19.7 us
    pallas_call x1, Pallas kernels, run_tail(): pl.pallas_call(functools.partial(tail_body, nh, hd), in_specs=[VM] * 5 +...  12.6 us
    pallas_call x1, Pallas kernels, run_query(): pl.pallas_call(functools.partial(query_body, nh, hd), in_specs=[VM] * 3 +...  9.63 us
    pallas_call x1, Pallas kernels, run_outer(): pl.pallas_call(functools.partial(outer_body, hd), grid=(nh // per,), in_s...  8.2 us
  transfers between devices with their start and end apart: 2, of which 0 were waited for; matrix products, arithmetic and copies ran while one was open for 0% of the time, Pallas kernels for 38%

profile of v4, /device:TPU:0, one launch (start us, length us, event | category | flops | bytes accessed | tf_op | source)
XLA Modules:
  0.0 124.0 jit_solution(7975222603642197207)
XLA Ops:
  0.6 9.6 %query_fold.1 = (bf16[32,1280]{1,0:T(8,128)(2,1)}, f32[1,128]{1,0:T(1,128)}, bf16[640,32]{1,0:T(8,128)(2,1)}, f32[1,640]{1,0:T(1,128)}, f32[160,1280]{1,0:T(8,128)}) custom-call(f32[1280]{0:T(1024)} %probe_ref.3, bf16[640,1280]{1,0:T(8,128)(2,1)} %bitcast.22, f32[8,80]{1,0:T(8,128)} %bq_ref.1, bf16[640,1280]{1,0:T(8,128)(2,1)} %bitcast.24, ...), custom_call_target="tpu_custom_call" | custom-call | flops 50000000 | bytes 6000000 | tf_op jit(solution)/shard_map/query_fold/pallas_call | solution.py:296
  10.3 1.3 %collective-permute-start = (f32[160,1280]{1,0:T(8,128)}, f32[160,1280]{1,0:T(8,128)S(1)}, u32[]{:S(2)}, u32[]{:S(2)}) collective-permute-start(f32[160,1280]{1,0:T(8,128)} %get-tuple-element.54), channel_id=1, source_target_pairs={{0,4},{4,0},{1,5},{5,1},{2,6},{6,2},{3,7},{7,3}} | collective-permute-start | bytes 2457608 | tf_op jit(solution)/shard_map/ppermute | solution.py:635
  11.6 19.7 %fwd_tokens.1 = (bf16[64,96,1280]{2,1,0:T(8,128)(2,1)}, f32[8,96,128]{2,1,0:T(8,128)}, f32[8,96,128]{2,1,0:T(8,128)}, f32[8,64,1280]{2,1,0:T(8,128)}, f32[8,8,128]{2,1,0:T(8,128)}) custom-call(bf16[64,96,1280]{2,1,0:T(8,128)(2,1)} %x_ref.1, bf16[32,1280]{1,0:T(8,128)(2,1)} %get-tuple-element.47.gu_ref, f32[1,128]{1,0:T(1,128)} %get-tuple-element.48.bu_ref), custom_call_target="tpu_custom_call" | custom-call | flops 8000000000 | bytes 40000000 | tf_op jit(solution)/shard_map/fwd_tokens/pallas_call | solution.py:64
  31.3 0.0 collective-permute-done.wvh_ref
  31.3 0.0 copy-start.1
  31.3 0.9 copy-done.1
  32.2 42.1 %pool_head.1 = (bf16[1280,64]{1,0:T(8,128)(2,1)}, bf16[2560,64]{1,0:T(8,128)(2,1)}, bf16[64,2560]{1,0:T(8,128)(2,1)}, bf16[640,64]{1,0:T(8,128)(2,1)}, bf16[64,1...) custom-call(f32[8,64,1280]{2,1,0:T(8,128)} %get-tuple-element.52.r_r, ...), custom_call_target="tpu_custom_call" | custom-call | flops 3000000000 | bytes 30000000 | tf_op jit(solution)/shard_map/pool_head/pallas_call | solution.py:486
  74.3 0.7 collective-permute-start.1
  75.0 27.2 %bwd_tokens.1 = (bf16[64,96,1280]{2,1,0:T(8,128)(2,1)}, f32[8,1280]{1,0:T(8,128)}, f32[8,8,128]{2,1,0:T(8,128)}, f32[1280,2560]{1,0:T(8,128)}, f32[2560,1280]{1,0:T(8,128)}, /*index=5*/f32[640,1280]{1,0:T(8,128)}) custom-call(bf16[64,96,1280]{2,1,0:T(8,128)(2,1)} %get-tuple-element.49.xh_ref, f32[8,96,128]{2,1,0:T(8,128)} %get-tuple-element.50.sx_ref, ...), custom_call_target="tpu_custom_call" | custom-call | flops 12000000000 | bytes 40000000 | tf_op jit(solution)/shard_map/bwd_tokens/pallas_call | solution.py:137
  102.2 0.0 collective-permute-done.1.rc_ref
  102.2 0.0 copy-start
  102.2 0.9 copy-done
  103.1 12.6 %query_back.1 = (bf16[32,1280]{1,0:T(8,128)(2,1)}, bf16[640,8]{1,0:T(8,128)(2,1)}, bf16[8,1280]{1,0:T(8,128)(2,1)}, f32[1280]{0:T(1024)}, f32[8,64,1280]{2,1,0:T(8,128)}) custom-call(f32[8,1280]{1,0:T(8,128)} %get-tuple-element.63.z_ref, f32[8,8,128]{2,1,0:T(8,128)} %get-tuple-element.64.dl_ref, f32[1,64,1280]{2,1,0:T(8,128)} %get-tuple-element.65.rf1_ref, ...), custom_call_target="tpu_custom_call" | custom-call | flops 50000000 | bytes 6000000 | tf_op jit(solution)/shard_map/query_back/pallas_call | solution.py:575
  115.8 8.2 %outer_grads.1 = (f32[640,1280]{1,0:T(8,128)}, f32[640,1280]{1,0:T(8,128)}, f32[640,1280]{1,0:T(8,128)}, bf16[64,1280]{1,0:T(8,128)(2,1)}, f32[1280]{0:T(1024)}) custom-call(bf16[640,32]{1,0:T(8,128)(2,1)} %get-tuple-element.46.qt_ref, bf16[32,1280]{1,0:T(8,128)(2,1)} %get-tuple-element.67.z_ref, bf16[640,8]{1,0:T(8,128)(2,1)} %get-tuple-element.68.dqt_ref, ...), custom_call_target="tpu_custom_call" | custom-call | flops 300000000 | bytes 14000000 | tf_op jit(solution)/shard_map/outer_grads/pallas_call | solution.py:611
Async XLA Ops:
  10.3 21.0 %collective-permute-start = (f32[160,1280]{1,0:T(8,128)}, f32[160,1280]{1,0:T(8,128)S(1)}, u32[]{:S(2)}, u32[]{:S(2)}) collective-permute-start(f32[160,1280]{1,0:T(8,128)} %get-tuple-element.54), channel_id=1, source_target_pairs={{0,4},{4,0},{1,5},{5,1},{2,6},{6,2},{3,7},{7,3}} | collective-permute-start | bytes 2457608 | tf_op jit(solution)/shard_map/ppermute | solution.py:635
  31.3 0.9 copy-start.1
  74.3 27.9 %collective-permute-start.1 = (f32[3,64,1280]{2,1,0:T(8,128)}, f32[3,64,1280]{2,1,0:T(8,128)S(1)}, u32[]{:S(2)}, u32[]{:S(2)}) collective-permute-start(f32[3,64,1280]{2,1,0:T(8,128)} %get-tuple-element.66.rb_ref), channel_id=1, source_target_pairs={{0,2},{1,3},{2,0},{3,1},{4,6},{5,7},{6,4},{7,5}} | collective-permute-start | bytes 2949128 | tf_op jit(solution)/shard_map/ppermute | solution.py:638
  102.2 0.9 copy-start

commit v5 on v4

--- a/solution.py
+++ b/solution.py
@@ -102,7 +102,7 @@
     gwo_ref[...] = mm(ot_ref[...], da_ref[...])
     sx = sx_ref[0]
     rstd = rs_ref[0]
-    gts = [gt_ref[:, i, :].astype(BF16) for i in range(images)]
+    gts = [gt_ref[:, i, :] for i in range(images)]
     dpx = jnp.concatenate([mm(xh_ref[i], gts[i], NT) for i in range(images)], axis=1)
     p = jnp.exp(sx - aux_ref[0, 0:1]) * aux_ref[0, 1:2]
     ds = p * (dpx + aux_ref[0, 2:3])
@@ -324,8 +324,8 @@
 
 
 def head_body(nh, hd, r_ref, ml_ref, wv_ref, wvh_ref, wo_hbm, wup_hbm, wdn_hbm, gain_ref, bu_ref, cb_ref, bo_ref, hg_ref, hb_ref, bup_ref, bdn_ref, og_ref,
-              yt_out, gt_t_out, dpre_out, ot_out, da_out, pooled_out, dot_out, gt_out, aux_out, rf1_out, rb2_out,
-              wo_ref, rb1, rc1, wup, wdn, wall, osd, mls, ora, mra, osd2, mls2, orb, mrb, aps, apr, rs, ra, dys, dyr, mps, mpr, dos, dor, kps, kpr, dg_s, lsem, sems):
+              yt_out, gt_t_out, dpre_out, ot_out, da_out, ab_out, mp_out, dot_out, gt_out, aux_out, rf1_out, rb2_out,
+              wo_ref, rb1, rc1, wup, wdn, wall, osd, mls, ora, mra, osd2, mls2, orb, mrb, aps, apr, rs, ra, dys, dyr, dos, dor, kps, kpr, dg_s, lsem, sems):
     tp_peer, sib, xp, core = places()
     sp = lax.axis_index('sp')
     nk = 2 * nh
@@ -417,9 +417,8 @@
     dyp = mm(dpre, wup[...], NT)
     dys[...] = dyp
     c7 = swap_halves(dys, dyr, sems, 9, tp_peer, core)
-    mp = mm(g, wdn[...])
-    mps[...] = mp
-    c8 = swap_halves(mps, mpr, sems, 10, tp_peer, core)
+    mp_out[...] = mm(g, wdn[...])
+    ab_out[...] = a + row_of(bdn_ref)
     yt_out[...] = jnp.transpose(y)
     gt_t_out[...] = jnp.transpose(g)
     ot_out[...] = jnp.transpose(o_bf)
@@ -441,7 +440,7 @@
     def back(k, h, d, w):
         t = mm(d, w) * gain
         t = t - jnp.mean(t, axis=1, keepdims=True)
-        gt_out[k * nh + h] = t
+        gt_out[k * nh + h] = t.astype(BF16)
 
     dot_out[...] = jnp.transpose(do_bf)
     for h in range(nh):
@@ -452,8 +451,6 @@
     w2.wait()
     from_x = lax.rem(sp + 2, 4)
     w3 = send(wall.at[from_x], wall.at[from_x], sems, 16, sib)
-    c8.wait()
-    c13 = pass_on(mpr, sems, 15, sib, core)
     c11.wait()
     kall = kap + pltpu.roll(kpr[...], nh, 1)
     kpk = pack(kall, nk)
@@ -468,8 +465,6 @@
     for h in range(nh):
         lo = (h % 2) * hd
         back(1, h, dob[:, h * hd:(h + 1) * hd], wall[h // 2, lo:lo + hd, :].astype(BF16))
-    c13.wait()
-    pooled_out[...] = (a + mp + mpr[...] + row_of(bdn_ref)).astype(BF16)
     r2.wait()
     rf1_out[...] = rb1[...] + rc1[...]
 
@@ -486,16 +481,17 @@
     return pl.pallas_call(
         functools.partial(head_body, nh, hd),
         in_specs=[VM] * 4 + [ANY] * 3 + [VM] * 9,
-        out_specs=[VM] * 11,
+        out_specs=[VM] * 12,
         out_shape=[
             jax.ShapeDtypeStruct((width, nb), BF16),
             jax.ShapeDtypeStruct((ff, nb), BF16),
             jax.ShapeDtypeStruct((nb, ff), BF16),
             jax.ShapeDtypeStruct((nd, nb), BF16),
             jax.ShapeDtypeStruct((nb, width), BF16),
-            jax.ShapeDtypeStruct((nb, width), BF16),
+            jax.ShapeDtypeStruct((nb, width), F32),
+            jax.ShapeDtypeStruct((nb, width), F32),
             jax.ShapeDtypeStruct((nd, nb), BF16),
-            jax.ShapeDtypeStruct((2 * nh, nb, width), F32),
+            jax.ShapeDtypeStruct((2 * nh, nb, width), BF16),
             jax.ShapeDtypeStruct((groups, 8, 128), F32),
             jax.ShapeDtypeStruct((1, nb, width), F32),
             jax.ShapeDtypeStruct((nh // 2 - 1, nb, width), F32),
@@ -504,7 +500,7 @@
             pltpu.VMEM(wo.shape, BF16), pltpu.VMEM((1, nb, width), F32), pltpu.VMEM((1, nb, width), F32), pltpu.VMEM(w_up.shape, BF16), pltpu.VMEM(w_down.shape, BF16), pltpu.VMEM((4,) + wvh.shape, F32),
             heads, stat, heads, stat, heads, stat, heads, stat,
             full, full, pltpu.VMEM((nh, nb, width), F32), rhalf,
-            full, full, full, full, heads, heads, pltpu.VMEM((nb, 128), F32), pltpu.VMEM((nb, 128), F32),
+            full, full, heads, heads, pltpu.VMEM((nb, 128), F32), pltpu.VMEM((nb, 128), F32),
             pltpu.VMEM((nb, ff), F32),
             pltpu.SemaphoreType.DMA((3,)), pltpu.SemaphoreType.DMA((2, 18)),
         ],
@@ -590,20 +586,20 @@
     )(z, dl, rf1, rb, rc, wk, wq, gain, probe)
 
 
-def outer_body(hd, qt_ref, z_ref, dqt_ref, pm_ref, dot_ref, rf_ref, gain_ref, bias_ref, pooled_ref, gp_ref, gwk_ref, gwq_ref, gwv_ref, pooled_out, gp_out):
+def outer_body(hd, qt_ref, z_ref, dqt_ref, pm_ref, dot_ref, rf_ref, gain_ref, bias_ref, ab_ref, mp_ref, mpo_ref, gp_ref, gwk_ref, gwq_ref, gwv_ref, pooled_out, gp_out):
     gwk_ref[...] = mm(qt_ref[...], z_ref[...])
     gwq_ref[...] = mm(dqt_ref[...], pm_ref[...])
     gain, bias = row_of(gain_ref), row_of(bias_ref)
     for h in range(rf_ref.shape[0]):
         r = (rf_ref[h] * gain + bias).astype(BF16)
         gwv_ref[h * hd:(h + 1) * hd, :] = mm(dot_ref[h * hd:(h + 1) * hd, :], r)
-    pooled_out[...] = pooled_ref[...]
+    pooled_out[...] = (ab_ref[...] + (mp_ref[...] + mpo_ref[...])).astype(BF16)
     gp_out[...] = gp_ref[...]
 
 
-def run_outer(nh, hd, qt, z, dqt, pm, dot, rf, gain, bias, pooled, gp):
-    nb, width = pooled.shape
-    per = 1
+def run_outer(nh, hd, qt, z, dqt, pm, dot, rf, gain, bias, ab, mp, mpo, gp):
+    nb, width = ab.shape
+    per = 2
     rows = per * hd
     blk = lambda a: pl.BlockSpec((rows, a.shape[1]), lambda i: (i, 0))
     whole = lambda a: pl.BlockSpec(a.shape, lambda i: (0,) * a.ndim)
@@ -611,12 +607,12 @@
     return pl.pallas_call(
         functools.partial(outer_body, hd),
         grid=(nh // per,),
-        in_specs=[blk(qt), whole(z), blk(dqt), whole(pm), blk(dot), pl.BlockSpec((per, nb, width), lambda i: (i, 0, 0)), whole(gain), whole(bias), whole(pooled), whole(gp)],
-        out_specs=[blk(big), blk(big), blk(big), whole(pooled), whole(gp)],
-        out_shape=[big, big, big, jax.ShapeDtypeStruct(pooled.shape, BF16), jax.ShapeDtypeStruct(gp.shape, F32)],
+        in_specs=[blk(qt), whole(z), blk(dqt), whole(pm), blk(dot), pl.BlockSpec((per, nb, width), lambda i: (i, 0, 0)), whole(gain), whole(bias), whole(ab), whole(mp), whole(mpo), whole(gp)],
+        out_specs=[blk(big), blk(big), blk(big), whole(ab), whole(gp)],
+        out_shape=[big, big, big, jax.ShapeDtypeStruct(ab.shape, BF16), jax.ShapeDtypeStruct(gp.shape, F32)],
         cost_estimate=pl.CostEstimate(flops=300_000_000, bytes_accessed=14_000_000, transcendentals=0),
         name='outer_grads',
-    )(qt, z, dqt, pm, dot, rf, gain, bias, pooled, gp)
+    )(qt, z, dqt, pm, dot, rf, gain, bias, ab, mp, mpo, gp)
 
 
 def local_head(encoded, enc_gain, enc_bias, probe, w_query, b_query, w_key, w_value, b_value, w_out, b_out, head_gain, head_bias, w_up, b_up, w_down, b_down, out_grad):
@@ -634,11 +630,12 @@
     gu2, bu, qt, cb, wvq = run_query(nh, hd, probe, wq, b_query, wk, wv, b_value, enc_gain, enc_bias)
     wvq = lax.ppermute(wvq, 'tp', [(0, 1), (1, 0)])
     xh, sx, rs, r_raw, ml = run_fwd(encoded, gu2, bu)
-    yt, ht, dpre, ot, da, pooled, do_t, gt, aux, rf1, rb = run_head(nh, hd, r_raw, ml, wv, wvq, wo, w_up, w_down, enc_gain, bu, cb, b_out, head_gain, head_bias, b_up, b_down, out_grad)
+    yt, ht, dpre, ot, da, ab, mp, do_t, gt, aux, rf1, rb = run_head(nh, hd, r_raw, ml, wv, wvq, wo, w_up, w_down, enc_gain, bu, cb, b_out, head_gain, head_bias, b_up, b_down, out_grad)
+    mpo = lax.ppermute(mp, 'tp', [(0, 1), (1, 0)])
     rc = lax.ppermute(rb, 'sp', [(i, (i + 2) % 4) for i in range(4)])
     grad_encoded, z, dl, grad_w_up, grad_w_down, grad_w_out = run_bwd(xh, sx, rs, gt, gu2, aux, yt, dpre, ht, out_grad, ot, da)
     z, dqt, pm, grad_probe, rf = run_tail(nh, hd, z, dl, rf1, rb, rc, wk, wq, enc_gain, probe)
-    gwk, gwq, gwv, pooled, grad_probe = run_outer(nh, hd, qt, z, dqt, pm, do_t, rf, enc_gain, enc_bias, pooled, grad_probe)
+    gwk, gwq, gwv, pooled, grad_probe = run_outer(nh, hd, qt, z, dqt, pm, do_t, rf, enc_gain, enc_bias, ab, mp, mpo, grad_probe)
     grad_w_query, grad_w_key, grad_w_value = heads(gwq), heads(gwk), heads(gwv)
     return (pooled, grad_encoded, grad_probe, grad_w_query, grad_w_key, grad_w_value, grad_w_out.reshape(nh, hd, width), grad_w_up, grad_w_down)
 

time: 124 us -> 121 us (0.976)
  Pallas kernels: 119 us -> 114 us
  starting transfers between devices: 2.06 us -> 3.36 us
    pallas_call x1, Pallas kernels: 27.2 us -> 25.2 us  [run_bwd(): pl.pallas_call(functools.partial(bwd_body, nk), grid=(ng,), in_specs=[pl....]
    pallas_call x1, Pallas kernels: 8.2 us -> 6.79 us  [run_outer(): pl.pallas_call(functools.partial(outer_body, hd), grid=(nh // per,), in_s...]
    ppermute x0 -> x1, starting transfers between devices: none -> 1.29 us  [local_head(): mpo = lax.ppermute(mp, 'tp', [(0, 1), (1, 0)])]
    unnamed x4 -> x6, local copies, waits for them, and re-layouts: 1.82 us -> 2.55 us
  transfers between devices with their start and end apart: 2 -> 3, of which waited for: 0 -> 0; matrix products, arithmetic and copies ran while one was open for 0% -> 0% of each run, Pallas kernels for 38% -> 47%
where the time goes in v5:
time: 121 us
  Pallas kernels  114 us (94%)
  starting transfers between devices  3.36 us (3%)
  local copies, waits for them, and re-layouts  2.55 us (2%)
    pallas_call x1, Pallas kernels, run_head(): pl.pallas_call(functools.partial(head_body, nh, hd), in_specs=[VM] * 4 +...  41.1 us
    pallas_call x1, Pallas kernels, run_bwd(): pl.pallas_call(functools.partial(bwd_body, nk), grid=(ng,), in_specs=[pl....  25.2 us
    pallas_call x1, Pallas kernels, run_fwd(): pl.pallas_call(functools.partial(fwd_body, nk), grid=(ng,), in_specs=[pl....  19.6 us
    pallas_call x1, Pallas kernels, run_tail(): pl.pallas_call(functools.partial(tail_body, nh, hd), in_specs=[VM] * 5 +...  12.1 us
    pallas_call x1, Pallas kernels, run_query(): pl.pallas_call(functools.partial(query_body, nh, hd), in_specs=[VM] * 3 +...  9.64 us
    pallas_call x1, Pallas kernels, run_outer(): pl.pallas_call(functools.partial(outer_body, hd), grid=(nh // per,), in_s...  6.79 us
    unnamed x6, local copies, waits for them, and re-layouts  2.55 us
  transfers between devices with their start and end apart: 3, of which 0 were waited for; matrix products, arithmetic and copies ran while one was open for 0% of the time, Pallas kernels for 47%

profile of v5, /device:TPU:0, one launch (start us, length us, event | category | flops | bytes accessed | tf_op | source)
XLA Modules:
  0.0 121.1 jit_solution(11956852965370660121)
XLA Ops:
  0.6 9.6 %query_fold.1 = (bf16[32,1280]{1,0:T(8,128)(2,1)}, f32[1,128]{1,0:T(1,128)}, bf16[640,32]{1,0:T(8,128)(2,1)}, f32[1,640]{1,0:T(1,128)}, f32[160,1280]{1,0:T(8,128)}) custom-call(f32[1280]{0:T(1024)} %probe_ref.3, bf16[640,1280]{1,0:T(8,128)(2,1)} %bitcast.22, f32[8,80]{1,0:T(8,128)} %bq_ref.1, bf16[640,1280]{1,0:T(8,128)(2,1)} %bitcast.24, ...), custom_call_target="tpu_custom_call" | custom-call | flops 50000000 | bytes 6000000 | tf_op jit(solution)/shard_map/query_fold/pallas_call | solution.py:296
  10.3 1.3 %collective-permute-start = (f32[160,1280]{1,0:T(8,128)}, f32[160,1280]{1,0:T(8,128)S(1)}, u32[]{:S(2)}, u32[]{:S(2)}) collective-permute-start(f32[160,1280]{1,0:T(8,128)} %get-tuple-element.55), channel_id=1, source_target_pairs={{0,4},{4,0},{1,5},{5,1},{2,6},{6,2},{3,7},{7,3}} | collective-permute-start | bytes 2457608 | tf_op jit(solution)/shard_map/ppermute | solution.py:631
  11.6 19.6 %fwd_tokens.1 = (bf16[64,96,1280]{2,1,0:T(8,128)(2,1)}, f32[8,96,128]{2,1,0:T(8,128)}, f32[8,96,128]{2,1,0:T(8,128)}, f32[8,64,1280]{2,1,0:T(8,128)}, f32[8,8,128]{2,1,0:T(8,128)}) custom-call(bf16[64,96,1280]{2,1,0:T(8,128)(2,1)} %x_ref.1, bf16[32,1280]{1,0:T(8,128)(2,1)} %get-tuple-element.48.gu_ref, f32[1,128]{1,0:T(1,128)} %get-tuple-element.49.bu_ref), custom_call_target="tpu_custom_call" | custom-call | flops 8000000000 | bytes 40000000 | tf_op jit(solution)/shard_map/fwd_tokens/pallas_call | solution.py:64
  31.3 0.0 collective-permute-done.wvh_ref
  31.3 0.0 copy-start.1
  31.3 0.9 copy-done.1
  32.2 41.1 %pool_head.1 = (bf16[1280,64]{1,0:T(8,128)(2,1)}, bf16[2560,64]{1,0:T(8,128)(2,1)}, bf16[64,2560]{1,0:T(8,128)(2,1)}, bf16[640,64]{1,0:T(8,128)(2,1)}, bf16[64,1...) custom-call(f32[8,64,1280]{2,1,0:T(8,128)} %get-tuple-element.53.r_r, ...), custom_call_target="tpu_custom_call" | custom-call | flops 3000000000 | bytes 30000000 | tf_op jit(solution)/shard_map/pool_head/pallas_call | solution.py:481
  73.2 0.8 collective-permute-start.1
  74.0 1.3 %collective-permute-start.2 = (f32[64,1280]{1,0:T(8,128)}, f32[64,1280]{1,0:T(8,128)S(1)}, u32[]{:S(2)}, u32[]{:S(2)}) collective-permute-start(f32[64,1280]{1,0:T(8,128)} %get-tuple-element.74.mp_ref), channel_id=1, source_target_pairs={{0,4},{4,0},{1,5},{5,1},{2,6},{6,2},{3,7},{7,3}} | collective-permute-start | bytes 983048 | tf_op jit(solution)/shard_map/ppermute | solution.py:634
  75.3 25.2 %bwd_tokens.1 = (bf16[64,96,1280]{2,1,0:T(8,128)(2,1)}, f32[8,1280]{1,0:T(8,128)}, f32[8,8,128]{2,1,0:T(8,128)}, f32[1280,2560]{1,0:T(8,128)}, f32[2560,1280]{1,0:T(8,128)}, /*index=5*/f32[640,1280]{1,0:T(8,128)}) custom-call(bf16[64,96,1280]{2,1,0:T(8,128)(2,1)} %get-tuple-element.50.xh_ref, f32[8,96,128]{2,1,0:T(8,128)} %get-tuple-element.51.sx_ref, ...), custom_call_target="tpu_custom_call" | custom-call | flops 12000000000 | bytes 40000000 | tf_op jit(solution)/shard_map/bwd_tokens/pallas_call | solution.py:137
  100.5 0.0 collective-permute-done.1.rc_ref
  100.5 0.0 copy-start
  100.5 0.9 copy-done
  101.4 12.1 %query_back.1 = (bf16[32,1280]{1,0:T(8,128)(2,1)}, bf16[640,8]{1,0:T(8,128)(2,1)}, bf16[8,1280]{1,0:T(8,128)(2,1)}, f32[1280]{0:T(1024)}, f32[8,64,1280]{2,1,0:T(8,128)}) custom-call(f32[8,1280]{1,0:T(8,128)} %get-tuple-element.64.z_ref, f32[8,8,128]{2,1,0:T(8,128)} %get-tuple-element.65.dl_ref, f32[1,64,1280]{2,1,0:T(8,128)} %get-tuple-element.66.rf1_ref, ...), custom_call_target="tpu_custom_call" | custom-call | flops 50000000 | bytes 6000000 | tf_op jit(solution)/shard_map/query_back/pallas_call | solution.py:571
  113.5 0.0 collective-permute-done.2.mpo_ref
  113.5 0.0 copy-start.2
  113.5 0.7 copy-done.2
  114.3 6.8 %outer_grads.1 = (f32[640,1280]{1,0:T(8,128)}, f32[640,1280]{1,0:T(8,128)}, f32[640,1280]{1,0:T(8,128)}, bf16[64,1280]{1,0:T(8,128)(2,1)}, f32[1280]{0:T(1024)}) custom-call(bf16[640,32]{1,0:T(8,128)(2,1)} %get-tuple-element.47.qt_ref, bf16[32,1280]{1,0:T(8,128)(2,1)} %get-tuple-element.68.z_ref, bf16[640,8]{1,0:T(8,128)(2,1)} %get-tuple-element.69.dqt_ref, ...), custom_call_target="tpu_custom_call" | custom-call | flops 300000000 | bytes 14000000 | tf_op jit(solution)/shard_map/outer_grads/pallas_call | solution.py:607
Async XLA Ops:
  10.3 21.0 %collective-permute-start = (f32[160,1280]{1,0:T(8,128)}, f32[160,1280]{1,0:T(8,128)S(1)}, u32[]{:S(2)}, u32[]{:S(2)}) collective-permute-start(f32[160,1280]{1,0:T(8,128)} %get-tuple-element.55), channel_id=1, source_target_pairs={{0,4},{4,0},{1,5},{5,1},{2,6},{6,2},{3,7},{7,3}} | collective-permute-start | bytes 2457608 | tf_op jit(solution)/shard_map/ppermute | solution.py:631
  31.3 0.9 copy-start.1
  73.2 27.2 %collective-permute-start.1 = (f32[3,64,1280]{2,1,0:T(8,128)}, f32[3,64,1280]{2,1,0:T(8,128)S(1)}, u32[]{:S(2)}, u32[]{:S(2)}) collective-permute-start(f32[3,64,1280]{2,1,0:T(8,128)} %get-tuple-element.67.rb_ref), channel_id=1, source_target_pairs={{0,2},{1,3},{2,0},{3,1},{4,6},{5,7},{6,4},{7,5}} | collective-permute-start | bytes 2949128 | tf_op jit(solution)/shard_map/ppermute | solution.py:635
  74.0 39.5 %collective-permute-start.2 = (f32[64,1280]{1,0:T(8,128)}, f32[64,1280]{1,0:T(8,128)S(1)}, u32[]{:S(2)}, u32[]{:S(2)}) collective-permute-start(f32[64,1280]{1,0:T(8,128)} %get-tuple-element.74.mp_ref), channel_id=1, source_target_pairs={{0,4},{4,0},{1,5},{5,1},{2,6},{6,2},{3,7},{7,3}} | collective-permute-start | bytes 983048 | tf_op jit(solution)/shard_map/ppermute | solution.py:634
  100.5 0.9 copy-start
  113.5 0.7 copy-start.2

commit v6 on v5

--- a/solution.py
+++ b/solution.py
@@ -83,6 +83,7 @@
             jax.ShapeDtypeStruct((nk // 2, nb, width), F32),
             jax.ShapeDtypeStruct((ng, 8, 128), F32),
         ],
+        compiler_params=pltpu.CompilerParams(vmem_limit_bytes=67043328),
         cost_estimate=pl.CostEstimate(flops=8_000_000_000, bytes_accessed=40_000_000, transcendentals=0),
         name='fwd_tokens',
     )(x, gu2, bu)
@@ -168,6 +169,7 @@
             jax.ShapeDtypeStruct((nd, width), F32),
         ],
         scratch_shapes=[pltpu.VMEM((nk // 2, width), F32)],
+        compiler_params=pltpu.CompilerParams(vmem_limit_bytes=67043328),
         cost_estimate=pl.CostEstimate(flops=12_000_000_000, bytes_accessed=40_000_000, transcendentals=0),
         name='bwd_tokens',
     )(xh, sx, rs, gt, gu2, aux, yt, dpre, ht, out_grad, ot, da)
@@ -305,7 +307,7 @@
             jax.ShapeDtypeStruct((nh * hd // 4, width), F32),
         ],
         scratch_shapes=[pltpu.VMEM((nh, width), F32), pltpu.VMEM((nh, width), F32), pltpu.VMEM(wk.shape, BF16), pltpu.VMEM(wv.shape, BF16), pltpu.SemaphoreType.DMA((2,)), pltpu.SemaphoreType.DMA((2, 1))],
-        compiler_params=pltpu.CompilerParams(collective_id=0, has_side_effects=True),
+        compiler_params=pltpu.CompilerParams(collective_id=0, has_side_effects=True, vmem_limit_bytes=67043328),
         cost_estimate=pl.CostEstimate(flops=50_000_000, bytes_accessed=6_000_000, transcendentals=0),
         name='query_fold',
     )(probe, wq, bq, wk, wv, bv, gain, bias)
@@ -504,7 +506,7 @@
             pltpu.VMEM((nb, ff), F32),
             pltpu.SemaphoreType.DMA((3,)), pltpu.SemaphoreType.DMA((2, 18)),
         ],
-        compiler_params=pltpu.CompilerParams(collective_id=1, has_side_effects=True, vmem_limit_bytes=60 * 1024 * 1024),
+        compiler_params=pltpu.CompilerParams(collective_id=1, has_side_effects=True, vmem_limit_bytes=67043328),
         cost_estimate=pl.CostEstimate(flops=3_000_000_000, bytes_accessed=30_000_000, transcendentals=0),
         name='pool_head',
     )(r_raw, ml, wv, wvh, wo, w_up, w_down, gain, bu, cb, b_out, hgain, hbias, b_up, b_down, out_grad)
@@ -580,7 +582,7 @@
             jax.ShapeDtypeStruct((nh,) + rb.shape[1:], F32),
         ],
         scratch_shapes=[zz, zz, zz, zz, dd, dd, dd, dd, pp, pp, rr, rr, pltpu.VMEM(wk.shape, BF16), pltpu.VMEM(wq.shape, BF16), pltpu.SemaphoreType.DMA((2,)), pltpu.SemaphoreType.DMA((2, 6))],
-        compiler_params=pltpu.CompilerParams(collective_id=2, has_side_effects=True),
+        compiler_params=pltpu.CompilerParams(collective_id=2, has_side_effects=True, vmem_limit_bytes=67043328),
         cost_estimate=pl.CostEstimate(flops=50_000_000, bytes_accessed=6_000_000, transcendentals=0),
         name='query_back',
     )(z, dl, rf1, rb, rc, wk, wq, gain, probe)
@@ -610,6 +612,7 @@
         in_specs=[blk(qt), whole(z), blk(dqt), whole(pm), blk(dot), pl.BlockSpec((per, nb, width), lambda i: (i, 0, 0)), whole(gain), whole(bias), whole(ab), whole(mp), whole(mpo), whole(gp)],
         out_specs=[blk(big), blk(big), blk(big), whole(ab), whole(gp)],
         out_shape=[big, big, big, jax.ShapeDtypeStruct(ab.shape, BF16), jax.ShapeDtypeStruct(gp.shape, F32)],
+        compiler_params=pltpu.CompilerParams(vmem_limit_bytes=67043328),
         cost_estimate=pl.CostEstimate(flops=300_000_000, bytes_accessed=14_000_000, transcendentals=0),
         name='outer_grads',
     )(qt, z, dqt, pm, dot, rf, gain, bias, ab, mp, mpo, gp)

time: 121 us -> 119 us (0.983)
  local copies, waits for them, and re-layouts: 2.55 us -> 0 us
    unnamed x6 -> x0, local copies, waits for them, and re-layouts: 2.55 us -> none
  transfers between devices with their start and end apart: 3 -> 3, of which waited for: 0 -> 0; matrix products, arithmetic and copies ran while one was open for 0% -> 0% of each run, Pallas kernels for 47% -> 48%
where the time goes in v6:
time: 119 us; the launch traced here: 118 us
  Pallas kernels  114 us (96%)
  starting transfers between devices  3.35 us (3%)
    pallas_call x1, Pallas kernels, run_head(): pl.pallas_call(functools.partial(head_body, nh, hd), in_specs=[VM] * 4 +...  41.1 us
    pallas_call x1, Pallas kernels, run_bwd(): pl.pallas_call(functools.partial(bwd_body, nk), grid=(ng,), in_specs=[pl....  25.2 us
    pallas_call x1, Pallas kernels, run_fwd(): pl.pallas_call(functools.partial(fwd_body, nk), grid=(ng,), in_specs=[pl....  19.7 us
    pallas_call x1, Pallas kernels, run_tail(): pl.pallas_call(functools.partial(tail_body, nh, hd), in_specs=[VM] * 5 +...  12.1 us
    pallas_call x1, Pallas kernels, run_query(): pl.pallas_call(functools.partial(query_body, nh, hd), in_specs=[VM] * 3 +...  9.64 us
    pallas_call x1, Pallas kernels, run_outer(): pl.pallas_call(functools.partial(outer_body, hd), grid=(nh // per,), in_s...  6.81 us
  transfers between devices with their start and end apart: 3, of which 0 were waited for; matrix products, arithmetic and copies ran while one was open for 0% of the time, Pallas kernels for 48%

profile of v6, /device:TPU:0, one launch (start us, length us, event | category | flops | bytes accessed | tf_op | source)
XLA Modules:
  0.0 118.5 jit_solution(12688288455203423841)
XLA Ops:
  0.6 9.6 %query_fold.1 = (bf16[32,1280]{1,0:T(8,128)(2,1)}, f32[1,128]{1,0:T(1,128)}, bf16[640,32]{1,0:T(8,128)(2,1)}, f32[1,640]{1,0:T(1,128)}, f32[160,1280]{1,0:T(8,128)}) custom-call(f32[1280]{0:T(1024)} %probe_ref.3, bf16[640,1280]{1,0:T(8,128)(2,1)} %bitcast.22, f32[8,80]{1,0:T(8,128)} %bq_ref.1, bf16[640,1280]{1,0:T(8,128)(2,1)} %bitcast.24, ...), custom_call_target="tpu_custom_call" | custom-call | flops 50000000 | bytes 6000000 | tf_op jit(solution)/shard_map/query_fold/pallas_call | solution.py:298
  10.3 1.3 %collective-permute-start = (f32[160,1280]{1,0:T(8,128)}, f32[160,1280]{1,0:T(8,128)}, u32[]{:S(2)}, u32[]{:S(2)}) collective-permute-start(f32[160,1280]{1,0:T(8,128)} %get-tuple-element.55), channel_id=1, source_target_pairs={{0,4},{4,0},{1,5},{5,1},{2,6},{6,2},{3,7},{7,3}} | collective-permute-start | bytes 2457608 | tf_op jit(solution)/shard_map/ppermute | solution.py:634
  11.6 19.7 %fwd_tokens.1 = (bf16[64,96,1280]{2,1,0:T(8,128)(2,1)}, f32[8,96,128]{2,1,0:T(8,128)}, f32[8,96,128]{2,1,0:T(8,128)}, f32[8,64,1280]{2,1,0:T(8,128)}, f32[8,8,128]{2,1,0:T(8,128)}) custom-call(bf16[64,96,1280]{2,1,0:T(8,128)(2,1)} %x_ref.1, bf16[32,1280]{1,0:T(8,128)(2,1)} %get-tuple-element.48.gu_ref, f32[1,128]{1,0:T(1,128)} %get-tuple-element.49.bu_ref), custom_call_target="tpu_custom_call" | custom-call | flops 8000000000 | bytes 40000000 | tf_op jit(solution)/shard_map/fwd_tokens/pallas_call | solution.py:64
  31.3 0.0 collective-permute-done.wvh_ref
  31.3 41.1 %pool_head.1 = (bf16[1280,64]{1,0:T(8,128)(2,1)}, bf16[2560,64]{1,0:T(8,128)(2,1)}, bf16[64,2560]{1,0:T(8,128)(2,1)}, bf16[640,64]{1,0:T(8,128)(2,1)}, bf16[64,1...) custom-call(f32[8,64,1280]{2,1,0:T(8,128)} %get-tuple-element.53.r_r, ...), custom_call_target="tpu_custom_call" | custom-call | flops 3000000000 | bytes 30000000 | tf_op jit(solution)/shard_map/pool_head/pallas_call | solution.py:483
  72.3 0.7 collective-permute-start.1
  73.1 1.3 %collective-permute-start.2 = (f32[64,1280]{1,0:T(8,128)}, f32[64,1280]{1,0:T(8,128)}, u32[]{:S(2)}, u32[]{:S(2)}) collective-permute-start(f32[64,1280]{1,0:T(8,128)} %get-tuple-element.74.mp_ref), channel_id=1, source_target_pairs={{0,4},{4,0},{1,5},{5,1},{2,6},{6,2},{3,7},{7,3}} | collective-permute-start | bytes 983048 | tf_op jit(solution)/shard_map/ppermute | solution.py:637
  74.4 25.2 %bwd_tokens.1 = (bf16[64,96,1280]{2,1,0:T(8,128)(2,1)}, f32[8,1280]{1,0:T(8,128)}, f32[8,8,128]{2,1,0:T(8,128)}, f32[1280,2560]{1,0:T(8,128)}, f32[2560,1280]{1,0:T(8,128)}, /*index=5*/f32[640,1280]{1,0:T(8,128)}) custom-call(bf16[64,96,1280]{2,1,0:T(8,128)(2,1)} %get-tuple-element.50.xh_ref, f32[8,96,128]{2,1,0:T(8,128)} %get-tuple-element.51.sx_ref, ...), custom_call_target="tpu_custom_call" | custom-call | flops 12000000000 | bytes 40000000 | tf_op jit(solution)/shard_map/bwd_tokens/pallas_call | solution.py:138
  99.5 0.0 collective-permute-done.1.rc_ref
  99.5 12.1 %query_back.1 = (bf16[32,1280]{1,0:T(8,128)(2,1)}, bf16[640,8]{1,0:T(8,128)(2,1)}, bf16[8,1280]{1,0:T(8,128)(2,1)}, f32[1280]{0:T(1024)}, f32[8,64,1280]{2,1,0:T(8,128)}) custom-call(f32[8,1280]{1,0:T(8,128)} %get-tuple-element.64.z_ref, f32[8,8,128]{2,1,0:T(8,128)} %get-tuple-element.65.dl_ref, f32[1,64,1280]{2,1,0:T(8,128)} %get-tuple-element.66.rf1_ref, ...), custom_call_target="tpu_custom_call" | custom-call | flops 50000000 | bytes 6000000 | tf_op jit(solution)/shard_map/query_back/pallas_call | solution.py:573
  111.6 0.0 collective-permute-done.2.mpo_ref
  111.7 6.8 %outer_grads.1 = (f32[640,1280]{1,0:T(8,128)}, f32[640,1280]{1,0:T(8,128)}, f32[640,1280]{1,0:T(8,128)}, bf16[64,1280]{1,0:T(8,128)(2,1)}, f32[1280]{0:T(1024)}) custom-call(bf16[640,32]{1,0:T(8,128)(2,1)} %get-tuple-element.47.qt_ref, bf16[32,1280]{1,0:T(8,128)(2,1)} %get-tuple-element.68.z_ref, bf16[640,8]{1,0:T(8,128)(2,1)} %get-tuple-element.69.dqt_ref, ...), custom_call_target="tpu_custom_call" | custom-call | flops 300000000 | bytes 14000000 | tf_op jit(solution)/shard_map/outer_grads/pallas_call | solution.py:609
Async XLA Ops:
  10.3 21.0 %collective-permute-start = (f32[160,1280]{1,0:T(8,128)}, f32[160,1280]{1,0:T(8,128)}, u32[]{:S(2)}, u32[]{:S(2)}) collective-permute-start(f32[160,1280]{1,0:T(8,128)} %get-tuple-element.55), channel_id=1, source_target_pairs={{0,4},{4,0},{1,5},{5,1},{2,6},{6,2},{3,7},{7,3}} | collective-permute-start | bytes 2457608 | tf_op jit(solution)/shard_map/ppermute | solution.py:634
  72.3 27.2 %collective-permute-start.1 = (f32[3,64,1280]{2,1,0:T(8,128)}, f32[3,64,1280]{2,1,0:T(8,128)}, u32[]{:S(2)}, u32[]{:S(2)}) collective-permute-start(f32[3,64,1280]{2,1,0:T(8,128)} %get-tuple-element.67.rb_ref), channel_id=1, source_target_pairs={{0,2},{1,3},{2,0},{3,1},{4,6},{5,7},{6,4},{7,5}} | collective-permute-start | bytes 2949128 | tf_op jit(solution)/shard_map/ppermute | solution.py:638
  73.1 38.6 %collective-permute-start.2 = (f32[64,1280]{1,0:T(8,128)}, f32[64,1280]{1,0:T(8,128)}, u32[]{:S(2)}, u32[]{:S(2)}) collective-permute-start(f32[64,1280]{1,0:T(8,128)} %get-tuple-element.74.mp_ref), channel_id=1, source_target_pairs={{0,4},{4,0},{1,5},{5,1},{2,6},{6,2},{3,7},{7,3}} | collective-permute-start | bytes 983048 | tf_op jit(solution)/shard_map/ppermute | solution.py:637
